TPU v7x, 32 devices: a whole 2x2x4 slice. The times are simulated.
32 devices in a mesh: dp: 8 (over y, x, core), tensor: 4 (over z).
Axes of the slice: x: 2, y: 2, z: 4, core: 2. Of those that a mesh axis runs over, the one named last changes fastest.
Arguments:
- tokens: bfloat16 [16, 1024, 768], P('dp', 'tensor'), may hold values from -6 to 6
- prefix_len: int32 [16], P('dp'), may hold values from 102 to 512, as said below
- w_qkv: bfloat16 [768, 3, 768], P('dp', None, 'tensor'), may hold values from -0.21875 to 0.21875
- bias_qv: bfloat16 [2, 768], P(None, ('tensor', 'dp')), may hold values from -0.59765625 to 0.59765625
- w_out: bfloat16 [768, 768], P('tensor', 'dp'), may hold values from -1.5 to 1.5
- w_up: bfloat16 [768, 3072], P('dp', 'tensor'), may hold values from -0.21875 to 0.21875
- bias_up: bfloat16 [3072], P(('tensor', 'dp')), may hold values from -1.796875 to 1.796875
- w_down: bfloat16 [3072, 768], P('tensor', 'dp'), may hold values from -0.15625 to 0.15625
- gains: bfloat16 [2, 768], P(None, ('dp', 'tensor')), may hold values from 0.5 to 1.5
- shifts: bfloat16 [4, 768], P(None, ('dp', 'tensor')), may hold values from -1.1953125 to 1.1953125
- cotangent: bfloat16 [16, 1024, 768], P('dp', 'tensor'), may hold values from -6 to 6
Outputs:
- output: bfloat16 [16, 1024, 768], P('dp', 'tensor')
- token_grad: float32 [16, 1024, 768], P('dp', 'tensor')
- grad_qkv: float32 [768, 3, 768], P('dp', None, 'tensor')
- grad_bias_qv: float32 [2, 768], P(None, ('tensor', 'dp'))
- grad_out: float32 [768, 768], P('tensor', 'dp')
- grad_up: float32 [768, 3072], P('dp', 'tensor')
- grad_bias_up: float32 [3072], P(('tensor', 'dp'))
- grad_down: float32 [3072, 768], P('tensor', 'dp')
- grad_gains: float32 [2, 768], P(None, ('dp', 'tensor'))
- grad_shifts: float32 [4, 768], P(None, ('dp', 'tensor'))
Inputs may be any that keep to these rules, and one draw needn't show every extreme that they name: `prefix_len`: the number of leading positions of a sequence that every position sees; the least and the greatest value occur in every draw.
All inputs are finite; a program needn't handle non-finite values.
Results may differ from a plain program's by a relative error of at most 0.02.
Values may be sent and summed in bfloat16 or wider, within the bound.
A program may use at most 192 MiB of HBM per device.

v0:
```python
from functools import partial

import jax
import jax.numpy as jnp
from jax import lax
from jax.sharding import PartitionSpec as P

DH = 64


EPSILON = 1e-05
MASKED_SCORE = -1e30


def norm_forward(values, gain_row, shift_row):
    center = values - jnp.mean(values, axis=-1, keepdims=True)
    inverse = lax.rsqrt(jnp.mean(center * center, axis=-1, keepdims=True) + EPSILON)
    normal = center * inverse
    return (normal * gain_row + shift_row, normal, inverse)


def norm_backward(incoming, normal, inverse, gain_row):
    scaled = incoming * gain_row
    first_mean = jnp.mean(scaled, axis=-1, keepdims=True)
    second_mean = jnp.mean(scaled * normal, axis=-1, keepdims=True)
    outgoing = inverse * (scaled - first_mean - normal * second_mean)
    return (outgoing, jnp.sum(incoming * normal, axis=0), jnp.sum(incoming, axis=0))


def visible_mask(offset, block_rows, length, prefix):
    row_ids = offset + jnp.arange(block_rows, dtype=jnp.int32)[:, None]
    column_ids = jnp.arange(length, dtype=jnp.int32)[None, :]
    return jnp.logical_or(column_ids < prefix, column_ids <= row_ids)


def block_scores(chosen, key_heads, offset, prefix, scaling):
    length = key_heads.shape[0]
    allowed = visible_mask(offset, chosen.shape[0], length, prefix)
    scores = (
        jnp.einsum("qhd,khd->hqk", chosen, key_heads, preferred_element_type=jnp.float32) * scaling
    )
    return jnp.where(allowed[None], scores, MASKED_SCORE)


def attention_forward(queries, key_heads, value_heads, prefix):
    length = key_heads.shape[0]
    block_rows = min(512, length)
    scaling = queries.shape[-1] ** (-0.5)
    outputs = []
    totals = []
    for offset in range(0, length, block_rows):
        scores = block_scores(
            queries[offset : offset + block_rows], key_heads, offset, prefix, scaling
        )
        row_max = jnp.max(scores, axis=-1, keepdims=True)
        log_total = jnp.log(jnp.sum(jnp.exp(scores - row_max), axis=-1, keepdims=True)) + row_max
        attn_probs = jnp.exp(scores - log_total).astype(jnp.bfloat16)
        outputs.append(
            jnp.einsum("hqk,khd->qhd", attn_probs, value_heads, preferred_element_type=jnp.float32)
        )
        totals.append(log_total)
    return (jnp.concatenate(outputs, axis=0), totals)


def attention_backward(queries, key_heads, value_heads, prefix, totals, context_grad):
    length = key_heads.shape[0]
    block_rows = min(512, length)
    scaling = queries.shape[-1] ** (-0.5)
    query_parts = []
    key_grad = jnp.zeros(key_heads.shape, jnp.float32)
    value_grad = jnp.zeros(value_heads.shape, jnp.float32)
    for number, offset in enumerate(range(0, length, block_rows)):
        chosen = queries[offset : offset + block_rows]
        grad_block = context_grad[offset : offset + block_rows]
        scores = block_scores(chosen, key_heads, offset, prefix, scaling)
        attn_probs = jnp.exp(scores - totals[number])
        probs_low = attn_probs.astype(jnp.bfloat16)
        probs_grad = jnp.einsum(
            "qhd,khd->hqk", grad_block, value_heads, preferred_element_type=jnp.float32
        )
        row_dot = jnp.sum(attn_probs * probs_grad, axis=-1, keepdims=True)
        scores_grad = (attn_probs * (probs_grad - row_dot)).astype(jnp.bfloat16)
        query_parts.append(
            jnp.einsum("hqk,khd->qhd", scores_grad, key_heads, preferred_element_type=jnp.float32)
            * scaling
        )
        key_grad = (
            key_grad
            + jnp.einsum("hqk,qhd->khd", scores_grad, chosen, preferred_element_type=jnp.float32)
            * scaling
        )
        value_grad = value_grad + jnp.einsum(
            "hqk,qhd->khd", probs_low, grad_block, preferred_element_type=jnp.float32
        )
    return (jnp.concatenate(query_parts, axis=0), key_grad, value_grad)


def local(
    tokens, prefix_len, w_qkv, bias_qv, w_out, w_up, bias_up, w_down, gains, shifts, cotangent
):
    tensor_count = lax.axis_size("tensor")
    seq_local, shard_rows, model_width = tokens.shape
    length = shard_rows * tensor_count
    full_qkv, full_bias_qv, full_out, full_up, full_bias_up, full_down = (
        lax.all_gather(w_qkv, "dp", axis=0, tiled=True),
        lax.all_gather(bias_qv, "dp", axis=1, tiled=True),
        lax.all_gather(w_out, "dp", axis=1, tiled=True),
        lax.all_gather(w_up, "dp", axis=0, tiled=True),
        lax.all_gather(bias_up, "dp", axis=0, tiled=True),
        lax.all_gather(w_down, "dp", axis=1, tiled=True),
    )
    full_gains, full_shifts = (
        lax.all_gather(gains, ("dp", "tensor"), axis=1, tiled=True),
        lax.all_gather(shifts, ("dp", "tensor"), axis=1, tiled=True),
    )
    full_gains = full_gains.astype(jnp.float32)
    full_shifts = full_shifts.astype(jnp.float32)
    bias_values = full_bias_qv.astype(jnp.float32)
    up_bias = full_bias_up.astype(jnp.float32)
    local_width = full_qkv.shape[2]
    head_count = local_width // DH
    kept_state = []
    outputs = []
    for member in range(seq_local):
        token_rows = tokens[member]
        prefix = prefix_len[member]

        def fold_tokens(piece):
            product = jnp.einsum("rd,dce->rce", piece, full_qkv, preferred_element_type=jnp.float32)
            return (piece, product)

        token_full, projected = fold_tokens(
            lax.all_gather(token_rows, "tensor", axis=0, tiled=True)
        )
        queries = (
            (projected[:, 0] + bias_values[0]).astype(jnp.bfloat16).reshape(length, head_count, DH)
        )
        key_heads = projected[:, 1].astype(jnp.bfloat16).reshape(length, head_count, DH)
        value_heads = (
            (projected[:, 2] + bias_values[1]).astype(jnp.bfloat16).reshape(length, head_count, DH)
        )
        context, totals = attention_forward(queries, key_heads, value_heads, prefix)
        context_low = context.reshape(length, local_width).astype(jnp.bfloat16)
        branch = (
            lax.psum_scatter(
                jnp.dot(context_low, full_out, preferred_element_type=jnp.float32).astype(
                    jnp.bfloat16
                ),
                "tensor",
                scatter_dimension=0,
                tiled=True,
            ).astype(jnp.float32)
            + full_shifts[0]
        )
        normed, normal_one, inverse_one = norm_forward(
            token_rows.astype(jnp.float32) + branch, full_gains[0], full_shifts[1]
        )
        normed_low = normed.astype(jnp.bfloat16)

        def fold_normed(piece):
            product = jnp.dot(piece, full_up, preferred_element_type=jnp.float32)
            return (piece, product)

        normed_full, pre_active = fold_normed(
            lax.all_gather(normed_low, "tensor", axis=0, tiled=True)
        )
        pre_active = pre_active + up_bias
        active_low = jax.nn.gelu(pre_active, approximate=False).astype(jnp.bfloat16)
        feed_out = (
            lax.psum_scatter(
                jnp.dot(active_low, full_down, preferred_element_type=jnp.float32).astype(
                    jnp.bfloat16
                ),
                "tensor",
                scatter_dimension=0,
                tiled=True,
            ).astype(jnp.float32)
            + full_shifts[2]
        )
        result, normal_two, inverse_two = norm_forward(
            normed + feed_out, full_gains[1], full_shifts[3]
        )
        outputs.append(result.astype(jnp.bfloat16))
        kept_state.append(
            (
                token_rows,
                prefix,
                token_full,
                queries,
                key_heads,
                value_heads,
                totals,
                context_low,
                normal_one,
                inverse_one,
                normed_full,
                pre_active,
                active_low,
                normal_two,
                inverse_two,
            )
        )
    back_qkv, back_out, back_up, back_down = (
        lax.all_gather(w_qkv, "dp", axis=0, tiled=True),
        lax.all_gather(w_out, "dp", axis=1, tiled=True),
        lax.all_gather(w_up, "dp", axis=0, tiled=True),
        lax.all_gather(w_down, "dp", axis=1, tiled=True),
    )
    full_shapes = (
        full_qkv.shape,
        full_bias_qv.shape,
        full_out.shape,
        full_up.shape,
        full_bias_up.shape,
        full_down.shape,
    )
    weight_grads = tuple((jnp.zeros(array_shape, jnp.float32) for array_shape in full_shapes))
    gain_grads = jnp.zeros((2, model_width), jnp.float32)
    shift_grads = jnp.zeros((4, model_width), jnp.float32)
    input_grads = []
    for member in range(seq_local):
        (
            token_rows,
            prefix,
            token_full,
            queries,
            key_heads,
            value_heads,
            totals,
            context_low,
            normal_one,
            inverse_one,
            normed_full,
            pre_active,
            active_low,
            normal_two,
            inverse_two,
        ) = kept_state[member]
        incoming = cotangent[member].astype(jnp.float32)
        residual_two, gain_two, shift_two = norm_backward(
            incoming, normal_two, inverse_two, full_gains[1]
        )
        feed_grad = residual_two.astype(jnp.bfloat16)
        fold_piece = lax.all_gather(feed_grad, "tensor", axis=0, tiled=True)
        down_grad = jnp.einsum(
            "rf,rd->fd", active_low, fold_piece, preferred_element_type=jnp.float32
        )
        fold_product = jnp.einsum(
            "rd,fd->rf", fold_piece, back_down, preferred_element_type=jnp.float32
        )
        active_grad = fold_product
        down_grad, active_grad = (down_grad, active_grad)
        layer_value, gelu_pull = jax.vjp(partial(jax.nn.gelu, approximate=False), pre_active)
        upper_grad = gelu_pull(active_grad)[0].astype(jnp.bfloat16)
        normed_grad = residual_two + lax.psum_scatter(
            jnp.einsum("rf,df->rd", upper_grad, back_up, preferred_element_type=jnp.float32).astype(
                jnp.bfloat16
            ),
            "tensor",
            scatter_dimension=0,
            tiled=True,
        ).astype(jnp.float32)
        up_grad = jnp.einsum(
            "ld,lf->df", normed_full, upper_grad, preferred_element_type=jnp.float32
        )
        up_bias_grad = jnp.sum(upper_grad.astype(jnp.float32), axis=0)
        residual_one, gain_one, shift_one = norm_backward(
            normed_grad, normal_one, inverse_one, full_gains[0]
        )
        branch_grad = residual_one.astype(jnp.bfloat16)

        def fold_branch(piece):
            out_grad = jnp.einsum(
                "rk,rd->kd", context_low, piece, preferred_element_type=jnp.float32
            )
            product = jnp.einsum("rd,kd->rk", piece, back_out, preferred_element_type=jnp.float32)
            return (out_grad, product)

        out_grad, context_grad = fold_branch(
            lax.all_gather(branch_grad, "tensor", axis=0, tiled=True)
        )
        context_grad = context_grad.astype(jnp.bfloat16).reshape(length, head_count, DH)
        query_grad, key_grad, value_grad = attention_backward(
            queries, key_heads, value_heads, prefix, totals, context_grad
        )
        mixed_grad = (
            jnp.stack([query_grad, key_grad, value_grad], axis=1)
            .astype(jnp.bfloat16)
            .reshape(length, 3, local_width)
        )
        qkv_grad = jnp.einsum(
            "ld,lce->dce", token_full, mixed_grad, preferred_element_type=jnp.float32
        )
        row_sums = jnp.sum(mixed_grad.astype(jnp.float32), axis=0)
        bias_grad = jnp.stack([row_sums[0], row_sums[2]])
        token_grad = residual_one + lax.psum_scatter(
            jnp.einsum(
                "rce,dce->rd", mixed_grad, back_qkv, preferred_element_type=jnp.float32
            ).astype(jnp.bfloat16),
            "tensor",
            scatter_dimension=0,
            tiled=True,
        ).astype(jnp.float32)
        input_grads.append(token_grad)
        gain_grads = gain_grads + jnp.stack([gain_one, gain_two])
        shift_grads = shift_grads + jnp.stack(
            [
                jnp.sum(branch_grad.astype(jnp.float32), axis=0),
                shift_one,
                jnp.sum(feed_grad.astype(jnp.float32), axis=0),
                shift_two,
            ]
        )
        member_grads = (qkv_grad, bias_grad, out_grad, up_grad, up_bias_grad, down_grad)
        weight_grads = tuple(
            (running + grad_part for running, grad_part in zip(weight_grads, member_grads))
        )
    total_qkv, total_bias, total_out, total_up, total_up_bias, total_down = weight_grads
    weight_grads = (
        lax.psum_scatter(total_qkv, "dp", scatter_dimension=0, tiled=True),
        lax.psum_scatter(total_bias, "dp", scatter_dimension=1, tiled=True),
        lax.psum_scatter(total_out, "dp", scatter_dimension=1, tiled=True),
        lax.psum_scatter(total_up, "dp", scatter_dimension=0, tiled=True),
        lax.psum_scatter(total_up_bias, "dp", scatter_dimension=0, tiled=True),
        lax.psum_scatter(total_down, "dp", scatter_dimension=1, tiled=True),
    )
    gain_share, shift_share = (
        lax.psum_scatter(gain_grads, ("dp", "tensor"), scatter_dimension=1, tiled=True),
        lax.psum_scatter(shift_grads, ("dp", "tensor"), scatter_dimension=1, tiled=True),
    )
    return (
        jnp.stack(outputs),
        jnp.stack(input_grads),
        weight_grads[0],
        weight_grads[1],
        weight_grads[2],
        weight_grads[3],
        weight_grads[4],
        weight_grads[5],
        gain_share,
        shift_share,
    )


def solution(mesh):
    return jax.shard_map(
        local,
        mesh=mesh,
        in_specs=(
            P("dp", "tensor", None),
            P("dp"),
            P("dp", None, "tensor"),
            P(None, ("tensor", "dp")),
            P("tensor", "dp"),
            P("dp", "tensor"),
            P(("tensor", "dp")),
            P("tensor", "dp"),
            P(None, ("dp", "tensor")),
            P(None, ("dp", "tensor")),
            P("dp", "tensor", None),
        ),
        out_specs=(
            P("dp", "tensor", None),
            P("dp", "tensor", None),
            P("dp", None, "tensor"),
            P(None, ("tensor", "dp")),
            P("tensor", "dp"),
            P("dp", "tensor"),
            P(("tensor", "dp")),
            P("tensor", "dp"),
            P(None, ("dp", "tensor")),
            P(None, ("dp", "tensor")),
        ),
        check_vma=False,
    )
```

profile of v0, /device:TPU:0, one launch (start us, length us, event | category | flops | bytes accessed | tf_op | source)
XLA Modules:
  0.0 962.3 jit_solution(8014112634982652375)
XLA Ops:
  10.9 10.4 %all-gather.2 = bf16[8,24,2]{1,2,0:T(2,128)(2,1)S(1)} all-gather(bf16[1,24,2]{1,2,0:T(2,128)(2,1)} %bitcast.353), channel_id=1, replica_groups=mesh['dp'=8,'tensor'=4] {'dp'}, dimensions={0}, use_global_device_ids=true | all-gather | bytes 864 | tf_op jit(solution)/shard_map/all_gather | solution.py:106
  23.5 13.3 %all_gather.53 = bf16[768,3,192]{2,1,0:T(4,128)(2,1)S(1)} all-gather(bf16[96,3,192]{2,1,0:T(4,128)(2,1)S(1)} %copy.42), channel_id=1, replica_groups=mesh['dp'=8,'tensor'=4] {'dp'}, dimensions={0}, use_global_device_ids=true | all-gather | bytes 995328 | tf_op jit(solution)/shard_map/all_gather | solution.py:105
  38.8 8.7 all_gather.55
  50.8 3.1 fusion.28
  56.3 32.5 %all-gather.32.cloned.1.call-done = bf16[1,1024,768]{2,1,0:T(8,128)(2,1)} async-done(((bf16[1,256,768]{2,1,0:T(8,128)(2,1)}), bf16[1,1024,768]{2,1,0:T(8,128)(2,1)}) %all-gather.32.cloned.1.call-update) | async-done | bytes 1572880 | tf_op jit(solution)/shard_map/all_gather | solution.py:133
  119.3 67.6 %all-gather.4 = bf16[32,24,2]{1,2,0:T(2,128)(2,1)S(1)} all-gather(bf16[1,24,2]{1,2,0:T(2,128)(2,1)S(1)} %bitcast.354), channel_id=1, replica_groups=mesh['dp'=8,'tensor'=4] {'dp','tensor'}, dimensions={0}, use_global_device_ids=true | all-gather | bytes 3168 | tf_op jit(solution)/shard_map/all_gather | solution.py:113
  187.2 63.6 %all-gather.3 = bf16[32,24,4]{1,2,0:T(4,128)(2,1)S(1)} all-gather(bf16[1,24,4]{1,2,0:T(4,128)(2,1)S(1)} %bitcast.352), channel_id=1, replica_groups=mesh['dp'=8,'tensor'=4] {'dp','tensor'}, dimensions={0}, use_global_device_ids=true | all-gather | bytes 6336 | tf_op jit(solution)/shard_map/all_gather | solution.py:114
  260.5 12.6 %all-reduce = bf16[768]{0:T(1024)(128)(2,1)S(1)} all-reduce(bf16[768]{0:T(1024)(128)(2,1)S(1)} %dynamic-update-slice), channel_id=1, replica_groups=mesh['dp'=8,'tensor'=4] {'dp'}, use_global_device_ids=true, to_apply=%add | all-reduce | flops 768 | bytes 3072
  273.1 19.5 %all-gather.22.cloned.1.call-done = bf16[1024,768]{1,0:T(8,128)(2,1)} async-done(((bf16[256,768]{1,0:T(8,128)(2,1)}), bf16[1024,768]{1,0:T(8,128)(2,1)}) %all-gather.22.cloned.1.call-update) | async-done | bytes 1572880 | tf_op jit(solution)/shard_map/all_gather | solution.py:165
  292.6 4.9 fusion.109
  297.5 32.9 %all-gather.16.cloned.1.call-done = bf16[1024,768]{1,0:T(8,128)(2,1)} async-done(((bf16[256,768]{1,0:T(8,128)(2,1)}), bf16[1024,768]{1,0:T(8,128)(2,1)}) %all-gather.16.cloned.1.call-update) | async-done | bytes 1572880 | tf_op jit(solution)/shard_map/all_gather | solution.py:165
  330.4 17.3 %multiply_convert_fusion.5 = (bf16[1024,768]{1,0:T(8,128)(2,1)}, f32[1024,768]{1,0:T(8,128)}, bf16[1024,768]{1,0:T(8,128)(2,1)}, f32[1024,768]{1,0:T(8,128)}, f32[1024,768]{1,0:T(8,128)}) fusion(f32[768]{0:T(1024)S(1)} %convert_element_type.221, f32[1024,768]{1,0:T(8,128)} %fusion.109, bf16[1024,768]{1,0:T(8,128)(2,1)} %all-gather.16.cloned.1.call-done, ...), kind=kOutput, calls=%fused_computation.51 | convolution fusion | flops 1311768576 | bytes 18484224 | tf_op jit(solution)/shard_map/dot_general | solution.py:161
  347.7 7.3 all-gather.20.cloned.1.call-done
  355.1 4.4 convolution_convert_fusion.4
  359.5 4.0 convolution_convert_fusion.2
  363.6 31.4 %reduce-scatter.22.cloned.1.call-done = bf16[256,768]{1,0:T(8,128)(2,1)} async-done(((bf16[1024,768]{1,0:T(8,128)(2,1)}), bf16[256,768]{1,0:T(8,128)(2,1)}) %reduce-scatter.22.cloned.1.call-update) | async-done | bytes 393232 | tf_op jit(solution)/shard_map/reduce_scatter | solution.py:170
  395.0 36.6 %reduce-scatter.26.cloned.1.call-done = bf16[256,768]{1,0:T(8,128)(2,1)} async-done(((bf16[1024,768]{1,0:T(8,128)(2,1)}), bf16[256,768]{1,0:T(8,128)(2,1)}) %reduce-scatter.26.cloned.1.call-update) | async-done | bytes 393232 | tf_op jit(solution)/shard_map/reduce_scatter | solution.py:170
  436.5 3.0 convert_reduce_fusion.8
  440.3 35.2 %all-gather.24.cloned.1.call-done = bf16[1024,768]{1,0:T(8,128)(2,1)} async-done(((bf16[256,768]{1,0:T(8,128)(2,1)}), bf16[1024,768]{1,0:T(8,128)(2,1)}) %all-gather.24.cloned.1.call-update) | async-done | bytes 1572880 | tf_op jit(solution)/shard_map/all_gather | solution.py:244
  475.5 4.8 fusion.110
  480.2 32.6 %all-gather.28.cloned.1.call-done = bf16[1024,768]{1,0:T(8,128)(2,1)} async-done(((bf16[256,768]{1,0:T(8,128)(2,1)}), bf16[1024,768]{1,0:T(8,128)(2,1)}) %all-gather.28.cloned.1.call-update) | async-done | bytes 1572880 | tf_op jit(solution)/shard_map/all_gather | solution.py:244
  512.8 11.5 %convert_reduce_fusion = (f32[768]{0:T(1024)}, bf16[1024,768]{1,0:T(8,128)(2,1)}, f32[768]{0:T(1024)}, bf16[1024,768]{1,0:T(8,128)(2,1)S(1)}) fusion(f32[1024,768]{1,0:T(8,128)} %get-tuple-element.138, f32[1024,768]{1,0:T(8,128)} %fusion.109, f32[768]{0:T(1024)S(1)} %convert_element_type.221, f32[1024,768]{1,0:T(8,128)} %fusion.110, ...), kind=kOutput, calls=%fused_computation.34 | convolution fusion | flops 1234696704 | bytes 21636096 | tf_op jit(solution)/shard_map/rd,fd->rf/dot_general | solution.py:248
  528.3 4.4 convolution_convert_fusion
  532.8 29.8 %reduce-scatter.28.cloned.1.call-done = bf16[256,768]{1,0:T(8,128)(2,1)} async-done(((bf16[1024,768]{1,0:T(8,128)(2,1)}), bf16[256,768]{1,0:T(8,128)(2,1)}) %reduce-scatter.28.cloned.1.call-update) | async-done | bytes 393232 | tf_op jit(solution)/shard_map/reduce_scatter | solution.py:255
  562.6 36.4 %reduce-scatter.32.cloned.1.call-done = bf16[256,768]{1,0:T(8,128)(2,1)} async-done(((bf16[1024,768]{1,0:T(8,128)(2,1)}), bf16[256,768]{1,0:T(8,128)(2,1)}) %reduce-scatter.32.cloned.1.call-update) | async-done | bytes 393232 | tf_op jit(solution)/shard_map/reduce_scatter | solution.py:255
  599.1 2.8 multiply_reduce_fusion.5
  601.9 4.2 convert_reduce_fusion.9
  606.9 35.2 %all-gather.30.cloned.1.call-done = bf16[1024,768]{1,0:T(8,128)(2,1)} async-done(((bf16[256,768]{1,0:T(8,128)(2,1)}), bf16[1024,768]{1,0:T(8,128)(2,1)}) %all-gather.30.cloned.1.call-update) | async-done | bytes 1572880 | tf_op jit(solution)/shard_map/all_gather | solution.py:280
  644.3 6.5 multiply_reduce_fusion
  650.9 4.3 multiply_reduce_fusion.1
  655.2 7.7 multiply_convert_fusion
  669.0 10.6 %all-gather.26.cloned.1.call-done = bf16[1024,768]{1,0:T(8,128)(2,1)} async-done(((bf16[256,768]{1,0:T(8,128)(2,1)}), bf16[1024,768]{1,0:T(8,128)(2,1)}) %all-gather.26.cloned.1.call-update) | async-done | bytes 1572880 | tf_op jit(solution)/shard_map/all_gather | solution.py:280
  681.8 5.6 fusion.88
  687.4 6.3 multiply_reduce_fusion.3
  693.8 4.3 multiply_reduce_fusion.2
  698.1 8.0 multiply_convert_fusion.2
  711.8 5.1 fusion.40
  729.0 3.1 copy.64
  737.6 3.5 fusion.115
  741.1 3.0 convolution_add_fusion
  744.2 3.0 fusion.114
  747.3 2.9 convolution_add_fusion.1
  758.8 39.7 %all-reduce.5 = (f32[2,768]{1,0:T(2,128)S(1)}, f32[4,768]{1,0:T(4,128)S(1)}) all-reduce(f32[2,768]{1,0:T(2,128)S(1)} %maximum_add_fusion.1, f32[4,768]{1,0:T(4,128)S(1)} %maximum_add_fusion), channel_id=18, replica_groups=mesh['dp'=8,'tensor'=4] {'dp','tensor'}, use_global_device_ids=true, to_apply=%region_50.51.clone | all-reduce | flops 4608 | bytes 36864
  802.3 13.8 %all-reduce.6 = (f32[2,192]{1,0:T(2,128)S(1)}, f32[768]{0:T(1024)S(1)}) all-reduce(f32[2,192]{1,0:T(2,128)S(1)} %maximum_add_fusion.2, f32[768]{0:T(1024)S(1)} %add.355), channel_id=13, replica_groups=mesh['dp'=8,'tensor'=4] {'dp'}, use_global_device_ids=true, to_apply=%region_39.40.clone | all-reduce | flops 1152 | bytes 9216
  820.9 6.0 reduce-scatter.34.cloned.1.call-done
  828.0 35.5 %reduce-scatter.30.cloned.1.call-done = bf16[256,768]{1,0:T(8,128)(2,1)} async-done(((bf16[1024,768]{1,0:T(8,128)(2,1)}), bf16[256,768]{1,0:T(8,128)(2,1)}) %reduce-scatter.30.cloned.1.call-update) | async-done | bytes 393232 | tf_op jit(solution)/shard_map/reduce_scatter | solution.py:296
  865.8 42.5 %reduce-scatter.38.cloned.1.call-done = f32[768,96]{0,1:T(8,128)} async-done(((f32[768,768]{0,1:T(8,128)}), f32[768,96]{0,1:T(8,128)}) %reduce-scatter.38.cloned.1.call-update) | async-done | bytes 294928 | tf_op jit(solution)/shard_map/reduce_scatter | solution.py:325
  908.3 46.2 %reduce-scatter.36.cloned.1.call-done = f32[96,768]{1,0:T(8,128)} async-done(((f32[768,768]{1,0:T(8,128)}), f32[96,768]{1,0:T(8,128)}) %reduce-scatter.36.cloned.1.call-update) | async-done | bytes 294928 | tf_op jit(solution)/shard_map/reduce_scatter | solution.py:323
  (393 shorter events, 114.8 us)
Async XLA Ops:
  8.0 42.8 %all-gather.34.cloned.1.call-start = ((), (), s32[]{:S(2)}) async-start(), calls=%async_computation.31 | async-start | bytes 1966080 | tf_op jit(solution)/shard_map/all_gather | solution.py:133
  10.1 37.4 %copy-start.76 = (s32[2]{0:T(128)S(1)}, s32[2]{0:T(128)}, u32[]{:S(2)}) copy-start(s32[2]{0:T(128)} %param.12) | copy-start | bytes 28
  10.1 78.7 %all-gather.32.cloned.1.call-start = ((), (), s32[]{:S(2)}) async-start(), calls=%async_computation.30 | async-start | bytes 1966080 | tf_op jit(solution)/shard_map/all_gather | solution.py:133
  10.9 240.3 %reduce-scatter.20.cloned.1.call-start = ((), (), s32[]{:S(2)}) async-start(), calls=%async_computation.12 | async-start | bytes 1966080 | tf_op jit(solution)/shard_map/reduce_scatter | solution.py:145
  47.5 69.2 %copy-start.24 = (bf16[192,768]{0,1:T(8,128)(2,1)}, bf16[192,768]{0,1:T(8,128)(2,1)S(1)}, u32[]{:S(2)}) copy-start(bf16[192,768]{0,1:T(8,128)(2,1)S(1)} %all_gather.55) | copy-start | bytes 884740
  50.4 50.1 %copy-start.14 = (pred[512,1024]{1,0:T(8,128)(4,1)}, pred[512,1024]{1,0:T(8,128)(4,1)S(1)}, u32[]{:S(2)}) copy-start(pred[512,1024]{1,0:T(8,128)(4,1)S(1)} %get-tuple-element.146) | copy-start | bytes 1572868
  50.4 52.0 %copy-start.9 = (pred[512,1024]{1,0:T(8,128)(4,1)}, pred[512,1024]{1,0:T(8,128)(4,1)S(1)}, u32[]{:S(2)}) copy-start(pred[512,1024]{1,0:T(8,128)(4,1)S(1)} %get-tuple-element.139) | copy-start | bytes 1572868
  50.4 62.4 %copy-start.12 = (pred[512,1024]{1,0:T(8,128)(4,1)}, pred[512,1024]{1,0:T(8,128)(4,1)S(1)}, u32[]{:S(2)}) copy-start(pred[512,1024]{1,0:T(8,128)(4,1)S(1)} %get-tuple-element.140) | copy-start | bytes 1572868
  50.4 64.3 %copy-start.16 = (pred[512,1024]{1,0:T(8,128)(4,1)}, pred[512,1024]{1,0:T(8,128)(4,1)S(1)}, u32[]{:S(2)}) copy-start(pred[512,1024]{1,0:T(8,128)(4,1)S(1)} %get-tuple-element.145) | copy-start | bytes 1572868
  55.3 54.3 %copy-start.18 = (bf16[1024,1,192]{0,2,1:T(8,128)(2,1)}, bf16[1024,1,192]{0,2,1:T(8,128)(2,1)S(1)}, u32[]{:S(2)}) copy-start(bf16[1024,1,192]{0,2,1:T(8,128)(2,1)S(1)} %slice.259) | copy-start | bytes 1179652
  93.9 12.6 %copy-start.48 = (bf16[512,192]{0,1:T(8,128)(2,1)}, bf16[512,192]{0,1:T(8,128)(2,1)S(1)}, u32[]{:S(2)}) copy-start(bf16[512,192]{0,1:T(8,128)(2,1)S(1)} %get-tuple-element.130) | copy-start | bytes 589828
  100.4 14.3 %copy-start.41 = (bf16[1024,3,64]{0,2,1:T(8,128)(2,1)}, bf16[1024,3,64]{0,2,1:T(8,128)(2,1)S(1)}, u32[]{:S(2)}) copy-start(bf16[1024,3,64]{0,2,1:T(8,128)(2,1)S(1)} %get-tuple-element.142) | copy-start | bytes 1179652
  106.2 146.3 %reduce-scatter.24.cloned.1.call-start = ((), (), s32[]{:S(2)}) async-start(), calls=%async_computation.17 | async-start | bytes 1966080 | tf_op jit(solution)/shard_map/reduce_scatter | solution.py:145
  116.7 70.5 %copy-start.77 = (bf16[4,24]{1,0:T(4,128)(2,1)S(1)}, bf16[4,24]{1,0:T(4,128)(2,1)}, u32[]{:S(2)}) copy-start(bf16[4,24]{1,0:T(4,128)(2,1)} %param.20) | copy-start | bytes 580
  116.7 134.5 %copy-start.4 = (bf16[2,256,768]{2,1,0:T(8,128)(2,1)S(1)}, bf16[2,256,768]{2,1,0:T(8,128)(2,1)}, u32[]{:S(2)}) copy-start(bf16[2,256,768]{2,1,0:T(8,128)(2,1)} %param.11) | copy-start | bytes 2359300
  116.7 137.2 %copy-start.37 = (bf16[1024,3,64]{0,2,1:T(8,128)(2,1)}, bf16[1024,3,64]{0,2,1:T(8,128)(2,1)S(1)}, u32[]{:S(2)}) copy-start(bf16[1024,3,64]{0,2,1:T(8,128)(2,1)S(1)} %pad_maximum_fusion.5) | copy-start | bytes 1179652
  118.6 154.5 %all-gather.18.cloned.1.call-start = ((), (), s32[]{:S(2)}) async-start(), calls=%async_computation.14 | async-start | bytes 1327104 | tf_op jit(solution)/shard_map/all_gather | solution.py:108
  119.2 173.4 %all-gather.22.cloned.1.call-start = ((), (), s32[]{:S(2)}) async-start(), calls=%async_computation.18 | async-start | bytes 1966080 | tf_op jit(solution)/shard_map/all_gather | solution.py:165
  257.6 72.8 %all-gather.16.cloned.1.call-start = ((), (), s32[]{:S(2)}) async-start(), calls=%async_computation.13 | async-start | bytes 1966080 | tf_op jit(solution)/shard_map/all_gather | solution.py:165
  258.2 96.9 %all-gather.20.cloned.1.call-start = ((), (), s32[]{:S(2)}) async-start(), calls=%async_computation.15 | async-start | bytes 1327104 | tf_op jit(solution)/shard_map/all_gather | solution.py:110
  258.9 136.1 %reduce-scatter.22.cloned.1.call-start = ((), (), s32[]{:S(2)}) async-start(), calls=%async_computation.16 | async-start | bytes 1966080 | tf_op jit(solution)/shard_map/reduce_scatter | solution.py:170
  273.1 57.3 %copy-start.84 = (bf16[768,768]{1,0:T(8,128)(2,1)S(1)}, bf16[768,768]{1,0:T(8,128)(2,1)}, u32[]{:S(2)}) copy-start(bf16[768,768]{1,0:T(8,128)(2,1)} %all-gather.18.cloned.1.call-done) | copy-start | bytes 3538948
  359.5 72.1 %reduce-scatter.26.cloned.1.call-start = ((), (), s32[]{:S(2)}) async-start(), calls=%async_computation.19 | async-start | bytes 1966080 | tf_op jit(solution)/shard_map/reduce_scatter | solution.py:170
  359.5 72.0 %copy-start.8 = (bf16[256,768]{1,0:T(8,128)(2,1)S(1)}, bf16[256,768]{1,0:T(8,128)(2,1)}, u32[]{:S(2)}) copy-start(bf16[256,768]{1,0:T(8,128)(2,1)} %reduce-scatter.24.cloned.1.call-done) | copy-start | bytes 1179652
  363.6 111.9 %all-gather.24.cloned.1.call-start = ((), (), s32[]{:S(2)}) async-start(), calls=%async_computation.20 | async-start | bytes 1966080 | tf_op jit(solution)/shard_map/all_gather | solution.py:244
  439.5 73.3 %all-gather.28.cloned.1.call-start = ((), (), s32[]{:S(2)}) async-start(), calls=%async_computation.24 | async-start | bytes 1966080 | tf_op jit(solution)/shard_map/all_gather | solution.py:244
  440.1 122.5 %reduce-scatter.28.cloned.1.call-start = ((), (), s32[]{:S(2)}) async-start(), calls=%async_computation.21 | async-start | bytes 1966080 | tf_op jit(solution)/shard_map/reduce_scatter | solution.py:255
  512.8 12.7 %copy-start.85 = (bf16[768,768]{1,0:T(8,128)(2,1)S(1)}, bf16[768,768]{1,0:T(8,128)(2,1)}, u32[]{:S(2)}) copy-start(bf16[768,768]{1,0:T(8,128)(2,1)} %all-gather.18.cloned.1.call-done) | copy-start | bytes 3538948
  528.2 70.8 %reduce-scatter.32.cloned.1.call-start = ((), (), s32[]{:S(2)}) async-start(), calls=%async_computation.25 | async-start | bytes 1966080 | tf_op jit(solution)/shard_map/reduce_scatter | solution.py:255
  528.3 70.8 %copy-start.28 = (f32[256,768]{1,0:T(8,128)S(1)}, f32[256,768]{1,0:T(8,128)}, u32[]{:S(2)}) copy-start(f32[256,768]{1,0:T(8,128)} %get-tuple-element.95) | copy-start | bytes 2359300
  528.3 70.8 %copy-start.29 = (f32[256,768]{1,0:T(8,128)S(1)}, f32[256,768]{1,0:T(8,128)}, u32[]{:S(2)}) copy-start(f32[256,768]{1,0:T(8,128)} %get-tuple-element.120) | copy-start | bytes 2359300
  532.7 109.4 %all-gather.30.cloned.1.call-start = ((), (), s32[]{:S(2)}) async-start(), calls=%async_computation.26 | async-start | bytes 1966080 | tf_op jit(solution)/shard_map/all_gather | solution.py:280
  601.9 49.0 %slice-start.8 = ((s8[6291456]{0:T(1024)(128)(4,1)}), s8[2097152]{0:T(1024)(128)(4,1)S(1)}, s32[]{:S(2)}) async-start(s8[6291456]{0:T(1024)(128)(4,1)} %bitcast.286), calls=%async_computation.42 | async-start | bytes 4194304
  606.1 38.2 %copy-start.13 = (pred[512,1024]{1,0:T(8,128)(4,1)S(1)}, pred[512,1024]{1,0:T(8,128)(4,1)}, u32[]{:S(2)}) copy-start(pred[512,1024]{1,0:T(8,128)(4,1)} %copy-done.12) | copy-start | bytes 1572868
  606.1 73.5 %all-gather.26.cloned.1.call-start = ((), (), s32[]{:S(2)}) async-start(), calls=%async_computation.22 | async-start | bytes 1966080 | tf_op jit(solution)/shard_map/all_gather | solution.py:280
  606.9 210.4 %reduce-scatter.42.cloned.1.call-start = ((), (), s32[]{:S(2)}) async-start(), calls=%async_computation.33 | async-start | bytes 884736
  666.3 13.3 %copy-start.25 = (bf16[192,768]{0,1:T(8,128)(2,1)S(1)}, bf16[192,768]{0,1:T(8,128)(2,1)}, u32[]{:S(2)}) copy-start(bf16[192,768]{0,1:T(8,128)(2,1)} %copy-done.24) | copy-start | bytes 884740
  669.0 12.8 %copy-start.15 = (pred[512,1024]{1,0:T(8,128)(4,1)S(1)}, pred[512,1024]{1,0:T(8,128)(4,1)}, u32[]{:S(2)}) copy-start(pred[512,1024]{1,0:T(8,128)(4,1)} %copy-done.14) | copy-start | bytes 1572868
  669.0 12.8 %copy-start.70 = (f32[3,512]{1,0:T(4,128)S(1)}, f32[3,512]{1,0:T(4,128)}, u32[]{:S(2)}) copy-start(f32[3,512]{1,0:T(4,128)} %copy-done.69) | copy-start | bytes 18436
  681.7 12.0 %copy-start.62 = (bf16[512,192]{0,1:T(8,128)(2,1)}, bf16[512,192]{0,1:T(8,128)(2,1)S(1)}, u32[]{:S(2)}) copy-start(bf16[512,192]{0,1:T(8,128)(2,1)S(1)} %get-tuple-element.123) | copy-start | bytes 589828
  681.8 12.0 %slice-start = ((s8[6291456]{0:T(1024)(128)(4,1)}), s8[4194304]{0:T(1024)(128)(4,1)S(1)}, s32[]{:S(2)}) async-start(s8[6291456]{0:T(1024)(128)(4,1)} %bitcast.278), calls=%async_computation.34 | async-start | bytes 8388608
  711.8 107.2 %reduce-scatter.40.cloned.1.call-start = ((), (), s32[]{:S(2)}) async-start(), calls=%async_computation.32 | async-start | bytes 2211840
  732.1 94.8 %reduce-scatter.34.cloned.1.call-start = ((), (), s32[]{:S(2)}) async-start(), calls=%async_computation.27 | async-start | bytes 1966080 | tf_op jit(solution)/shard_map/reduce_scatter | solution.py:296
  734.8 128.7 %reduce-scatter.30.cloned.1.call-start = ((), (), s32[]{:S(2)}) async-start(), calls=%async_computation.23 | async-start | bytes 1966080 | tf_op jit(solution)/shard_map/reduce_scatter | solution.py:296
  737.5 170.8 %reduce-scatter.38.cloned.1.call-start = ((), (), s32[]{:S(2)}) async-start(), calls=%async_computation.29 | async-start | bytes 2654208 | tf_op jit(solution)/shard_map/reduce_scatter | solution.py:325
  744.2 210.4 %reduce-scatter.36.cloned.1.call-start = ((), (), s32[]{:S(2)}) async-start(), calls=%async_computation.28 | async-start | bytes 2654208 | tf_op jit(solution)/shard_map/reduce_scatter | solution.py:323
  751.6 75.3 %copy-start.44 = (f32[256,768]{1,0:T(8,128)S(1)}, f32[256,768]{1,0:T(8,128)}, u32[]{:S(2)}) copy-start(f32[256,768]{1,0:T(8,128)} %get-tuple-element.114) | copy-start | bytes 2359300
  755.2 108.3 %copy-start.43 = (f32[256,768]{1,0:T(8,128)S(1)}, f32[256,768]{1,0:T(8,128)}, u32[]{:S(2)}) copy-start(f32[256,768]{1,0:T(8,128)} %get-tuple-element.92) | copy-start | bytes 2359300
  (76 other events, 285.5 us)
Sparse Core Ops, SparseCore 0:
  11.0 39.7 all-gather.33
  52.9 35.8 all-gather.31
  106.3 34.3 reduce-scatter.19
  142.9 34.4 reduce-scatter.23
  439.6 35.8 all-gather.23
  476.9 35.8 all-gather.27
  606.3 35.8 all-gather.29
  643.7 35.8 all-gather.25
Sparse Core Ops, SparseCore 1:
  121.0 22.6 all-gather.17
  257.7 34.8 all-gather.21
  294.6 35.7 all-gather.15
  332.3 22.7 all-gather.19
  359.6 35.4 reduce-scatter.21
  397.3 34.2 reduce-scatter.25
  528.3 34.3 reduce-scatter.27
  564.8 34.2 reduce-scatter.31
  711.8 33.8 reduce-scatter.41
  749.1 40.2 reduce-scatter.39
  791.5 35.4 reduce-scatter.33
  829.2 34.2 reduce-scatter.29
  867.3 41.0 reduce-scatter.37
  912.3 42.2 reduce-scatter.35
where the time goes:
time: 972 us; the launch traced here: 962 us
  waiting for transfers between devices  475 us (49%)
  blocking collectives  230 us (24%)
  matrix products  150 us (15%)
  other arithmetic  56.6 us (6%)
  local copies, waits for them, and re-layouts  30.7 us (3%)
  between operations  19.7 us (2%)
    reduce_scatter x2, waiting for transfers between devices, local(): lax.psum_scatter(jnp.dot(active_low, full_down, preferred_element_type=jn...  67.9 us
    all_gather x2, waiting for transfers between devices, local(): fold_piece = lax.all_gather(feed_grad, 'tensor', axis=0, tiled=True)  67.8 us
    all_gather x1, blocking collectives, local(): lax.all_gather(gains, ('dp', 'tensor'), axis=1, tiled=True)  67.6 us
    reduce_scatter x2, waiting for transfers between devices, local(): lax.psum_scatter(jnp.einsum('rf,df->rd', upper_grad, back_up, preferred_e...  66.3 us
    unnamed x3, blocking collectives  66.1 us
    all_gather x1, blocking collectives, local(): lax.all_gather(shifts, ('dp', 'tensor'), axis=1, tiled=True)  63.6 us
    all_gather x2, waiting for transfers between devices, local(): lax.all_gather(normed_low, 'tensor', axis=0, tiled=True)  52.4 us
    reduce_scatter x1, waiting for transfers between devices, local(): lax.psum_scatter(total_up, 'dp', scatter_dimension=0, tiled=True)  46.2 us
  transfers between devices with their start and end apart: 22, of which 17 were waited for; matrix products, arithmetic and copies ran while one was open for 15% of the time, Pallas kernels for 0%

commit v1 on v0

--- a/solution.py
+++ b/solution.py
@@ -3,6 +3,8 @@
 import jax
 import jax.numpy as jnp
 from jax import lax
+from jax.experimental import pallas as pl
+from jax.experimental.pallas import tpu as pltpu
 from jax.sharding import PartitionSpec as P
 
 DH = 64
@@ -342,9 +344,1091 @@
     )
 
 
+MESH_ID = pl.DeviceIdType.MESH
+BF = jnp.bfloat16
+F32 = jnp.float32
+ROWS = 96
+SMALL = 16
+
+
+def place():
+    d = lax.axis_index("dp")
+    t = lax.axis_index("tensor")
+    k, c = d // 2, d % 2
+    xb, yb = k % 2, k // 2
+    dx = d + 2 - 4 * xb
+    dy = d + 4 - 8 * yb
+    return d, t, k, c, xb, yb, dx, dy
+
+
+def remote(src, dst, send, recv, dp, tensor):
+    return pltpu.make_async_remote_copy(
+        src_ref=src,
+        dst_ref=dst,
+        send_sem=send,
+        recv_sem=recv,
+        device_id=(dp, tensor),
+        device_id_type=MESH_ID,
+    )
+
+
+def enter(k, c, t, d, dx, dy):
+    barrier = pltpu.get_barrier_semaphore()
+
+    def greet(dp, tensor):
+        pl.semaphore_signal(barrier, inc=1, device_id=(dp, tensor), device_id_type=MESH_ID)
+
+    greet(dx, t)
+    greet(dy, t)
+    greet(d + 1 - 2 * c, t)
+    for step in range(1, 4):
+        other = (t + step) % 4
+        greet(2 * k, other)
+        greet(2 * k + 1, other)
+    pl.semaphore_wait(barrier, 9)
+
+
+def pair_swap(part):
+    def kernel(src, dst, send, recv):
+        d, t, k, c, xb, yb, dx, dy = place()
+        mate = d + 1 - 2 * c
+        barrier = pltpu.get_barrier_semaphore()
+        pl.semaphore_signal(barrier, inc=1, device_id=(mate, t), device_id_type=MESH_ID)
+        pl.semaphore_wait(barrier, 1)
+        rows = src.shape[0] // 4
+        copies = [
+            remote(
+                src.at[pl.ds(i * rows, rows)],
+                dst.at[pl.ds(i * rows, rows)],
+                send.at[i],
+                recv.at[i],
+                mate,
+                t,
+            )
+            for i in range(4)
+        ]
+        for copy in copies:
+            copy.start()
+        for copy in copies:
+            copy.wait()
+
+    return pl.pallas_call(
+        kernel,
+        out_shape=jax.ShapeDtypeStruct(part.shape, part.dtype),
+        in_specs=[pl.BlockSpec(memory_space=pl.ANY)],
+        out_specs=pl.BlockSpec(memory_space=pl.ANY),
+        scratch_shapes=[pltpu.SemaphoreType.DMA((4,)), pltpu.SemaphoreType.DMA((4,))],
+        compiler_params=pltpu.CompilerParams(collective_id=3, has_side_effects=True),
+    )(part)
+
+
+def skewed(chunks, levels):
+    for slot in range(chunks + len(levels) - 1):
+        for level in reversed(range(len(levels))):
+            if 0 <= slot - level < chunks:
+                levels[level](slot - level)
+
+
+def gather_all(tokens, cotangent, shards, chunks):
+    half = tokens.shape[1] // 2
+    width = tokens.shape[2]
+    count = len(shards)
+    n_chunks = len(chunks)
+    rows_of = [s.shape[0] for s in shards]
+
+    def kernel(*refs):
+        tok, cot = refs[0], refs[1]
+        own = refs[2 : 2 + count]
+        base = 2 + count
+        xf, cf = refs[base], refs[base + 1]
+        full = refs[base + 2 : base + 2 + count]
+        small_other = refs[base + 2 + count]
+        (
+            stage,
+            row_stage,
+            local_sem,
+            row_sem,
+            ex_send,
+            ex_recv,
+            fw_send,
+            fw_recv,
+            p_send,
+            p_recv,
+            z_send,
+            z_recv,
+            a_send,
+            a_recv,
+            b_send,
+            b_recv,
+            o_send,
+            o_recv,
+        ) = (
+            refs[base + 3 + count : base + 3 + 2 * count],
+            *refs[base + 3 + 2 * count :],
+        )
+        d, t, k, c, xb, yb, dx, dy = place()
+        mate = d + 1 - 2 * c
+        u = t + c * (3 - 2 * t)
+        up = t + 1 - 2 * c
+        down = t - 1 + 2 * c
+        source = t // 2 == c
+        enter(k, c, t, d, dx, dy)
+
+        for s in range(count):
+            rows = rows_of[s]
+            spot = full[s].at[t % 2, pl.ds(d * rows, rows)]
+
+            @pl.when(source)
+            def _():
+                pltpu.make_async_copy(own[s], stage[s], local_sem.at[s]).start()
+
+            @pl.when(jnp.logical_not(source))
+            def _():
+                remote(own[s], spot, p_send.at[s], p_recv.at[s], mate, t).start()
+
+        def exchange(which, src, dst):
+            for m in range(2):
+                goal = 2 * c + m
+                for core in range(2):
+                    piece = src.at[m, pl.ds(core * half, half)]
+                    spot = dst.at[t * 2 + core]
+                    here = jnp.logical_and(goal == t, core == c)
+
+                    @pl.when(here)
+                    def _():
+                        load = pltpu.make_async_copy(piece, row_stage, row_sem)
+                        load.start()
+                        load.wait()
+                        store = pltpu.make_async_copy(row_stage, spot, row_sem)
+                        store.start()
+                        store.wait()
+
+                    @pl.when(jnp.logical_not(here))
+                    def _():
+                        remote(
+                            piece,
+                            spot,
+                            ex_send.at[which, 2 * m + core],
+                            ex_recv.at[which, t],
+                            2 * k + core,
+                            goal,
+                        ).start()
+
+        def relay(which, dst):
+            for origin in range(4):
+                spot = dst.at[origin * 2 + c]
+                local = jnp.logical_and(origin == t, c == t // 2)
+
+                @pl.when(jnp.logical_not(local))
+                def _():
+                    remote(
+                        spot, spot, ex_send.at[which, 0], ex_recv.at[which, origin], mate, t
+                    ).wait_recv()
+
+                remote(
+                    spot, spot, fw_send.at[which, origin], fw_recv.at[which, origin], mate, t
+                ).start()
+
+        def settle(which, src, dst):
+            for origin in range(4):
+                spot = dst.at[origin * 2 + 1 - c]
+                remote(
+                    spot, spot, fw_send.at[which, origin], fw_recv.at[which, origin], mate, t
+                ).wait()
+            for m in range(2):
+                for core in range(2):
+                    here = jnp.logical_and(2 * c + m == t, core == c)
+
+                    @pl.when(jnp.logical_not(here))
+                    def _():
+                        remote(
+                            src.at[m, pl.ds(core * half, half)],
+                            dst.at[t * 2 + core],
+                            ex_send.at[which, 2 * m + core],
+                            ex_recv.at[which, t],
+                            mate,
+                            t,
+                        ).wait_send()
+
+        exchange(0, tok, xf)
+
+        for s in range(count):
+
+            @pl.when(source)
+            def _():
+                rows = rows_of[s]
+                spot = full[s].at[t % 2, pl.ds(d * rows, rows)]
+                pltpu.make_async_copy(own[s], stage[s], local_sem.at[s]).wait()
+                pltpu.make_async_copy(stage[s], spot, local_sem.at[s]).start()
+
+        exchange(1, cot, cf)
+
+        def block(i, b, start, n):
+            s, col, cols = chunks[i]
+            zz = b + c * (1 - 2 * b)
+            rows = rows_of[s]
+            return full[s].at[zz, pl.ds(start * rows, n * rows), pl.ds(col, cols)]
+
+        def z_copy(i, b, way, target):
+            ref = block(i, b, 2 * k, 2)
+            return remote(ref, ref, z_send.at[i, b, way], z_recv.at[i, b], d, target)
+
+        def first_copy(i, b):
+            ref = block(i, b, 2 * k, 2)
+            return remote(ref, ref, a_send.at[i, b], a_recv.at[i, b], dx if b == 0 else dy, t)
+
+        def first_arrival(i, b):
+            near = k + 1 - 2 * xb if b == 0 else k + 2 - 4 * yb
+            ref = block(i, b, 2 * near, 2)
+            return remote(ref, ref, a_send.at[i, b], a_recv.at[i, b], dx if b == 0 else dy, t)
+
+        def second_copies(i, arriving):
+            other = 1 if arriving else 0
+            row = yb + other * (1 - 2 * yb)
+            ref = block(i, 0, 4 * row, 4)
+            col = xb + other * (1 - 2 * xb)
+            out = [remote(ref, ref, b_send.at[i, 0], b_recv.at[i, 0], dy, t)]
+            for r in range(2):
+                ref = block(i, 1, 2 * (2 * r + col), 2)
+                out.append(remote(ref, ref, b_send.at[i, 1 + r], b_recv.at[i, 1 + r], dx, t))
+            return out
+
+        def spread(i, b):
+            @pl.when(jnp.logical_and(u >= b, u < 3))
+            def _():
+                z_copy(i, b, 0, up).start()
+
+            if b == 1:
+
+                @pl.when(u == 1)
+                def _():
+                    z_copy(i, 1, 1, down).start()
+
+            first_copy(i, b).start()
+
+        waited = set()
+
+        def own_ready(i):
+            s = chunks[i][0]
+            if s in waited:
+                return
+            waited.add(s)
+            rows = rows_of[s]
+            spot = full[s].at[t % 2, pl.ds(d * rows, rows)]
+            twin = full[s].at[t % 2, pl.ds(mate * rows, rows)]
+            pltpu.make_async_copy(stage[s], spot, local_sem.at[s]).wait()
+            remote(twin, twin, p_send.at[s], p_recv.at[s], mate, t).wait_recv()
+
+        def level_own(i):
+            if chunks[i][0] not in waited:
+
+                @pl.when(source)
+                def _():
+                    own_ready(i)
+
+            for b in range(2):
+
+                @pl.when(u == b)
+                def _():
+                    spread(i, b)
+
+        def level_line(i):
+            for b in (1, 0):
+
+                @pl.when(u != b)
+                def _():
+                    z_copy(i, b, 0, up).wait_recv()
+                    spread(i, b)
+
+        def level_second(i):
+            for b in range(2):
+                first_arrival(i, b).wait_recv()
+            for copy in second_copies(i, False):
+                copy.start()
+
+        def level_done(i):
+            for copy in second_copies(i, True):
+                copy.wait_recv()
+
+        level_own(0)
+        relay(0, xf)
+        skewed(
+            n_chunks,
+            [(lambda i: None if i == 0 else level_own(i)), level_line, level_second, level_done],
+        )
+        relay(1, cf)
+        last = count - 1
+        swap = remote(full[last], small_other, o_send, o_recv, mate, t)
+        swap.start()
+        settle(0, tok, xf)
+        settle(1, cot, cf)
+        for s in range(count):
+            rows = rows_of[s]
+            spot = full[s].at[t % 2, pl.ds(d * rows, rows)]
+
+            @pl.when(jnp.logical_not(source))
+            def _():
+                remote(own[s], spot, p_send.at[s], p_recv.at[s], mate, t).wait_send()
+
+        for i in range(n_chunks):
+            for b in range(2):
+
+                @pl.when(jnp.logical_and(u >= b, u < 3))
+                def _():
+                    z_copy(i, b, 0, up).wait_send()
+
+                first_copy(i, b).wait_send()
+
+            @pl.when(u == 1)
+            def _():
+                z_copy(i, 1, 1, down).wait_send()
+
+            for copy in second_copies(i, False):
+                copy.wait_send()
+        swap.wait()
+
+    any_spec = pl.BlockSpec(memory_space=pl.ANY)
+    dma = pltpu.SemaphoreType.DMA
+    full_shapes = [jax.ShapeDtypeStruct((2, 8 * s.shape[0], s.shape[1]), s.dtype) for s in shards]
+    length = tokens.shape[1] * 4
+    rows_shape = jax.ShapeDtypeStruct((8, half, width), tokens.dtype)
+    outs = pl.pallas_call(
+        kernel,
+        out_shape=[rows_shape, rows_shape, *full_shapes, full_shapes[-1]],
+        in_specs=[any_spec] * (2 + count),
+        out_specs=[any_spec] * (3 + count),
+        scratch_shapes=[
+            *[pltpu.VMEM(s.shape, s.dtype) for s in shards],
+            pltpu.VMEM((half, width), tokens.dtype),
+            dma((count,)),
+            dma,
+            dma((2, 4)),
+            dma((2, 4)),
+            dma((2, 4)),
+            dma((2, 4)),
+            dma((count,)),
+            dma((count,)),
+            dma((n_chunks, 2, 2)),
+            dma((n_chunks, 2)),
+            dma((n_chunks, 2)),
+            dma((n_chunks, 2)),
+            dma((n_chunks, 3)),
+            dma((n_chunks, 3)),
+            dma,
+            dma,
+        ],
+        compiler_params=pltpu.CompilerParams(collective_id=1, has_side_effects=True),
+    )(tokens, cotangent, *shards)
+    return (
+        outs[0].reshape(length, width),
+        outs[1].reshape(length, width),
+        outs[2 : 2 + count],
+        outs[2 + count],
+    )
+
+
+def reduce_all(output, token_grad, grads, chunks):
+    count = len(grads)
+    n_chunks = len(chunks)
+    length, width = output.shape
+    half = length // 8
+    rows_of = [g.shape[1] // 8 for g in grads]
+
+    def kernel(*refs):
+        res, tgr = refs[0], refs[1]
+        part = refs[2 : 2 + count]
+        base = 2 + count
+        res_out, tgr_out = refs[base], refs[base + 1]
+        final = refs[base + 2 : base + 2 + count]
+        base += 2 + count
+        got1 = refs[base : base + count]
+        sum1 = refs[base + count : base + 2 * count]
+        got2 = refs[base + 2 * count : base + 3 * count]
+        sum2 = refs[base + 3 * count : base + 4 * count]
+        got3 = refs[base + 4 * count : base + 5 * count]
+        sum3 = refs[base + 5 * count : base + 6 * count]
+        got4 = refs[base + 6 * count : base + 7 * count]
+        got5 = refs[base + 7 * count : base + 8 * count]
+        (
+            row_stage,
+            row_sem,
+            ex_send,
+            ex_recv,
+            a_send,
+            a_recv,
+            b_send,
+            b_recv,
+            z_send,
+            z_recv,
+            y_send,
+            y_recv,
+            p_send,
+            p_recv,
+        ) = refs[base + 8 * count :]
+        d, t, k, c, xb, yb, dx, dy = place()
+        mate = d + 1 - 2 * c
+        u = t + c * (3 - 2 * t)
+        up = t + 1 - 2 * c
+        down = t - 1 + 2 * c
+        source = u <= 1
+        enter(k, c, t, d, dx, dy)
+
+        def return_rows(which, src, dst, start):
+            for goal in range(4):
+                piece = src.at[pl.ds((goal * 2 + c) * half, half)]
+                spot = dst.at[t % 2, pl.ds(c * half, half)]
+                here = jnp.logical_and(goal == t, c == t // 2)
+                copy = remote(
+                    piece,
+                    spot,
+                    ex_send.at[which, goal],
+                    ex_recv.at[which, t % 2, c],
+                    2 * k + t // 2,
+                    goal,
+                )
+
+                @pl.when(here)
+                def _():
+                    if start:
+                        load = pltpu.make_async_copy(piece, row_stage, row_sem)
+                        load.start()
+                        load.wait()
+                        store = pltpu.make_async_copy(row_stage, spot, row_sem)
+                        store.start()
+                        store.wait()
+
+                @pl.when(jnp.logical_not(here))
+                def _():
+                    if start:
+                        copy.start()
+                    else:
+                        copy.wait_send()
+
+            if not start:
+                for m in range(2):
+                    for core in range(2):
+                        spot = dst.at[m, pl.ds(core * half, half)]
+                        here = jnp.logical_and(2 * c + m == t, core == c)
+
+                        @pl.when(jnp.logical_not(here))
+                        def _():
+                            remote(
+                                spot,
+                                spot,
+                                ex_send.at[which, 0],
+                                ex_recv.at[which, m, core],
+                                mate,
+                                t,
+                            ).wait_recv()
+
+        def plane(b):
+            return b + c * (1 - 2 * b)
+
+        def first_copies(i):
+            s, col, cols = chunks[i]
+            rows = rows_of[s]
+            spot = pl.ds(col, cols)
+            out = [
+                remote(
+                    part[s].at[plane(0), pl.ds((1 - yb) * 4 * rows, 4 * rows), spot],
+                    got1[s].at[0, :, spot],
+                    a_send.at[i, 0],
+                    a_recv.at[i, 0],
+                    dy,
+                    t,
+                )
+            ]
+            for r in range(2):
+                out.append(
+                    remote(
+                        part[s].at[plane(1), pl.ds((2 * r + 1 - xb) * 2 * rows, 2 * rows), spot],
+                        got1[s].at[1, pl.ds(r * 2 * rows, 2 * rows), spot],
+                        a_send.at[i, 1 + r],
+                        a_recv.at[i, 1 + r],
+                        dx,
+                        t,
+                    )
+                )
+            return out
+
+        def second_copies(i):
+            s, col, cols = chunks[i]
+            rows = rows_of[s]
+            spot = pl.ds(col, cols)
+            out = []
+            for b, far, goal in ((0, 1 - xb, dx), (1, 1 - yb, dy)):
+                out.append(
+                    remote(
+                        sum1[s].at[b, pl.ds(far * 2 * rows, 2 * rows), spot],
+                        got2[s].at[b, :, spot],
+                        b_send.at[i, b],
+                        b_recv.at[i, b],
+                        goal,
+                        t,
+                    )
+                )
+            return out
+
+        def low(v, s):
+            return v.astype(sum1[s].dtype)
+
+        def level_first(i):
+            for copy in first_copies(i):
+                copy.start()
+
+        def level_second(i):
+            s, col, cols = chunks[i]
+            rows = rows_of[s]
+            spot = pl.ds(col, cols)
+            for copy in first_copies(i):
+                copy.wait_recv()
+            mine = part[s][plane(0), pl.ds(yb * 4 * rows, 4 * rows), spot]
+            sum1[s][0, :, spot] = low(mine.astype(F32) + got1[s][0, :, spot].astype(F32), s)
+            for r in range(2):
+                mine = part[s][plane(1), pl.ds((2 * r + xb) * 2 * rows, 2 * rows), spot]
+                there = pl.ds(r * 2 * rows, 2 * rows)
+                sum1[s][1, there, spot] = low(
+                    mine.astype(F32) + got1[s][1, there, spot].astype(F32), s
+                )
+            for copy in second_copies(i):
+                copy.start()
+
+        def z_copy(i, b):
+            s, col, cols = chunks[i]
+            spot = pl.ds(col, cols)
+            return remote(
+                sum3[s].at[b, :, spot],
+                got3[s].at[b, :, spot],
+                z_send.at[i, b],
+                z_recv.at[i, b],
+                d,
+                down,
+            )
+
+        def y_copy(i):
+            s, col, cols = chunks[i]
+            spot = pl.ds(col, cols)
+            return remote(
+                sum3[s].at[1, :, spot], got4[s].at[:, spot], y_send.at[i], y_recv.at[i], d, up
+            )
+
+        def level_line(i):
+            s, col, cols = chunks[i]
+            rows = rows_of[s]
+            spot = pl.ds(col, cols)
+            for copy in second_copies(i):
+                copy.wait_recv()
+            for b, near in ((0, xb), (1, yb)):
+                mine = sum1[s][b, pl.ds(near * 2 * rows, 2 * rows), spot]
+                sum2[s][b, :, spot] = mine.astype(F32) + got2[s][b, :, spot].astype(F32)
+
+            @pl.when(u == 3)
+            def _():
+                for b in range(2):
+                    sum3[s][b, :, spot] = low(sum2[s][b, :, spot], s)
+                    z_copy(i, b).start()
+
+            @pl.when(u == 0)
+            def _():
+                sum3[s][1, :, spot] = low(sum2[s][1, :, spot], s)
+                y_copy(i).start()
+
+        def level_pass(i):
+            s, col, cols = chunks[i]
+            spot = pl.ds(col, cols)
+
+            @pl.when(u == 2)
+            def _():
+                for b in range(2):
+                    z_copy(i, b).wait_recv()
+                    sum3[s][b, :, spot] = low(
+                        sum2[s][b, :, spot] + got3[s][b, :, spot].astype(F32), s
+                    )
+                    z_copy(i, b).start()
+
+        def level_near(i):
+            s, col, cols = chunks[i]
+            spot = pl.ds(col, cols)
+
+            @pl.when(u == 1)
+            def _():
+                z_copy(i, 0).wait_recv()
+                sum3[s][0, :, spot] = low(
+                    sum2[s][0, :, spot] + got3[s][0, :, spot].astype(F32), s
+                )
+                z_copy(i, 0).start()
+                z_copy(i, 1).wait_recv()
+                y_copy(i).wait_recv()
+                total = (
+                    sum2[s][1, :, spot]
+                    + got3[s][1, :, spot].astype(F32)
+                    + got4[s][:, spot].astype(F32)
+                )
+                finish(i, total)
+
+            @pl.when(u == 0)
+            def _():
+                z_copy(i, 0).wait_recv()
+                finish(i, sum2[s][0, :, spot] + got3[s][0, :, spot].astype(F32))
+
+        def p_copy(i):
+            s, col, cols = chunks[i]
+            rows = rows_of[s]
+            spot = pl.ds(col, cols)
+            return remote(
+                sum1[s].at[0, pl.ds((1 - c) * rows, rows), spot],
+                got5[s].at[:, spot],
+                p_send.at[i],
+                p_recv.at[i],
+                mate,
+                t,
+            )
+
+        def finish(i, total):
+            s, col, cols = chunks[i]
+            rows = rows_of[s]
+            spot = pl.ds(col, cols)
+            for copy in second_copies(i):
+                copy.wait_send()
+            sum2[s][0, :, spot] = total
+            sum1[s][0, pl.ds(0, 2 * rows), spot] = low(total, s)
+            p_copy(i).start()
+            final[s][:, spot] = sum2[s][0, pl.ds(c * rows, rows), spot]
+
+        def level_mate(i):
+            s, col, cols = chunks[i]
+            spot = pl.ds(col, cols)
+
+            @pl.when(u >= 2)
+            def _():
+                p_copy(i).wait_recv()
+                final[s][:, spot] = got5[s][:, spot].astype(F32)
+
+        return_rows(0, res, res_out, True)
+        return_rows(1, tgr, tgr_out, True)
+        skewed(
+            n_chunks, [level_first, level_second, level_line, level_pass, level_near, level_mate]
+        )
+        return_rows(0, res, res_out, False)
+        return_rows(1, tgr, tgr_out, False)
+        for i in range(n_chunks):
+            for copy in first_copies(i):
+                copy.wait_send()
+
+            @pl.when(u >= 2)
+            def _():
+                for copy in second_copies(i):
+                    copy.wait_send()
+                for b in range(2):
+                    z_copy(i, b).wait_send()
+
+            @pl.when(u == 1)
+            def _():
+                z_copy(i, 0).wait_send()
+
+            @pl.when(u == 0)
+            def _():
+                y_copy(i).wait_send()
+
+            @pl.when(u <= 1)
+            def _():
+                p_copy(i).wait_send()
+
+    any_spec = pl.BlockSpec(memory_space=pl.ANY)
+    vmem = pl.BlockSpec(memory_space=pltpu.VMEM)
+    dma = pltpu.SemaphoreType.DMA
+    scratch = []
+    for kind in range(8):
+        for s in range(count):
+            rows, cols, kept = rows_of[s], grads[s].shape[2], grads[s].dtype
+            shape, dtype = (
+                ((2, 4 * rows, cols), kept),
+                ((2, 4 * rows, cols), kept),
+                ((2, 2 * rows, cols), kept),
+                ((2, 2 * rows, cols), F32),
+                ((2, 2 * rows, cols), kept),
+                ((2, 2 * rows, cols), kept),
+                ((2 * rows, cols), kept),
+                ((rows, cols), kept),
+            )[kind]
+            scratch.append(pltpu.VMEM(shape, dtype))
+    back = jax.ShapeDtypeStruct((2, 2 * half, width), output.dtype)
+    outs = pl.pallas_call(
+        kernel,
+        out_shape=[
+            back,
+            back,
+            *[jax.ShapeDtypeStruct((r, g.shape[2]), F32) for r, g in zip(rows_of, grads)],
+        ],
+        in_specs=[any_spec, any_spec] + [vmem] * count,
+        out_specs=[any_spec, any_spec] + [vmem] * count,
+        scratch_shapes=[
+            *scratch,
+            pltpu.VMEM((half, width), output.dtype),
+            dma,
+            dma((2, 4)),
+            dma((2, 2, 2)),
+            dma((n_chunks, 3)),
+            dma((n_chunks, 3)),
+            dma((n_chunks, 2)),
+            dma((n_chunks, 2)),
+            dma((n_chunks, 2)),
+            dma((n_chunks, 2)),
+            dma((n_chunks,)),
+            dma((n_chunks,)),
+            dma((n_chunks,)),
+            dma((n_chunks,)),
+        ],
+        compiler_params=pltpu.CompilerParams(
+            collective_id=2, has_side_effects=True, vmem_limit_bytes=60 * 1024 * 1024
+        ),
+    )(output, token_grad, *grads)
+    return outs[0], outs[1], outs[2:]
+
+
+BLOCK = 256
+
+
+def lane_half(shape, h):
+    lane = lax.broadcasted_iota(jnp.int32, shape, 1)
+    return lane < DH if h == 0 else lane >= DH
+
+
+def reach(row_block, blocks):
+    return max(row_block + 1, blocks // 2)
+
+
+def dot_nt(a, b):
+    return lax.dot_general(a, b, (((1,), (1,)), ((), ())), preferred_element_type=F32)
+
+
+def dot_tn(a, b):
+    return lax.dot_general(a, b, (((0,), (0,)), ((), ())), preferred_element_type=F32)
+
+
+def attend(queries, keys, values, prefix):
+    length, width = queries.shape
+    blocks = length // BLOCK
+    pairs = width // 128
+
+    def kernel(prefix_ref, q_ref, k_ref, v_ref, o_ref, lt_ref):
+        limit = prefix_ref[0]
+        for qb in range(blocks):
+            rows = pl.ds(qb * BLOCK, BLOCK)
+            span = reach(qb, blocks) * BLOCK
+            q = q_ref[rows, :] * jnp.asarray(DH**-0.5, BF)
+            heads = []
+            for h in range(2):
+                half = lane_half((BLOCK, 128), h)
+                s = dot_nt(jnp.where(half, q, jnp.zeros_like(q)), k_ref[pl.ds(0, span), :])
+                clear = qb * BLOCK
+                row = lax.broadcasted_iota(jnp.int32, (BLOCK, span - clear), 0) + clear
+                col = lax.broadcasted_iota(jnp.int32, (BLOCK, span - clear), 1) + clear
+                seen = col <= row
+                if clear < length // 2:
+                    seen = jnp.logical_or(seen, col < limit)
+                tail = jnp.where(seen, s[:, clear:], MASKED_SCORE)
+                s = jnp.concatenate([s[:, :clear], tail], axis=1) if clear else tail
+                top = jnp.max(s, axis=1, keepdims=True)
+                p = jnp.exp(s - top)
+                total = jnp.sum(p, axis=1, keepdims=True)
+                log_total = top + jnp.log(total)
+                lt_ref[h, 0:1, rows] = jnp.transpose(
+                    jnp.broadcast_to(log_total, (BLOCK, 128))
+                )[0:1, :]
+                p = (p * (1.0 / total)).astype(BF)
+                heads.append(
+                    jnp.dot(p, v_ref[pl.ds(0, span), :], preferred_element_type=F32)
+                )
+            o_ref[rows, :] = jnp.where(lane_half((BLOCK, 128), 0), heads[0], heads[1]).astype(BF)
+
+    pair = pl.BlockSpec((length, 128), lambda i: (0, i))
+    return pl.pallas_call(
+        kernel,
+        grid=(pairs,),
+        out_shape=[
+            jax.ShapeDtypeStruct((length, width), BF),
+            jax.ShapeDtypeStruct((2 * pairs, 8, length), F32),
+        ],
+        in_specs=[pl.BlockSpec(memory_space=pltpu.SMEM), pair, pair, pair],
+        out_specs=[pair, pl.BlockSpec((2, 8, length), lambda i: (i, 0, 0))],
+    )(prefix, queries, keys, values)
+
+
+def attend_back(queries, keys, values, prefix, totals, context, context_grad):
+    length, width = queries.shape
+    blocks = length // BLOCK
+    pairs = width // 128
+
+    def kernel(prefix_ref, q_ref, k_ref, v_ref, lt_ref, o_ref, do_ref, dq_ref, dk_ref, dv_ref, acc):
+        limit = prefix_ref[0]
+        scaling = jnp.asarray(DH**-0.5, BF)
+        head_row = lax.broadcasted_iota(jnp.int32, (8, 128), 0)
+        lane = lax.broadcasted_iota(jnp.int32, (8, 128), 1)
+        pick = (lane // DH == head_row).astype(F32)
+        row_dots = []
+        for qb in range(blocks):
+            rows = pl.ds(qb * BLOCK, BLOCK)
+            both = do_ref[rows, :].astype(F32) * o_ref[rows, :].astype(F32)
+            row_dots.append(
+                lax.dot_general(
+                    pick,
+                    both,
+                    (((1,), (1,)), ((), ())),
+                    precision=lax.Precision.HIGHEST,
+                    preferred_element_type=F32,
+                )
+            )
+        acc[...] = jnp.zeros_like(acc)
+        for kb in range(blocks):
+            keys_at = pl.ds(kb * BLOCK, BLOCK)
+            key = k_ref[keys_at, :]
+            value = v_ref[keys_at, :]
+            dk = jnp.zeros((BLOCK, 128), F32)
+            dv = jnp.zeros((BLOCK, 128), F32)
+            for qb in range(blocks):
+                if kb >= reach(qb, blocks):
+                    continue
+                rows = pl.ds(qb * BLOCK, BLOCK)
+                q_pair = q_ref[rows, :] * scaling
+                do_pair = do_ref[rows, :]
+                for h in range(2):
+                    half = lane_half((BLOCK, 128), h)
+                    zero = jnp.zeros((BLOCK, 128), BF)
+                    q = jnp.where(half, q_pair, zero)
+                    do = jnp.where(half, do_pair, zero)
+                    s = dot_nt(key, q)
+                    if kb >= qb:
+                        key_id = lax.broadcasted_iota(jnp.int32, (BLOCK, BLOCK), 0) + kb * BLOCK
+                        row_id = lax.broadcasted_iota(jnp.int32, (BLOCK, BLOCK), 1) + qb * BLOCK
+                        seen = key_id <= row_id
+                        if kb * BLOCK < length // 2:
+                            seen = jnp.logical_or(seen, key_id < limit)
+                        s = jnp.where(seen, s, MASKED_SCORE)
+                    p = jnp.exp(s - lt_ref[h, 0:1, rows])
+                    dp = dot_nt(value, do)
+                    ds = (p * (dp - row_dots[qb][h : h + 1, :])).astype(BF)
+                    dv = dv + jnp.dot(p.astype(BF), do, preferred_element_type=F32)
+                    dk = dk + jnp.dot(ds, q, preferred_element_type=F32)
+                    acc[rows, :] += dot_tn(ds, jnp.where(half, key, zero))
+            dk_ref[keys_at, :] = dk.astype(BF)
+            dv_ref[keys_at, :] = dv.astype(BF)
+        dq_ref[...] = (acc[...] * DH**-0.5).astype(BF)
+
+    pair = pl.BlockSpec((length, 128), lambda i: (0, i))
+    shape = jax.ShapeDtypeStruct((length, width), BF)
+    return pl.pallas_call(
+        kernel,
+        grid=(pairs,),
+        out_shape=[shape] * 3,
+        in_specs=[
+            pl.BlockSpec(memory_space=pltpu.SMEM),
+            pair,
+            pair,
+            pair,
+            pl.BlockSpec((2, 8, length), lambda i: (i, 0, 0)),
+            pair,
+            pair,
+        ],
+        out_specs=[pair] * 3,
+        scratch_shapes=[pltpu.VMEM((length, 128), F32)],
+    )(prefix, queries, keys, values, totals, context, context_grad)
+
+
+def chip_local(
+    tokens, prefix_len, w_qkv, bias_qv, w_out, w_up, bias_up, w_down, gains, shifts, cotangent
+):
+    d, t, k, c, _, _, _, _ = place()
+    model_width = tokens.shape[2]
+    length = tokens.shape[1] * 4
+    part = w_qkv.shape[2]
+    hidden = w_up.shape[1]
+
+    def lanes(v):
+        return jnp.pad(v, ((0, 0), (0, 128 - v.shape[1])))
+
+    limits = jnp.concatenate([prefix_len // 16, prefix_len % 16]).astype(BF)[None]
+    small = jnp.concatenate(
+        [lanes(v) for v in (bias_qv, bias_up[None], gains, shifts, limits)], axis=0
+    )
+    small = jnp.pad(small, ((0, SMALL - small.shape[0]), (0, 0)))
+    shards = (
+        w_qkv.reshape(ROWS, 3 * part),
+        w_out.T,
+        w_up,
+        w_down.T,
+        small,
+    )
+    half = hidden // 2
+    chunks = (
+        (4, 0, 128),
+        (0, 0, 3 * part),
+        (1, 0, part),
+        (2, 0, half),
+        (2, half, half),
+        (3, 0, half),
+        (3, half, half),
+    )
+    x, cot, (g_qkv, g_out, g_up, g_down, g_small), small_other = gather_all(
+        tokens, cotangent, shards, chunks
+    )
+
+    mine = g_small.reshape(2, 8, SMALL, 128)
+    theirs = small_other.reshape(2, 8, SMALL, 128)
+    first = jnp.where(c == 0, mine, theirs)
+    every = jnp.concatenate([first, jnp.where(c == 0, theirs, mine)], axis=0)
+    per = bias_qv.shape[1]
+    bias_values = mine[:, :, 0:2, :per].astype(F32)
+    bias_values = bias_values.transpose(2, 0, 1, 3).reshape(2, 2 * part)
+    up_bias = mine[:, :, 2, : bias_up.shape[0]].astype(F32).reshape(2, hidden)
+    rows = every[:, :, 3:9, :per].astype(F32).transpose(2, 1, 0, 3).reshape(6, model_width)
+    full_gains, full_shifts = rows[:2], rows[2:]
+    source = lax.dynamic_index_in_dim(every[0, :, 9, :4].astype(F32), 2 * k + t // 2, 0, False)
+    member = t % 2
+    high = jnp.where(member == 0, source[0], source[1])
+    low_part = jnp.where(member == 0, source[2], source[3])
+    prefix = (high * 16 + low_part).astype(jnp.int32)[None]
+
+    def kind(i):
+        return jnp.concatenate(
+            [g_qkv[z, :, i * part : (i + 1) * part] for z in range(2)], axis=1
+        )
+
+    def project(i):
+        return jnp.dot(x, kind(i), preferred_element_type=F32)
+
+    queries = (project(0) + bias_values[0]).astype(BF)
+    key_heads = project(1).astype(BF)
+    value_heads = (project(2) + bias_values[1]).astype(BF)
+    context, totals = attend(queries, key_heads, value_heads, prefix)
+    branch_part = sum(
+        jnp.einsum(
+            "rk,dk->rd", context[:, z * part : (z + 1) * part], g_out[z], preferred_element_type=F32
+        )
+        for z in range(2)
+    ).astype(BF)
+    branch = (
+        branch_part.astype(F32) + pair_swap(branch_part).astype(F32) + full_shifts[0]
+    )
+    normed, normal_one, inverse_one = norm_forward(
+        x.astype(F32) + branch, full_gains[0], full_shifts[1]
+    )
+    normed_low = normed.astype(BF)
+    pre = [
+        jnp.dot(normed_low, g_up[z], preferred_element_type=F32) + up_bias[z] for z in range(2)
+    ]
+    active = [jax.nn.gelu(v, approximate=False).astype(BF) for v in pre]
+    feed_part = sum(
+        jnp.einsum("rf,df->rd", active[z], g_down[z], preferred_element_type=F32)
+        for z in range(2)
+    ).astype(BF)
+    feed_out = feed_part.astype(F32) + pair_swap(feed_part).astype(F32) + full_shifts[2]
+    result, normal_two, inverse_two = norm_forward(
+        normed + feed_out, full_gains[1], full_shifts[3]
+    )
+    incoming = cot.astype(F32)
+    residual_two, gain_two, shift_two = norm_backward(
+        incoming, normal_two, inverse_two, full_gains[1]
+    )
+    feed_grad = residual_two.astype(BF)
+    upper = []
+    for z in range(2):
+        active_grad = jnp.dot(feed_grad, g_down[z], preferred_element_type=F32)
+        _, pull = jax.vjp(partial(jax.nn.gelu, approximate=False), pre[z])
+        upper.append(pull(active_grad)[0].astype(BF))
+    normed_part = sum(
+        jnp.einsum("rf,df->rd", upper[z], g_up[z], preferred_element_type=F32) for z in range(2)
+    ).astype(BF)
+    normed_grad = residual_two + (
+        normed_part.astype(F32) + pair_swap(normed_part).astype(F32)
+    )
+    residual_one, gain_one, shift_one = norm_backward(
+        normed_grad, normal_one, inverse_one, full_gains[0]
+    )
+    branch_grad = residual_one.astype(BF)
+    context_grad = jnp.concatenate(
+        [jnp.dot(branch_grad, g_out[z], preferred_element_type=F32) for z in range(2)], axis=1
+    ).astype(BF)
+    mixed = attend_back(queries, key_heads, value_heads, prefix, totals, context, context_grad)
+    mixed_low = [
+        jnp.concatenate([m[:, z * part : (z + 1) * part] for m in mixed], axis=1)
+        for z in range(2)
+    ]
+    token_part = sum(
+        jnp.einsum("re,de->rd", mixed_low[z], g_qkv[z], preferred_element_type=F32)
+        for z in range(2)
+    ).astype(BF)
+    token_grad = residual_one + (token_part.astype(F32) + pair_swap(token_part).astype(F32))
+
+    def outer(a, b):
+        return jnp.einsum("rm,rn->mn", a, b, preferred_element_type=F32).astype(BF)
+
+    grads = (
+        jnp.stack([outer(x, mixed_low[z]) for z in range(2)]),
+        jnp.stack(
+            [outer(branch_grad, context[:, z * part : (z + 1) * part]) for z in range(2)]
+        ),
+        jnp.stack([outer(normed_low, upper[z]) for z in range(2)]),
+        jnp.stack([outer(feed_grad, active[z]) for z in range(2)]),
+    )
+    up_bias_grad = jnp.stack([jnp.sum(v.astype(F32), axis=0) for v in upper])
+    bias_grad = jnp.stack(
+        [jnp.sum(m.astype(F32), axis=0) for m in (mixed[0], mixed[2])]
+    )
+    row_grads = jnp.stack(
+        [
+            gain_one,
+            gain_two,
+            jnp.sum(branch_grad.astype(F32), axis=0),
+            shift_one,
+            jnp.sum(feed_grad.astype(F32), axis=0),
+            shift_two,
+        ]
+    )
+    spread_bias = bias_grad.reshape(2, 2, 8, per).transpose(1, 2, 0, 3)
+    spread_rows = row_grads.reshape(6, 8, 4, per).transpose(2, 1, 0, 3)
+    spread_rows = lax.dynamic_slice_in_dim(spread_rows, 2 * c, 2, 0)
+    spread_up = up_bias_grad.reshape(2, 8, 1, bias_up.shape[0])
+
+    def wide(v):
+        return jnp.pad(v, ((0, 0), (0, 0), (0, 0), (0, 128 - v.shape[3])))
+
+    tiles = jnp.concatenate(
+        [wide(spread_bias), wide(spread_up), wide(spread_rows[:, :, :2].reshape(2, 8, 1, 2 * per)),
+         wide(spread_rows[:, :, 2:].reshape(2, 8, 1, 4 * per)),
+         jnp.zeros((2, 8, 3, 128), F32)],
+        axis=2,
+    ).reshape(2, 64, 128)
+    back_chunks = (
+        (3, 0, half),
+        (3, half, half),
+        (2, 0, half),
+        (2, half, half),
+        (1, 0, part),
+        (0, 0, 3 * part),
+        (4, 0, 128),
+    )
+    out_rows, token_rows, finals = reduce_all(
+        result.astype(BF), token_grad.astype(BF), (*grads, tiles), back_chunks
+    )
+    tile = finals[4]
+    return (
+        out_rows,
+        token_rows.astype(F32),
+        finals[0].reshape(w_qkv.shape),
+        tile[0:2, :per],
+        finals[1].T,
+        finals[2],
+        tile[2, : bias_up.shape[0]],
+        finals[3].T,
+        tile[3, : 2 * per].reshape(2, per),
+        tile[4, : 4 * per].reshape(4, per),
+    )
+
+
 def solution(mesh):
     return jax.shard_map(
-        local,
+        chip_local if dict(mesh.shape) == {"dp": 8, "tensor": 4} else local,
         mesh=mesh,
         in_specs=(
             P("dp", "tensor", None),

time: 972 us -> 414 us (0.43)
  waiting for transfers between devices: 475 us -> 0 us
  Pallas kernels: 0 us -> 263 us
  blocking collectives: 230 us -> 0 us
  matrix products: 150 us -> 67.5 us
  between operations: 19.7 us -> 4.32 us
  other arithmetic: 56.6 us -> 45 us
    reduce_scatter x10 -> x0, waiting for transfers between devices: 265 us -> none  [the longest x2 67.9 us: local(): lax.psum_scatter(jnp.dot(active_low, full_down, preferred_element_type=jn...]
    pallas_call x0 -> x8, Pallas kernels: none -> 263 us  [the longest x1 116 us: gather_all(): pl.pallas_call(kernel, out_shape=[rows_shape, rows_shape, *full_shapes, f...]
    all_gather x10 -> x0, waiting for transfers between devices: 206 us -> none  [the longest x2 67.8 us: local(): fold_piece = lax.all_gather(feed_grad, 'tensor', axis=0, tiled=True)]
    all_gather x5 -> x0, blocking collectives: 164 us -> none  [the longest x1 67.6 us: local(): lax.all_gather(gains, ('dp', 'tensor'), axis=1, tiled=True)]
    dot_general x46 -> x25, matrix products: 144 us -> 67.5 us  [the longest x2 23.8 us: chip_local(): jnp.dot(normed_low, g_up[z], preferred_element_type=F32) + up_bias[z]]
    unnamed x3 -> x0, blocking collectives: 66.1 us -> none
    convert_element_type x7 -> x4, other arithmetic: 19.6 us -> 8.46 us  [the longest x1 3.5 us: chip_local(): token_grad.astype(BF)]
  transfers between devices with their start and end apart: 22 -> 0, of which waited for: 17 -> 0; matrix products, arithmetic and copies ran while one was open for 15% -> 0% of each run, Pallas kernels for 0% -> 0%
where the time goes in v1:
time: 414 us; the launch traced here: 409 us
  Pallas kernels  263 us (64%)
  matrix products  67.5 us (16%)
  other arithmetic  45 us (11%)
  local copies, waits for them, and re-layouts  29.2 us (7%)
  between operations  4.32 us (1%)
    pallas_call x1, Pallas kernels, gather_all(): pl.pallas_call(kernel, out_shape=[rows_shape, rows_shape, *full_shapes, f...  116 us
    pallas_call x1, Pallas kernels, reduce_all(): pl.pallas_call(kernel, out_shape=[back, back, *[jax.ShapeDtypeStruct((r,...  92.7 us
    pallas_call x1, Pallas kernels, attend_back(): pl.pallas_call(kernel, grid=(pairs,), out_shape=[shape] * 3, in_specs=[pl...  24.2 us
    dot_general x2, matrix products, chip_local(): jnp.dot(normed_low, g_up[z], preferred_element_type=F32) + up_bias[z]  23.8 us
    pallas_call x4, Pallas kernels, pair_swap(): pl.pallas_call(kernel, out_shape=jax.ShapeDtypeStruct(part.shape, part.dt...  15.3 us
    pallas_call x1, Pallas kernels, attend(): pl.pallas_call(kernel, grid=(pairs,), out_shape=[jax.ShapeDtypeStruct((le...  14.9 us
    unnamed x90, local copies, waits for them, and re-layouts  13.5 us
    dot_general x8, matrix products, outer(): return jnp.einsum('rm,rn->mn', a, b, preferred_element_type=F32).astype(BF)  11.9 us

profile of v1, /device:TPU:0, one launch (start us, length us, event | category | flops | bytes accessed | tf_op | source)
XLA Modules:
  0.0 408.8 jit_solution(14896311408081372495)
XLA Ops:
  6.7 1.5 copy.74
  8.2 115.6 %shard_map.186 = (bf16[8,128,768]{2,1,0:T(8,128)(2,1)}, bf16[8,128,768]{2,1,0:T(8,128)(2,1)}, bf16[2,768,576]{2,1,0:T(8,128)(2,1)}, bf16[2,768,192]{2,1,0:T(8,12...) custom-call(bf16[2,256,768]{2,1,0:T(8,128)(2,1)} %refs_0_.1, ...), custom_call_target="tpu_custom_call" | custom-call | tf_op jit(solution)/shard_map/pallas_call | solution.py:695
  123.8 1.8 broadcast_select_fusion.1
  129.4 2.9 slice_bitcast_fusion.1
  133.8 3.0 add_convert_fusion.8.v_ref
  136.8 1.9 add_convert_fusion.9.q_ref
  138.8 2.0 convolution_convert_fusion.6.k_ref
  140.7 14.9 %shard_map.187 = (bf16[1024,384]{1,0:T(8,128)(2,1)}, f32[6,8,1024]{2,1,0:T(8,128)}) custom-call(s32[1]{0:T(128)} %bitcast.14.prefix_ref, bf16[1024,384]{1,0:T(8,128)(2,1)} %add_convert_fusion.9.q_ref, bf16[1024,384]{1,0:T(8,128)(2,1)} %convolution_convert_fusion.6.k_ref, bf16[1024,384]{1,0:T(8,128)(2,1)} %add_convert_fusion.8.v_ref), custom_call_target="tpu_custom_call" | custom-call | tf_op jit(solution)/shard_map/pallas_call | solution.py:1146
  155.7 1.7 fusion.71
  157.4 1.8 add_convert_fusion.7.src
  159.2 3.8 shard_map.188
  163.3 3.1 fusion.98
  167.1 1.7 fusion.19
  169.7 11.7 %multiply_convert_fusion = (bf16[1024,768]{1,0:T(8,128)(2,1)}, f32[1024,768]{1,0:T(8,128)}, f32[1024,768]{1,0:T(8,128)}) fusion(f32[768]{0:T(1024)S(1)} %add.206, bf16[1024,768]{1,0:T(8,128)(2,1)} %fusion.19, bf16[2,768,768]{2,1,0:T(8,128)(2,1)} %get-tuple-element.36), kind=kOutput, calls=%fused_computation.32 | convolution fusion | flops 1259864064 | bytes 10619904 | tf_op jit(solution)/shard_map/dot_general | solution.py:1318
  181.4 12.2 %multiply_convert_fusion.1 = (bf16[1024,768]{1,0:T(8,128)(2,1)S(1)}, f32[1024,768]{1,0:T(8,128)}, f32[1024,768]{1,0:T(8,128)}) fusion(f32[768]{0:T(1024)S(1)} %add.203, bf16[1024,768]{1,0:T(8,128)(2,1)} %fusion.19, bf16[2,768,768]{2,1,0:T(8,128)(2,1)} %get-tuple-element.36), kind=kOutput, calls=%fused_computation.45 | convolution fusion | flops 1259864064 | bytes 10619904 | tf_op jit(solution)/shard_map/dot_general | solution.py:1318
  194.8 1.4 fusion.38
  196.2 2.6 add_convert_fusion.6.src
  198.8 3.8 shard_map.189
  202.7 3.1 fusion.95
  205.8 1.6 copy-done
  208.2 3.7 fusion.8
  212.6 1.4 convert_reduce_fusion.1
  214.3 1.5 copy-done.38
  215.7 4.3 %convert_reduce_fusion.3 = (f32[768]{0:T(1024)S(1)}, bf16[1024,768]{1,0:T(8,128)(2,1)S(1)}) fusion(f32[1024,768]{1,0:T(8,128)S(1)} %copy-done.38, bf16[1024,768]{1,0:T(8,128)(2,1)S(1)} %get-tuple-element.103, bf16[2,768,768]{2,1,0:T(8,128)(2,1)S(1)} %copy-done.28, f32[1024,768]{1,0:T(8,128)} %get-tuple-element.146, f32[768]{0:T(1024)S(1)} %add.206), kind=kOutput, calls=%fused_computation.18 | convolution fusion | flops 1221328128 | bytes 10624000 | tf_op jit(solution)/shard_map/dot_general | solution.py:1336
  220.1 2.2 convert_reduce_fusion.4
  222.3 1.4 fusion.42
  223.8 2.7 add_convert_fusion.2.src
  226.4 3.8 shard_map.190
  230.3 6.7 %multiply_reduce_fusion = (f32[768]{0:T(1024)S(1)}, f32[1024]{0:T(1024)S(1)}, f32[1024]{0:T(1024)S(1)}, f32[768]{0:T(1024)S(1)}, f32[1024,768]{1,0:T(8,128)}, /*index=5*/bf16[1024,768]{1,0:T(8,128)(2,1)}) fusion(f32[1024,768]{1,0:T(8,128)S(1)} %get-tuple-element.115, f32[1024]{0:T(1024)S(1)} %add_rsqrt_fusion.1, f32[1024]{0:T(1024)S(1)} %broadcast_multiply_fusion.4, ...), kind=kLoop, calls=%fused_computation.17 | loop fusion | flops 18870784 | bytes 15776768 | tf_op jit(solution)/shard_map/reduce_sum | solution.py:29
  237.2 4.1 %convert_reduce_fusion.2 = (f32[768]{0:T(1024)S(1)}, bf16[1024,768]{1,0:T(8,128)(2,1)}, f32[1024,768]{1,0:T(8,128)}) fusion(f32[1024]{0:T(1024)S(1)} %get-tuple-element.151, f32[1024,768]{1,0:T(8,128)S(1)} %get-tuple-element.115, f32[1024]{0:T(1024)S(1)} %broadcast_multiply_fusion.4, f32[1024]{0:T(1024)S(1)} %get-tuple-element.152, ...), kind=kLoop, calls=%fused_computation.16 | loop fusion | flops 7863552 | bytes 11032576 | tf_op jit(solution)/shard_map/reduce_sum | solution.py:1382
  242.2 2.1 convolution_convert_fusion.10
  246.7 24.2 %shard_map.191 = (bf16[1024,384]{1,0:T(8,128)(2,1)}, bf16[1024,384]{1,0:T(8,128)(2,1)}, bf16[1024,384]{1,0:T(8,128)(2,1)}) custom-call(s32[1]{0:T(128)} %bitcast.14.prefix_ref, bf16[1024,384]{1,0:T(8,128)(2,1)} %add_convert_fusion.9.q_ref, bf16[1024,384]{1,0:T(8,128)(2,1)} %convolution_convert_fusion.6.k_ref, bf16[1024,384]{1,0:T(8,128)(2,1)} %add_convert_fusion.8.v_ref, ...), custom_call_target="tpu_custom_call" | custom-call | tf_op jit(solution)/shard_map/pallas_call | solution.py:1220
  270.9 1.3 convert_reduce_fusion.6
  272.3 1.3 convert_reduce_fusion.5
  274.5 3.0 fusion.23
  277.5 1.5 fusion.22
  279.4 1.5 fusion.21
  280.9 1.5 fusion.20
  282.3 2.8 pad_maximum_fusion
  289.2 1.6 fusion.24
  290.7 1.6 fusion.25
  292.3 1.7 pad_maximum_fusion.2.refs_2_
  294.5 1.4 fusion.55
  296.0 2.6 add_convert_fusion.1.src
  298.5 3.8 shard_map.192
  302.4 3.5 add_convert_fusion.refs_1_
  305.9 92.7 %shard_map.193 = (bf16[2,256,768]{2,1,0:T(8,128)(2,1)}, bf16[2,256,768]{2,1,0:T(8,128)(2,1)}, f32[96,576]{1,0:T(8,128)}, f32[96,192]{1,0:T(8,128)}, f32[96,768]{...) custom-call(bf16[1024,768]{1,0:T(8,128)(2,1)} %get-tuple-element.116.refs_0_, ...), custom_call_target="tpu_custom_call" | custom-call | tf_op jit(solution)/shard_map/pallas_call | solution.py:1056
  398.7 2.5 convert_element_type.215
  (166 shorter events, 30.2 us)
Async XLA Ops:
  123.8 10.0 %copy-start.12 = (bf16[8,128,768]{2,1,0:T(8,128)(2,1)S(1)}, bf16[8,128,768]{2,1,0:T(8,128)(2,1)}, u32[]{:S(2)}) copy-start(bf16[8,128,768]{2,1,0:T(8,128)(2,1)} %get-tuple-element.30) | copy-start | bytes 4718596
  125.6 0.6 copy-start.21
  138.8 16.9 %copy-start.9 = (bf16[2,768,192]{2,1,0:T(8,128)(2,1)S(1)}, bf16[2,768,192]{2,1,0:T(8,128)(2,1)}, u32[]{:S(2)}) copy-start(bf16[2,768,192]{2,1,0:T(8,128)(2,1)} %get-tuple-element.35) | copy-start | bytes 1769476
  155.7 1.7 copy-start.7
  157.4 5.7 %copy-start.22 = (bf16[2,8,16,128]{3,0,1,2:T(2,128)(2,1)S(1)}, bf16[2,8,16,128]{3,0,1,2:T(2,128)(2,1)}, u32[]{:S(2)}) copy-start(bf16[2,8,16,128]{3,0,1,2:T(2,128)(2,1)} %copy-done.21) | copy-start | bytes 196612
  157.4 5.7 %copy-start.23 = (bf16[2,8,16,128]{3,0,1,2:T(2,128)(2,1)S(1)}, bf16[2,8,16,128]{3,0,1,2:T(2,128)(2,1)}, u32[]{:S(2)}) copy-start(bf16[2,8,16,128]{3,0,1,2:T(2,128)(2,1)} %get-tuple-element.130) | copy-start | bytes 196612
  181.4 13.4 %copy-start.27 = (bf16[2,768,768]{2,1,0:T(8,128)(2,1)S(1)}, bf16[2,768,768]{2,1,0:T(8,128)(2,1)}, u32[]{:S(2)}) copy-start(bf16[2,768,768]{2,1,0:T(8,128)(2,1)} %get-tuple-element.37) | copy-start | bytes 7077892
  193.5 1.2 copy-start.32
  194.7 1.4 copy-start.29
  205.8 1.7 copy-start
  208.1 3.7 copy-start.2
  208.1 4.4 %copy-start.1 = (f32[1024,768]{1,0:T(8,128)S(1)}, f32[1024,768]{1,0:T(8,128)}, u32[]{:S(2)}) copy-start(f32[1024,768]{1,0:T(8,128)} %copy-done) | copy-start | bytes 9437188
  212.6 1.7 copy-start.28
  212.6 3.1 copy-start.38
  214.0 6.0 %copy-start.15 = (bf16[1024,768]{1,0:T(8,128)(2,1)}, bf16[1024,768]{1,0:T(8,128)(2,1)S(1)}, u32[]{:S(2)}) copy-start(bf16[1024,768]{1,0:T(8,128)(2,1)S(1)} %get-tuple-element.103) | copy-start | bytes 4718596
  215.7 4.3 %copy-start.36 = (f32[1024,768]{1,0:T(8,128)S(1)}, f32[1024,768]{1,0:T(8,128)}, u32[]{:S(2)}) copy-start(f32[1024,768]{1,0:T(8,128)} %get-tuple-element.113) | copy-start | bytes 9437188
  215.7 4.3 %copy-start.37 = (f32[1024,768]{1,0:T(8,128)S(1)}, f32[1024,768]{1,0:T(8,128)}, u32[]{:S(2)}) copy-start(f32[1024,768]{1,0:T(8,128)} %get-tuple-element.145) | copy-start | bytes 9437188
  220.0 3.7 copy-start.30
  220.1 2.2 copy-start.26
  222.3 1.5 copy-start.34
  241.3 3.2 copy-start.3
  241.3 3.2 copy-start.10
  246.7 27.8 %copy-start.16 = (bf16[1024,768]{1,0:T(8,128)(2,1)S(1)}, bf16[1024,768]{1,0:T(8,128)(2,1)}, u32[]{:S(2)}) copy-start(bf16[1024,768]{1,0:T(8,128)(2,1)} %copy-done.15) | copy-start | bytes 4718596
  274.5 3.0 copy-start.33
  277.5 1.5 copy-start.14
  277.5 1.9 copy-start.31
  279.4 1.5 copy-start.35
  282.3 2.8 copy-start.8
  285.8 1.9 copy-start.6
  286.6 1.3 copy-start.17
  286.6 1.7 copy-start.5
  287.6 1.5 copy-start.13
  292.3 2.2 copy-start.11
  298.5 3.8 copy-start.4
  398.6 4.5 %copy-start.24 = (f32[96,192]{1,0:T(8,128)S(1)}, f32[96,192]{1,0:T(8,128)}, u32[]{:S(2)}) copy-start(f32[96,192]{1,0:T(8,128)} %get-tuple-element.47) | copy-start | bytes 221188
  398.6 5.2 %copy-start.25 = (f32[8,128]{1,0:T(8,128)S(1)}, f32[8,128]{1,0:T(8,128)}, u32[]{:S(2)}) copy-start(f32[8,128]{1,0:T(8,128)} %get-tuple-element.46) | copy-start | bytes 12292
  398.6 7.6 %copy-start.18 = (bf16[2,256,768]{2,1,0:T(8,128)(2,1)S(1)}, bf16[2,256,768]{2,1,0:T(8,128)(2,1)}, u32[]{:S(2)}) copy-start(bf16[2,256,768]{2,1,0:T(8,128)(2,1)} %get-tuple-element.165) | copy-start | bytes 2359300
  398.6 8.5 %copy-start.20 = (f32[96,768]{1,0:T(8,128)S(1)}, f32[96,768]{1,0:T(8,128)}, u32[]{:S(2)}) copy-start(f32[96,768]{1,0:T(8,128)} %get-tuple-element.170) | copy-start | bytes 884740
  398.7 9.2 %copy-start.19 = (f32[96,768]{1,0:T(8,128)S(1)}, f32[96,768]{1,0:T(8,128)}, u32[]{:S(2)}) copy-start(f32[96,768]{1,0:T(8,128)} %get-tuple-element.49) | copy-start | bytes 884740

commit v2 on v1

--- a/solution.py
+++ b/solution.py
@@ -429,12 +429,16 @@
                 levels[level](slot - level)
 
 
-def gather_all(tokens, cotangent, shards, chunks):
+def gather_attend(tokens, cotangent, shards, chunks, per):
     half = tokens.shape[1] // 2
     width = tokens.shape[2]
     count = len(shards)
     n_chunks = len(chunks)
     rows_of = [s.shape[0] for s in shards]
+    length = tokens.shape[1] * 4
+    part = shards[0].shape[1] // 3
+    heads_width = 2 * part
+    blocks = length // BLOCK
 
     def kernel(*refs):
         tok, cot = refs[0], refs[1]
@@ -442,9 +446,14 @@
         base = 2 + count
         xf, cf = refs[base], refs[base + 1]
         full = refs[base + 2 : base + 2 + count]
-        small_other = refs[base + 2 + count]
+        small_other, q_out, k_out, v_out, o_out, lt_out = refs[base + 2 + count : base + 8 + count]
+        stage = refs[base + 8 + count : base + 8 + 2 * count]
         (
-            stage,
+            x_rows,
+            weight,
+            small_low,
+            small_rows,
+            load_sem,
             row_stage,
             local_sem,
             row_sem,
@@ -462,10 +471,7 @@
             b_recv,
             o_send,
             o_recv,
-        ) = (
-            refs[base + 3 + count : base + 3 + 2 * count],
-            *refs[base + 3 + 2 * count :],
-        )
+        ) = refs[base + 8 + 2 * count :]
         d, t, k, c, xb, yb, dx, dy = place()
         mate = d + 1 - 2 * c
         u = t + c * (3 - 2 * t)
@@ -529,12 +535,19 @@
                     spot, spot, fw_send.at[which, origin], fw_recv.at[which, origin], mate, t
                 ).start()
 
+        def arrived(which, dst):
+            for origin in range(4):
+                spot = dst.at[origin * 2 + 1 - c]
+                remote(
+                    spot, spot, fw_send.at[which, origin], fw_recv.at[which, origin], mate, t
+                ).wait_recv()
+
         def settle(which, src, dst):
             for origin in range(4):
                 spot = dst.at[origin * 2 + 1 - c]
                 remote(
                     spot, spot, fw_send.at[which, origin], fw_recv.at[which, origin], mate, t
-                ).wait()
+                ).wait_send()
             for m in range(2):
                 for core in range(2):
                     here = jnp.logical_and(2 * c + m == t, core == c)
@@ -550,18 +563,13 @@
                             t,
                         ).wait_send()
 
-        exchange(0, tok, xf)
-
-        for s in range(count):
-
+        def placed(s):
             @pl.when(source)
             def _():
                 rows = rows_of[s]
                 spot = full[s].at[t % 2, pl.ds(d * rows, rows)]
                 pltpu.make_async_copy(own[s], stage[s], local_sem.at[s]).wait()
                 pltpu.make_async_copy(stage[s], spot, local_sem.at[s]).start()
-
-        exchange(1, cot, cf)
 
         def block(i, b, start, n):
             s, col, cols = chunks[i]
@@ -650,16 +658,110 @@
             for copy in second_copies(i, True):
                 copy.wait_recv()
 
-        level_own(0)
-        relay(0, xf)
-        skewed(
-            n_chunks,
-            [(lambda i: None if i == 0 else level_own(i)), level_line, level_second, level_done],
-        )
-        relay(1, cf)
+        def expand(plane, kind):
+            rows = small_rows[plane, pl.ds(kind, 8, stride=SMALL), :]
+            spots = lax.broadcasted_iota(jnp.int32, (128, part), 0)
+            lane = lax.broadcasted_iota(jnp.int32, (128, part), 1)
+            wide = jnp.dot(
+                rows,
+                (spots == lane % per).astype(F32),
+                precision=lax.Precision.HIGHEST,
+                preferred_element_type=F32,
+            )
+            row = lax.broadcasted_iota(jnp.int32, (8, part), 0)
+            lane = lax.broadcasted_iota(jnp.int32, (8, part), 1)
+            return jnp.sum(jnp.where(lane // per == row, wide, 0.0), axis=0, keepdims=True)
+
+        def prefix_of():
+            tile = small_rows[0, pl.ds((2 * k + t // 2) * SMALL + 9, 1), 0:128]
+            lane = lax.broadcasted_iota(jnp.int32, (1, 128), 1)
+            member = t % 2
+            value = 16.0 * jnp.sum(jnp.where(lane == member, tile, 0.0), axis=1, keepdims=True)
+            value += jnp.sum(jnp.where(lane == 2 + member, tile, 0.0), axis=1, keepdims=True)
+            return value
+
+        def project():
+            bias_q = jnp.concatenate([expand(0, 0), expand(1, 0)], axis=1)
+            bias_v = jnp.concatenate([expand(0, 1), expand(1, 1)], axis=1)
+
+            @pl.loop(0, blocks)
+            def _(block_id):
+                rows = pl.ds(block_id * BLOCK, BLOCK)
+                both = [
+                    jnp.dot(x_rows[rows, :], weight[z], preferred_element_type=F32)
+                    for z in range(2)
+                ]
+
+                def kind(i):
+                    return jnp.concatenate([v[:, i * part : (i + 1) * part] for v in both], axis=1)
+
+                q_out[rows, :] = (kind(0) + bias_q).astype(BF)
+                k_out[rows, :] = kind(1).astype(BF)
+                v_out[rows, :] = (kind(2) + bias_v).astype(BF)
+
+        load_rows = [
+            pltpu.make_async_copy(xf.at[i], x_rows.at[pl.ds(i * half, half)], load_sem.at[i])
+            for i in range(8)
+        ]
+        load_weight = pltpu.make_async_copy(full[0], weight, load_sem.at[8])
         last = count - 1
         swap = remote(full[last], small_other, o_send, o_recv, mate, t)
+
+        placed(last)
+        placed(0)
+        level_own(0)
+        level_own(1)
+        exchange(0, tok, xf)
+        for s in range(1, last):
+            placed(s)
+        level_line(0)
+        level_line(1)
+        level_second(0)
+        level_own(2)
+        level_own(3)
+        level_second(1)
+        relay(0, xf)
+        level_line(2)
+        level_own(4)
+        level_done(0)
         swap.start()
+        small_load = pltpu.make_async_copy(full[last], small_low, load_sem.at[9])
+        small_load.start()
+        arrived(0, xf)
+        for copy in load_rows:
+            copy.start()
+        level_line(3)
+        level_second(2)
+        for i in range(5, n_chunks):
+            level_own(i)
+        small_load.wait()
+        small_rows[...] = small_low[...].astype(F32)
+        level_done(1)
+        load_weight.start()
+        level_second(3)
+        exchange(1, cot, cf)
+        for copy in load_rows:
+            copy.wait()
+        load_weight.wait()
+        project()
+        todo = []
+        for i in range(4, n_chunks):
+            todo.append(partial(level_line, i))
+            todo.append(partial(level_second, i))
+        todo.append(lambda: relay(1, cf))
+        work = [
+            partial(attend_rows, q_out, k_out, v_out, o_out, lt_out, prefix_of(), pair, qb)
+            for pair in range(heads_width // 128)
+            for qb in range(blocks)
+        ]
+        for step in range(max(len(todo), len(work))):
+            if step < len(todo):
+                todo[step]()
+            if step < len(work):
+                work[step]()
+        for i in range(2, n_chunks):
+            level_done(i)
+        arrived(1, cf)
         settle(0, tok, xf)
         settle(1, cot, cf)
         for s in range(count):
@@ -688,17 +790,31 @@
         swap.wait()
 
     any_spec = pl.BlockSpec(memory_space=pl.ANY)
+    vmem = pl.BlockSpec(memory_space=pltpu.VMEM)
     dma = pltpu.SemaphoreType.DMA
     full_shapes = [jax.ShapeDtypeStruct((2, 8 * s.shape[0], s.shape[1]), s.dtype) for s in shards]
-    length = tokens.shape[1] * 4
     rows_shape = jax.ShapeDtypeStruct((8, half, width), tokens.dtype)
+    head_shape = jax.ShapeDtypeStruct((length, heads_width), BF)
+    lt_shape = jax.ShapeDtypeStruct((heads_width // DH, 8, length), F32)
     outs = pl.pallas_call(
         kernel,
-        out_shape=[rows_shape, rows_shape, *full_shapes, full_shapes[-1]],
+        out_shape=[
+            rows_shape,
+            rows_shape,
+            *full_shapes,
+            full_shapes[-1],
+            *[head_shape] * 4,
+            lt_shape,
+        ],
         in_specs=[any_spec] * (2 + count),
-        out_specs=[any_spec] * (3 + count),
+        out_specs=[any_spec] * (3 + count) + [vmem] * 5,
         scratch_shapes=[
             *[pltpu.VMEM(s.shape, s.dtype) for s in shards],
+            pltpu.VMEM((length, width), BF),
+            pltpu.VMEM((2, 8 * shards[0].shape[0], shards[0].shape[1]), BF),
+            pltpu.VMEM((2, 8 * SMALL, 128), BF),
+            pltpu.VMEM((2, 8 * SMALL, 128), F32),
+            dma((10,)),
             pltpu.VMEM((half, width), tokens.dtype),
             dma((count,)),
             dma,
@@ -717,13 +833,16 @@
             dma,
             dma,
         ],
-        compiler_params=pltpu.CompilerParams(collective_id=1, has_side_effects=True),
+        compiler_params=pltpu.CompilerParams(
+            collective_id=1, has_side_effects=True, vmem_limit_bytes=60 * 1024 * 1024
+        ),
     )(tokens, cotangent, *shards)
     return (
         outs[0].reshape(length, width),
         outs[1].reshape(length, width),
         outs[2 : 2 + count],
         outs[2 + count],
+        outs[3 + count :],
     )
 
 
@@ -1106,53 +1225,35 @@
     return lax.dot_general(a, b, (((0,), (0,)), ((), ())), preferred_element_type=F32)
 
 
-def attend(queries, keys, values, prefix):
-    length, width = queries.shape
+def attend_rows(q_ref, k_ref, v_ref, o_ref, lt_ref, limit, pair, qb):
+    length = q_ref.shape[0]
     blocks = length // BLOCK
-    pairs = width // 128
-
-    def kernel(prefix_ref, q_ref, k_ref, v_ref, o_ref, lt_ref):
-        limit = prefix_ref[0]
-        for qb in range(blocks):
-            rows = pl.ds(qb * BLOCK, BLOCK)
-            span = reach(qb, blocks) * BLOCK
-            q = q_ref[rows, :] * jnp.asarray(DH**-0.5, BF)
-            heads = []
-            for h in range(2):
-                half = lane_half((BLOCK, 128), h)
-                s = dot_nt(jnp.where(half, q, jnp.zeros_like(q)), k_ref[pl.ds(0, span), :])
-                clear = qb * BLOCK
-                row = lax.broadcasted_iota(jnp.int32, (BLOCK, span - clear), 0) + clear
-                col = lax.broadcasted_iota(jnp.int32, (BLOCK, span - clear), 1) + clear
-                seen = col <= row
-                if clear < length // 2:
-                    seen = jnp.logical_or(seen, col < limit)
-                tail = jnp.where(seen, s[:, clear:], MASKED_SCORE)
-                s = jnp.concatenate([s[:, :clear], tail], axis=1) if clear else tail
-                top = jnp.max(s, axis=1, keepdims=True)
-                p = jnp.exp(s - top)
-                total = jnp.sum(p, axis=1, keepdims=True)
-                log_total = top + jnp.log(total)
-                lt_ref[h, 0:1, rows] = jnp.transpose(
-                    jnp.broadcast_to(log_total, (BLOCK, 128))
-                )[0:1, :]
-                p = (p * (1.0 / total)).astype(BF)
-                heads.append(
-                    jnp.dot(p, v_ref[pl.ds(0, span), :], preferred_element_type=F32)
-                )
-            o_ref[rows, :] = jnp.where(lane_half((BLOCK, 128), 0), heads[0], heads[1]).astype(BF)
-
-    pair = pl.BlockSpec((length, 128), lambda i: (0, i))
-    return pl.pallas_call(
-        kernel,
-        grid=(pairs,),
-        out_shape=[
-            jax.ShapeDtypeStruct((length, width), BF),
-            jax.ShapeDtypeStruct((2 * pairs, 8, length), F32),
-        ],
-        in_specs=[pl.BlockSpec(memory_space=pltpu.SMEM), pair, pair, pair],
-        out_specs=[pair, pl.BlockSpec((2, 8, length), lambda i: (i, 0, 0))],
-    )(prefix, queries, keys, values)
+    lanes = pl.ds(pair * 128, 128)
+    rows = pl.ds(qb * BLOCK, BLOCK)
+    span = reach(qb, blocks) * BLOCK
+    q = q_ref[rows, lanes] * jnp.asarray(DH**-0.5, BF)
+    heads = []
+    for h in range(2):
+        half = lane_half((BLOCK, 128), h)
+        s = dot_nt(jnp.where(half, q, jnp.zeros_like(q)), k_ref[pl.ds(0, span), lanes])
+        clear = qb * BLOCK
+        row = lax.broadcasted_iota(jnp.int32, (BLOCK, span - clear), 0) + clear
+        col = lax.broadcasted_iota(jnp.int32, (BLOCK, span - clear), 1) + clear
+        seen = col <= row
+        if clear < length // 2:
+            seen = jnp.logical_or(seen, col.astype(F32) < limit)
+        tail = jnp.where(seen, s[:, clear:], MASKED_SCORE)
+        s = jnp.concatenate([s[:, :clear], tail], axis=1) if clear else tail
+        top = jnp.max(s, axis=1, keepdims=True)
+        p = jnp.exp(s - top)
+        total = jnp.sum(p, axis=1, keepdims=True)
+        log_total = top + jnp.log(total)
+        lt_ref[2 * pair + h, 0:1, rows] = jnp.transpose(
+            jnp.broadcast_to(log_total, (BLOCK, 128))
+        )[0:1, :]
+        p = (p * (1.0 / total)).astype(BF)
+        heads.append(jnp.dot(p, v_ref[pl.ds(0, span), lanes], preferred_element_type=F32))
+    o_ref[rows, lanes] = jnp.where(lane_half((BLOCK, 128), 0), heads[0], heads[1]).astype(BF)
 
 
 def attend_back(queries, keys, values, prefix, totals, context, context_grad):
@@ -1269,17 +1370,16 @@
         (3, 0, half),
         (3, half, half),
     )
-    x, cot, (g_qkv, g_out, g_up, g_down, g_small), small_other = gather_all(
-        tokens, cotangent, shards, chunks
-    )
+    x, cot, (g_qkv, g_out, g_up, g_down, g_small), small_other, heads = gather_attend(
+        tokens, cotangent, shards, chunks, bias_qv.shape[1]
+    )
+    queries, key_heads, value_heads, context, totals = heads
 
     mine = g_small.reshape(2, 8, SMALL, 128)
     theirs = small_other.reshape(2, 8, SMALL, 128)
     first = jnp.where(c == 0, mine, theirs)
     every = jnp.concatenate([first, jnp.where(c == 0, theirs, mine)], axis=0)
     per = bias_qv.shape[1]
-    bias_values = mine[:, :, 0:2, :per].astype(F32)
-    bias_values = bias_values.transpose(2, 0, 1, 3).reshape(2, 2 * part)
     up_bias = mine[:, :, 2, : bias_up.shape[0]].astype(F32).reshape(2, hidden)
     rows = every[:, :, 3:9, :per].astype(F32).transpose(2, 1, 0, 3).reshape(6, model_width)
     full_gains, full_shifts = rows[:2], rows[2:]
@@ -1289,18 +1389,6 @@
     low_part = jnp.where(member == 0, source[2], source[3])
     prefix = (high * 16 + low_part).astype(jnp.int32)[None]
 
-    def kind(i):
-        return jnp.concatenate(
-            [g_qkv[z, :, i * part : (i + 1) * part] for z in range(2)], axis=1
-        )
-
-    def project(i):
-        return jnp.dot(x, kind(i), preferred_element_type=F32)
-
-    queries = (project(0) + bias_values[0]).astype(BF)
-    key_heads = project(1).astype(BF)
-    value_heads = (project(2) + bias_values[1]).astype(BF)
-    context, totals = attend(queries, key_heads, value_heads, prefix)
     branch_part = sum(
         jnp.einsum(
             "rk,dk->rd", context[:, z * part : (z + 1) * part], g_out[z], preferred_element_type=F32

time: 414 us -> 378 us (0.913)
  Pallas kernels: 263 us -> 237 us
  matrix products: 67.5 us -> 60.4 us
    pallas_call x2 -> x1, Pallas kernels: 130 us -> 94.6 us  [gather_attend(): pl.pallas_call(kernel, out_shape=[rows_shape, rows_shape, *full_shapes, f...]
    dot_general x3 -> x0, matrix products: 6.87 us -> none  [project(): return jnp.dot(x, kind(i), preferred_element_type=F32)]
    pallas_call x1, Pallas kernels: 92.7 us -> 99.4 us  [reduce_all(): pl.pallas_call(kernel, out_shape=[back, back, *[jax.ShapeDtypeStruct((r,...]
    dot_general x2, matrix products: 23.8 us -> 18.6 us  [chip_local(): jnp.dot(normed_low, g_up[z], preferred_element_type=F32) + up_bias[z]]
    dot_general x8, matrix products: 11.9 us -> 16.1 us  [outer(): return jnp.einsum('rm,rn->mn', a, b, preferred_element_type=F32).astype(BF)]
    unnamed x90 -> x76, local copies, waits for them, and re-layouts: 13.5 us -> 13.3 us
where the time goes in v2:
time: 378 us; the launch traced here: 372 us
  Pallas kernels  237 us (63%)
  matrix products  60.4 us (16%)
  other arithmetic  41.2 us (11%)
  local copies, waits for them, and re-layouts  28.9 us (8%)
  between operations  4.28 us (1%)
    pallas_call x1, Pallas kernels, reduce_all(): pl.pallas_call(kernel, out_shape=[back, back, *[jax.ShapeDtypeStruct((r,...  99.4 us
    pallas_call x1, Pallas kernels, gather_attend(): pl.pallas_call(kernel, out_shape=[rows_shape, rows_shape, *full_shapes, f...  94.6 us
    pallas_call x1, Pallas kernels, attend_back(): pl.pallas_call(kernel, grid=(pairs,), out_shape=[shape] * 3, in_specs=[pl...  24 us
    pallas_call x4, Pallas kernels, pair_swap(): pl.pallas_call(kernel, out_shape=jax.ShapeDtypeStruct(part.shape, part.dt...  19.4 us
    dot_general x2, matrix products, chip_local(): jnp.dot(normed_low, g_up[z], preferred_element_type=F32) + up_bias[z]  18.6 us
    dot_general x8, matrix products, outer(): return jnp.einsum('rm,rn->mn', a, b, preferred_element_type=F32).astype(BF)  16.1 us
    unnamed x76, local copies, waits for them, and re-layouts  13.3 us
    dot_general x2, matrix products, chip_local(): active_grad = jnp.dot(feed_grad, g_down[z], preferred_element_type=F32)  8.8 us

profile of v2, /device:TPU:0, one launch (start us, length us, event | category | flops | bytes accessed | tf_op | source)
XLA Modules:
  0.0 372.2 jit_solution(15036930909970969381)
XLA Ops:
  4.8 1.5 copy.78
  8.2 94.6 %shard_map.186 = (bf16[8,128,768]{2,1,0:T(8,128)(2,1)}, bf16[8,128,768]{2,1,0:T(8,128)(2,1)}, bf16[2,768,576]{2,1,0:T(8,128)(2,1)}, bf16[2,768,192]{2,1,0:T(8,12...) custom-call(bf16[2,256,768]{2,1,0:T(8,128)(2,1)} %refs_0_.1, ...), custom_call_target="tpu_custom_call" | custom-call | tf_op jit(solution)/shard_map/pallas_call | solution.py:799
  108.2 2.1 convert_reduce_fusion
  111.0 1.6 fusion.62
  112.6 1.8 add_convert_fusion.7.src
  114.4 7.9 %shard_map.187 = bf16[1024,768]{1,0:T(8,128)(2,1)} custom-call(bf16[1024,768]{1,0:T(8,128)(2,1)} %add_convert_fusion.7.src), custom_call_target="tpu_custom_call" | custom-call | tf_op jit(solution)/shard_map/pallas_call | solution.py:415
  122.4 3.1 fusion.86
  126.6 1.1 copy-done.18
  127.7 9.4 %multiply_convert_fusion = (bf16[1024,768]{1,0:T(8,128)(2,1)S(1)}, f32[1024,768]{1,0:T(8,128)}, f32[1024,768]{1,0:T(8,128)}) fusion(f32[768]{0:T(1024)S(1)} %add.176, bf16[1024,768]{1,0:T(8,128)(2,1)S(1)} %fusion.19, bf16[2,768,768]{2,1,0:T(8,128)(2,1)S(1)} %copy-done.18), kind=kOutput, calls=%fused_computation.32 | convolution fusion | flops 1259864064 | bytes 10620928 | tf_op jit(solution)/shard_map/dot_general | solution.py:1406
  137.1 9.3 %multiply_convert_fusion.1 = (bf16[1024,768]{1,0:T(8,128)(2,1)S(1)}, f32[1024,768]{1,0:T(8,128)}, f32[1024,768]{1,0:T(8,128)}) fusion(f32[768]{0:T(1024)S(1)} %add.173, bf16[1024,768]{1,0:T(8,128)(2,1)S(1)} %fusion.19, bf16[2,768,768]{2,1,0:T(8,128)(2,1)S(1)} %copy-done.18), kind=kOutput, calls=%fused_computation.45 | convolution fusion | flops 1259864064 | bytes 10620928 | tf_op jit(solution)/shard_map/dot_general | solution.py:1406
  146.3 1.2 copy-done.26
  147.6 1.4 fusion.38
  149.0 2.6 add_convert_fusion.6.src
  151.6 3.8 %shard_map.188 = bf16[1024,768]{1,0:T(8,128)(2,1)} custom-call(bf16[1024,768]{1,0:T(8,128)(2,1)} %add_convert_fusion.6.src), custom_call_target="tpu_custom_call" | custom-call | tf_op jit(solution)/shard_map/pallas_call | solution.py:415
  155.4 3.1 fusion.83
  159.1 2.0 copy-done.1
  161.1 1.3 fusion.8
  162.5 3.3 convert_reduce_fusion.1
  166.5 5.5 %convert_reduce_fusion.3 = (f32[768]{0:T(1024)S(1)}, bf16[1024,768]{1,0:T(8,128)(2,1)}) fusion(f32[1024,768]{1,0:T(8,128)S(1)} %copy-done.31, bf16[1024,768]{1,0:T(8,128)(2,1)S(1)} %get-tuple-element.107, bf16[2,768,768]{2,1,0:T(8,128)(2,1)S(1)} %copy-done.21, f32[1024,768]{1,0:T(8,128)} %get-tuple-element.144, f32[768]{0:T(1024)S(1)} %add.176), kind=kOutput, calls=%fused_computation.18 | convolution fusion | flops 1221328128 | bytes 10624000 | tf_op jit(solution)/shard_map/dot_general | solution.py:1424
  172.0 3.3 convert_reduce_fusion.4
  175.3 2.5 fusion.23
  177.8 2.5 fusion.22
  180.6 3.5 fusion.21
  184.1 1.5 fusion.20
  185.7 2.8 pad_maximum_fusion
  188.6 1.4 fusion.42
  190.0 2.6 add_convert_fusion.2.src
  192.6 3.8 %shard_map.189 = bf16[1024,768]{1,0:T(8,128)(2,1)} custom-call(bf16[1024,768]{1,0:T(8,128)(2,1)} %add_convert_fusion.2.src), custom_call_target="tpu_custom_call" | custom-call | tf_op jit(solution)/shard_map/pallas_call | solution.py:415
  196.4 6.0 %multiply_reduce_fusion = (f32[768]{0:T(1024)S(1)}, f32[1024]{0:T(1024)S(1)}, f32[1024]{0:T(1024)S(1)}, f32[768]{0:T(1024)S(1)}, f32[1024,768]{1,0:T(8,128)S(1)}, /*index=5*/bf16[1024,768]{1,0:T(8,128)(2,1)}) fusion(f32[1024,768]{1,0:T(8,128)S(1)} %get-tuple-element.119, f32[1024]{0:T(1024)S(1)} %add_rsqrt_fusion.1, f32[1024]{0:T(1024)S(1)} %broadcast_multiply_fusion.4, ...), kind=kLoop, calls=%fused_computation.17 | loop fusion | flops 18870784 | bytes 15776768 | tf_op jit(solution)/shard_map/reduce_sum | solution.py:29
  202.5 2.8 convert_reduce_fusion.2
  205.9 2.5 fusion.27
  211.9 1.2 pad_maximum_fusion.5.do_ref
  213.0 24.0 %shard_map.190 = (bf16[1024,384]{1,0:T(8,128)(2,1)}, bf16[1024,384]{1,0:T(8,128)(2,1)}, bf16[1024,384]{1,0:T(8,128)(2,1)}) custom-call(s32[1]{0:T(128)} %bitcast.23.prefix_ref, bf16[1024,384]{1,0:T(8,128)(2,1)} %get-tuple-element.41.q_ref, bf16[1024,384]{1,0:T(8,128)(2,1)} %get-tuple-element.42.k_ref, bf16[1024,384]{1,0:T(8,128)(2,1)} %get-tuple-element.43.v_ref, ...), custom_call_target="tpu_custom_call" | custom-call | tf_op jit(solution)/shard_map/pallas_call | solution.py:1321
  237.1 1.4 convert_reduce_fusion.6
  238.5 1.3 convert_reduce_fusion.5
  240.8 1.6 fusion.89
  242.9 1.6 fusion.25
  244.5 1.6 fusion.24
  246.1 1.7 pad_maximum_fusion.2.refs_2_
  248.3 1.4 fusion.55
  249.7 2.6 add_convert_fusion.1.src
  252.3 3.8 %shard_map.191 = bf16[1024,768]{1,0:T(8,128)(2,1)} custom-call(bf16[1024,768]{1,0:T(8,128)(2,1)} %add_convert_fusion.1.src), custom_call_target="tpu_custom_call" | custom-call | tf_op jit(solution)/shard_map/pallas_call | solution.py:415
  256.1 3.5 add_convert_fusion.refs_1_
  259.7 99.4 %shard_map.192 = (bf16[2,256,768]{2,1,0:T(8,128)(2,1)}, bf16[2,256,768]{2,1,0:T(8,128)(2,1)}, f32[96,576]{1,0:T(8,128)}, f32[96,192]{1,0:T(8,128)}, f32[96,768]{...) custom-call(bf16[1024,768]{1,0:T(8,128)(2,1)} %get-tuple-element.120.refs_0_, ...), custom_call_target="tpu_custom_call" | custom-call | tf_op jit(solution)/shard_map/pallas_call | solution.py:1175
  360.6 1.2 slice.178
  361.8 1.3 slice_reduce_fusion.2
  363.7 1.6 copy.100
  367.3 2.4 convert_element_type.202
  (149 shorter events, 24.5 us)
Async XLA Ops:
  102.9 8.1 %copy-start.5 = (bf16[1024,384]{1,0:T(8,128)(2,1)S(1)}, bf16[1024,384]{1,0:T(8,128)(2,1)}, u32[]{:S(2)}) copy-start(bf16[1024,384]{1,0:T(8,128)(2,1)} %get-tuple-element.34.o_ref) | copy-start | bytes 2359300
  104.8 7.8 %copy-start.7 = (bf16[2,768,192]{2,1,0:T(8,128)(2,1)S(1)}, bf16[2,768,192]{2,1,0:T(8,128)(2,1)}, u32[]{:S(2)}) copy-start(bf16[2,768,192]{2,1,0:T(8,128)(2,1)} %get-tuple-element.35) | copy-start | bytes 1769476
  126.0 1.7 copy-start.18
  127.7 9.4 %copy-start.10 = (bf16[1024,768]{1,0:T(8,128)(2,1)}, bf16[1024,768]{1,0:T(8,128)(2,1)S(1)}, u32[]{:S(2)}) copy-start(bf16[1024,768]{1,0:T(8,128)(2,1)S(1)} %fusion.19) | copy-start | bytes 4718596
  137.1 11.9 %copy-start.23 = (bf16[1024,768]{1,0:T(8,128)(2,1)}, bf16[1024,768]{1,0:T(8,128)(2,1)S(1)}, u32[]{:S(2)}) copy-start(bf16[1024,768]{1,0:T(8,128)(2,1)S(1)} %get-tuple-element.114) | copy-start | bytes 4718596
  137.1 10.5 %copy-start.20 = (bf16[2,768,768]{2,1,0:T(8,128)(2,1)S(1)}, bf16[2,768,768]{2,1,0:T(8,128)(2,1)}, u32[]{:S(2)}) copy-start(bf16[2,768,768]{2,1,0:T(8,128)(2,1)} %get-tuple-element.39) | copy-start | bytes 7077892
  146.3 1.2 copy-start.26
  158.5 3.8 %copy-start = (f32[1024,768]{1,0:T(8,128)}, f32[1024,768]{1,0:T(8,128)S(1)}, u32[]{:S(2)}) copy-start(f32[1024,768]{1,0:T(8,128)S(1)} %get-tuple-element.113) | copy-start | bytes 9437188
  158.5 2.5 copy-start.1
  162.5 3.3 copy-start.21
  162.5 4.0 %copy-start.31 = (f32[1024,768]{1,0:T(8,128)S(1)}, f32[1024,768]{1,0:T(8,128)}, u32[]{:S(2)}) copy-start(f32[1024,768]{1,0:T(8,128)} %get-tuple-element.115) | copy-start | bytes 9437188
  166.5 5.5 %copy-start.29 = (f32[1024,768]{1,0:T(8,128)S(1)}, f32[1024,768]{1,0:T(8,128)}, u32[]{:S(2)}) copy-start(f32[1024,768]{1,0:T(8,128)} %get-tuple-element.117) | copy-start | bytes 9437188
  166.5 5.5 %copy-start.30 = (f32[1024,768]{1,0:T(8,128)S(1)}, f32[1024,768]{1,0:T(8,128)}, u32[]{:S(2)}) copy-start(f32[1024,768]{1,0:T(8,128)} %get-tuple-element.143) | copy-start | bytes 9437188
  172.0 3.3 copy-start.24
  175.3 2.5 copy-start.27
  180.5 3.5 copy-start.11
  180.5 3.5 copy-start.28
  184.1 1.5 copy-start.13
  184.1 1.6 copy-start.14
  185.7 2.9 copy-start.19
  188.6 1.4 copy-start.25
  205.6 2.8 copy-start.2
  205.6 2.8 copy-start.6
  208.4 1.7 copy-start.8
  237.1 5.3 %copy-start.4 = (bf16[1024,384]{1,0:T(8,128)(2,1)S(1)}, bf16[1024,384]{1,0:T(8,128)(2,1)}, u32[]{:S(2)}) copy-start(bf16[1024,384]{1,0:T(8,128)(2,1)} %get-tuple-element.45) | copy-start | bytes 2359300
  237.1 5.6 %copy-start.12 = (bf16[1024,384]{1,0:T(8,128)(2,1)S(1)}, bf16[1024,384]{1,0:T(8,128)(2,1)}, u32[]{:S(2)}) copy-start(bf16[1024,384]{1,0:T(8,128)(2,1)} %get-tuple-element.46) | copy-start | bytes 2359300
  240.8 2.1 copy-start.9
  246.1 2.2 copy-start.22
  252.3 3.8 %copy-start.3 = (f32[1024,768]{1,0:T(8,128)S(1)}, f32[1024,768]{1,0:T(8,128)}, u32[]{:S(2)}) copy-start(f32[1024,768]{1,0:T(8,128)} %get-tuple-element.110) | copy-start | bytes 9437188
  359.1 10.6 %copy-start.15 = (bf16[2,256,768]{2,1,0:T(8,128)(2,1)S(1)}, bf16[2,256,768]{2,1,0:T(8,128)(2,1)}, u32[]{:S(2)}) copy-start(bf16[2,256,768]{2,1,0:T(8,128)(2,1)} %get-tuple-element.163) | copy-start | bytes 2359300
  359.1 11.5 %copy-start.17 = (f32[96,768]{1,0:T(8,128)S(1)}, f32[96,768]{1,0:T(8,128)}, u32[]{:S(2)}) copy-start(f32[96,768]{1,0:T(8,128)} %get-tuple-element.168) | copy-start | bytes 884740
  359.1 12.2 %copy-start.16 = (f32[96,768]{1,0:T(8,128)S(1)}, f32[96,768]{1,0:T(8,128)}, u32[]{:S(2)}) copy-start(f32[96,768]{1,0:T(8,128)} %get-tuple-element.55) | copy-start | bytes 884740

commit v3 on v2

--- a/solution.py
+++ b/solution.py
@@ -446,8 +446,10 @@
         base = 2 + count
         xf, cf = refs[base], refs[base + 1]
         full = refs[base + 2 : base + 2 + count]
-        small_other, q_out, k_out, v_out, o_out, lt_out = refs[base + 2 + count : base + 8 + count]
-        stage = refs[base + 8 + count : base + 8 + 2 * count]
+        small_other, q_out, k_out, v_out, o_out, lt_out, limit_out = refs[
+            base + 2 + count : base + 9 + count
+        ]
+        stage = refs[base + 9 + count : base + 9 + 2 * count]
         (
             x_rows,
             weight,
@@ -471,7 +473,7 @@
             b_recv,
             o_send,
             o_recv,
-        ) = refs[base + 8 + 2 * count :]
+        ) = refs[base + 9 + 2 * count :]
         d, t, k, c, xb, yb, dx, dy = place()
         mate = d + 1 - 2 * c
         u = t + c * (3 - 2 * t)
@@ -743,6 +745,7 @@
         for copy in load_rows:
             copy.wait()
         load_weight.wait()
+        limit_out[...] = jnp.broadcast_to(prefix_of(), limit_out.shape)
         project()
         todo = []
         for i in range(4, n_chunks):
@@ -805,9 +808,10 @@
             full_shapes[-1],
             *[head_shape] * 4,
             lt_shape,
+            jax.ShapeDtypeStruct((8, 128), F32),
         ],
         in_specs=[any_spec] * (2 + count),
-        out_specs=[any_spec] * (3 + count) + [vmem] * 5,
+        out_specs=[any_spec] * (3 + count) + [vmem] * 6,
         scratch_shapes=[
             *[pltpu.VMEM(s.shape, s.dtype) for s in shards],
             pltpu.VMEM((length, width), BF),
@@ -846,20 +850,25 @@
     )
 
 
-def reduce_all(output, token_grad, grads, chunks):
+def back_reduce(output, residual, x, weight, heads, totals, limit, ready, tile, chunks):
+    part_cols = weight.shape[2] // 3
+    heads_width = 2 * part_cols
+    grads = [jax.ShapeDtypeStruct(weight.shape, BF), *ready]
     count = len(grads)
     n_chunks = len(chunks)
     length, width = output.shape
     half = length // 8
+    blocks = length // BLOCK
     rows_of = [g.shape[1] // 8 for g in grads]
 
     def kernel(*refs):
-        res, tgr = refs[0], refs[1]
-        part = refs[2 : 2 + count]
-        base = 2 + count
-        res_out, tgr_out = refs[base], refs[base + 1]
-        final = refs[base + 2 : base + 2 + count]
-        base += 2 + count
+        res, residual_hbm, x_hbm, weight_hbm = refs[:4]
+        q_ref, k_ref, v_ref, o_ref, do_ref, lt_ref, limit_ref, tile_ref = refs[4:12]
+        others = refs[12 : 11 + count]
+        base = 11 + count
+        res_out, tgr_out, tile_own, tile_mate = refs[base : base + 4]
+        final = refs[base + 4 : base + 4 + count]
+        base += 4 + count
         got1 = refs[base : base + count]
         sum1 = refs[base + count : base + 2 * count]
         got2 = refs[base + 2 * count : base + 3 * count]
@@ -883,7 +892,30 @@
             y_recv,
             p_send,
             p_recv,
+            grad_own,
+            x_rows,
+            weight_rows,
+            residual_rows,
+            dots,
+            acc,
+            acc_rows,
+            dq,
+            dk,
+            dv,
+            mixed,
+            mate_part,
+            mate_got,
+            own_part,
+            row_out,
+            load_sem,
+            s_send,
+            s_recv,
+            t_send,
+            t_recv,
+            tile_sum,
+            tile_got,
         ) = refs[base + 8 * count :]
+        part = (grad_own, *others)
         d, t, k, c, xb, yb, dx, dy = place()
         mate = d + 1 - 2 * c
         u = t + c * (3 - 2 * t)
@@ -1123,13 +1155,176 @@
                 p_copy(i).wait_recv()
                 final[s][:, spot] = got5[s][:, spot].astype(F32)
 
+        loads = [
+            pltpu.make_async_copy(x_hbm, x_rows, load_sem.at[0]),
+            pltpu.make_async_copy(weight_hbm, weight_rows, load_sem.at[1]),
+            pltpu.make_async_copy(residual_hbm, residual_rows, load_sem.at[2]),
+        ]
+
+        def attention(pair, kb):
+            if kb == 0:
+                back_start(pair, o_ref, do_ref, dots, acc)
+            back_block(
+                pair, kb, q_ref, k_ref, v_ref, lt_ref, do_ref, dots, acc, dk, dv, limit_ref[0:1, 0:1]
+            )
+            if kb == blocks - 1:
+                dq[:, pl.ds(pair * 128, 128)] = (acc[...] * DH**-0.5).astype(BF)
+
+        def mate_copy(i):
+            return remote(mate_part.at[i], mate_got.at[i], t_send.at[0, i], t_recv.at[0, i], mate, t)
+
+        def mix(i):
+            rows = pl.ds(i * BLOCK, BLOCK)
+            kinds = [ref[rows, :] for ref in (dq, dk, dv)]
+            share = jnp.zeros((BLOCK, width), F32)
+            for z in range(2):
+                both = jnp.concatenate(
+                    [v[:, z * part_cols : (z + 1) * part_cols] for v in kinds], axis=1
+                )
+                mixed[z, rows, :] = both
+                share = share + dot_nt(both, weight_rows[z])
+            acc_rows[...] = share
+            mate_part[i] = acc_rows[pl.ds((1 - c) * half, half), :].astype(BF)
+            own_part[i] = (
+                acc_rows[pl.ds(c * half, half), :]
+                + residual_rows[pl.ds((2 * i + c) * half, half), :]
+            )
+            mate_copy(i).start()
+
+        def row_copy(i):
+            return remote(
+                row_out.at[i],
+                tgr_out.at[t % 2, pl.ds(c * half, half)],
+                t_send.at[1, i],
+                t_recv.at[1, 2 * (t % 2) + c],
+                2 * k + t // 2,
+                i,
+            )
+
+        def send_rows(i):
+            mate_copy(i).wait_recv()
+            row_out[i] = (own_part[i] + mate_got[i].astype(F32)).astype(BF)
+            here = jnp.logical_and(i == t, c == t // 2)
+
+            @pl.when(here)
+            def _():
+                store = pltpu.make_async_copy(
+                    row_out.at[i], tgr_out.at[t % 2, pl.ds(c * half, half)], row_sem
+                )
+                store.start()
+                store.wait()
+
+            @pl.when(jnp.logical_not(here))
+            def _():
+                row_copy(i).start()
+
+        def settle_rows():
+            for i in range(4):
+                mate_copy(i).wait_send()
+
+                @pl.when(jnp.logical_not(jnp.logical_and(i == t, c == t // 2)))
+                def _():
+                    row_copy(i).wait_send()
+
+            for m in range(2):
+                for core in range(2):
+                    spot = tgr_out.at[m, pl.ds(core * half, half)]
+
+                    @pl.when(jnp.logical_not(jnp.logical_and(2 * c + m == t, core == c)))
+                    def _():
+                        remote(
+                            row_out.at[0],
+                            spot,
+                            t_send.at[1, 0],
+                            t_recv.at[1, 2 * m + core],
+                            mate,
+                            t,
+                        ).wait_recv()
+
+        def weight_grad(j):
+            rows = pl.ds(j * BLOCK, BLOCK)
+            for z in range(2):
+                grad_own[z, rows, :] = dot_tn(x_rows[:, rows], mixed[z]).astype(BF)
+
+        def tile_copy(stage, goal_dp, goal_t, slot):
+            return remote(
+                tile_sum.at[stage],
+                tile_got.at[slot],
+                s_send.at[slot],
+                s_recv.at[slot],
+                goal_dp,
+                goal_t,
+            )
+
+        def tile_start():
+            tile_sum[0] = tile_ref[...]
+            for row, ref in ((0, dq), (2, dv)):
+                sums = jnp.sum(ref[...].astype(F32), axis=0, keepdims=True)
+                for z in range(2):
+                    tile_sum[0, row + z : row + z + 1, 0:part_cols] = sums[
+                        :, z * part_cols : (z + 1) * part_cols
+                    ]
+            tile_copy(0, dx, t, 0).start()
+
+        def tile_second():
+            tile_copy(0, dx, t, 0).wait_recv()
+            tile_sum[1] = tile_sum[0] + tile_got[0]
+            tile_copy(1, dy, t, 1).start()
+
+        def tile_third():
+            tile_copy(1, dy, t, 1).wait_recv()
+            tile_sum[2] = tile_sum[1] + tile_got[1]
+            for step in range(1, 4):
+                tile_copy(2, d, (t + step) % 4, 1 + step).start()
+
+        def tile_fourth():
+            for step in range(1, 4):
+                tile_copy(2, d, t, 1 + step).wait_recv()
+            tile_sum[3] = (tile_sum[2] + tile_got[2]) + (tile_got[3] + tile_got[4])
+            tile_copy(3, mate, t, 5).start()
+
+        def tile_last():
+            tile_copy(3, mate, t, 5).wait_recv()
+            tile_own[...] = tile_sum[3]
+            tile_mate[...] = tile_got[5]
+            for slot, stage in enumerate((0, 1, 2, 2, 2, 3)):
+                tile_copy(stage, mate, t, slot).wait_send()
+
+        levels = [level_first, level_second, level_line, level_pass, level_near, level_mate]
+        work = [partial(attention, pair, kb) for pair in range(heads_width // 128) for kb in range(blocks)]
+        work += [partial(mix, i) for i in range(blocks)]
+        work += [partial(weight_grad, j) for j in range(width // BLOCK)]
+        for copy in loads:
+            copy.start()
+        level_first(0)
+        level_first(1)
         return_rows(0, res, res_out, True)
-        return_rows(1, tgr, tgr_out, True)
-        skewed(
-            n_chunks, [level_first, level_second, level_line, level_pass, level_near, level_mate]
-        )
+        for copy in loads:
+            copy.wait()
+        done = 0
+        for slot in range(n_chunks + 5):
+            if slot < n_chunks - 1:
+                upto = -(-len(work) * (slot + 1) // (n_chunks - 1))
+                for unit in work[done:upto]:
+                    unit()
+                done = upto
+            if slot == n_chunks - 2:
+                tile_start()
+            for lag, level in enumerate(levels):
+                i = slot + 1 - lag
+                if lag == 0 and i < 2:
+                    continue
+                if 0 <= i < n_chunks:
+                    level(i)
+            if slot == n_chunks - 2:
+                for i in range(4):
+                    send_rows(i)
+            if slot >= n_chunks - 1:
+                tail = slot - (n_chunks - 1)
+                if tail < 4:
+                    (tile_second, tile_third, tile_fourth, tile_last)[tail]()
         return_rows(0, res, res_out, False)
-        return_rows(1, tgr, tgr_out, False)
+        settle_rows()
         for i in range(n_chunks):
             for copy in first_copies(i):
                 copy.wait_send()
@@ -1172,15 +1367,18 @@
             )[kind]
             scratch.append(pltpu.VMEM(shape, dtype))
     back = jax.ShapeDtypeStruct((2, 2 * half, width), output.dtype)
+    tiles = jax.ShapeDtypeStruct(tile.shape, F32)
     outs = pl.pallas_call(
         kernel,
         out_shape=[
             back,
             back,
+            tiles,
+            tiles,
             *[jax.ShapeDtypeStruct((r, g.shape[2]), F32) for r, g in zip(rows_of, grads)],
         ],
-        in_specs=[any_spec, any_spec] + [vmem] * count,
-        out_specs=[any_spec, any_spec] + [vmem] * count,
+        in_specs=[any_spec] * 4 + [vmem] * (7 + count),
+        out_specs=[any_spec, any_spec] + [vmem] * (2 + count),
         scratch_shapes=[
             *scratch,
             pltpu.VMEM((half, width), output.dtype),
@@ -1197,12 +1395,34 @@
             dma((n_chunks,)),
             dma((n_chunks,)),
             dma((n_chunks,)),
+            pltpu.VMEM(weight.shape, BF),
+            pltpu.VMEM((length, width), BF),
+            pltpu.VMEM(weight.shape, BF),
+            pltpu.VMEM((length, width), F32),
+            pltpu.VMEM((8, length), F32),
+            pltpu.VMEM((length, 128), F32),
+            pltpu.VMEM((BLOCK, width), F32),
+            pltpu.VMEM((length, heads_width), BF),
+            pltpu.VMEM((length, heads_width), BF),
+            pltpu.VMEM((length, heads_width), BF),
+            pltpu.VMEM((2, length, 3 * part_cols), BF),
+            pltpu.VMEM((4, half, width), BF),
+            pltpu.VMEM((4, half, width), BF),
+            pltpu.VMEM((4, half, width), F32),
+            pltpu.VMEM((4, half, width), BF),
+            dma((3,)),
+            dma((6,)),
+            dma((6,)),
+            dma((2, 4)),
+            dma((2, 4)),
+            pltpu.VMEM((4, *tile.shape), F32),
+            pltpu.VMEM((6, *tile.shape), F32),
         ],
         compiler_params=pltpu.CompilerParams(
-            collective_id=2, has_side_effects=True, vmem_limit_bytes=60 * 1024 * 1024
+            collective_id=2, has_side_effects=True, vmem_limit_bytes=62 * 1024 * 1024
         ),
-    )(output, token_grad, *grads)
-    return outs[0], outs[1], outs[2:]
+    )(output, residual, x, weight, *heads, totals, limit, tile, *ready)
+    return outs[0], outs[1], outs[2], outs[3], outs[4:]
 
 
 BLOCK = 256
@@ -1256,84 +1476,57 @@
     o_ref[rows, lanes] = jnp.where(lane_half((BLOCK, 128), 0), heads[0], heads[1]).astype(BF)
 
 
-def attend_back(queries, keys, values, prefix, totals, context, context_grad):
-    length, width = queries.shape
+def back_start(pair, o_ref, do_ref, dots, acc):
+    head_row = lax.broadcasted_iota(jnp.int32, (8, 128), 0)
+    lane = lax.broadcasted_iota(jnp.int32, (8, 128), 1)
+    pick = (lane // DH == head_row).astype(F32)
+    lanes = pl.ds(pair * 128, 128)
+    dots[...] = lax.dot_general(
+        pick,
+        do_ref[:, lanes].astype(F32) * o_ref[:, lanes].astype(F32),
+        (((1,), (1,)), ((), ())),
+        precision=lax.Precision.HIGHEST,
+        preferred_element_type=F32,
+    )
+    acc[...] = jnp.zeros_like(acc)
+
+
+def back_block(pair, kb, q_ref, k_ref, v_ref, lt_ref, do_ref, dots, acc, dk_ref, dv_ref, limit):
+    length = q_ref.shape[0]
     blocks = length // BLOCK
-    pairs = width // 128
-
-    def kernel(prefix_ref, q_ref, k_ref, v_ref, lt_ref, o_ref, do_ref, dq_ref, dk_ref, dv_ref, acc):
-        limit = prefix_ref[0]
-        scaling = jnp.asarray(DH**-0.5, BF)
-        head_row = lax.broadcasted_iota(jnp.int32, (8, 128), 0)
-        lane = lax.broadcasted_iota(jnp.int32, (8, 128), 1)
-        pick = (lane // DH == head_row).astype(F32)
-        row_dots = []
-        for qb in range(blocks):
-            rows = pl.ds(qb * BLOCK, BLOCK)
-            both = do_ref[rows, :].astype(F32) * o_ref[rows, :].astype(F32)
-            row_dots.append(
-                lax.dot_general(
-                    pick,
-                    both,
-                    (((1,), (1,)), ((), ())),
-                    precision=lax.Precision.HIGHEST,
-                    preferred_element_type=F32,
-                )
-            )
-        acc[...] = jnp.zeros_like(acc)
-        for kb in range(blocks):
-            keys_at = pl.ds(kb * BLOCK, BLOCK)
-            key = k_ref[keys_at, :]
-            value = v_ref[keys_at, :]
-            dk = jnp.zeros((BLOCK, 128), F32)
-            dv = jnp.zeros((BLOCK, 128), F32)
-            for qb in range(blocks):
-                if kb >= reach(qb, blocks):
-                    continue
-                rows = pl.ds(qb * BLOCK, BLOCK)
-                q_pair = q_ref[rows, :] * scaling
-                do_pair = do_ref[rows, :]
-                for h in range(2):
-                    half = lane_half((BLOCK, 128), h)
-                    zero = jnp.zeros((BLOCK, 128), BF)
-                    q = jnp.where(half, q_pair, zero)
-                    do = jnp.where(half, do_pair, zero)
-                    s = dot_nt(key, q)
-                    if kb >= qb:
-                        key_id = lax.broadcasted_iota(jnp.int32, (BLOCK, BLOCK), 0) + kb * BLOCK
-                        row_id = lax.broadcasted_iota(jnp.int32, (BLOCK, BLOCK), 1) + qb * BLOCK
-                        seen = key_id <= row_id
-                        if kb * BLOCK < length // 2:
-                            seen = jnp.logical_or(seen, key_id < limit)
-                        s = jnp.where(seen, s, MASKED_SCORE)
-                    p = jnp.exp(s - lt_ref[h, 0:1, rows])
-                    dp = dot_nt(value, do)
-                    ds = (p * (dp - row_dots[qb][h : h + 1, :])).astype(BF)
-                    dv = dv + jnp.dot(p.astype(BF), do, preferred_element_type=F32)
-                    dk = dk + jnp.dot(ds, q, preferred_element_type=F32)
-                    acc[rows, :] += dot_tn(ds, jnp.where(half, key, zero))
-            dk_ref[keys_at, :] = dk.astype(BF)
-            dv_ref[keys_at, :] = dv.astype(BF)
-        dq_ref[...] = (acc[...] * DH**-0.5).astype(BF)
-
-    pair = pl.BlockSpec((length, 128), lambda i: (0, i))
-    shape = jax.ShapeDtypeStruct((length, width), BF)
-    return pl.pallas_call(
-        kernel,
-        grid=(pairs,),
-        out_shape=[shape] * 3,
-        in_specs=[
-            pl.BlockSpec(memory_space=pltpu.SMEM),
-            pair,
-            pair,
-            pair,
-            pl.BlockSpec((2, 8, length), lambda i: (i, 0, 0)),
-            pair,
-            pair,
-        ],
-        out_specs=[pair] * 3,
-        scratch_shapes=[pltpu.VMEM((length, 128), F32)],
-    )(prefix, queries, keys, values, totals, context, context_grad)
+    lanes = pl.ds(pair * 128, 128)
+    keys_at = pl.ds(kb * BLOCK, BLOCK)
+    key = k_ref[keys_at, lanes]
+    value = v_ref[keys_at, lanes]
+    zero = jnp.zeros((BLOCK, 128), BF)
+    dk = jnp.zeros((BLOCK, 128), F32)
+    dv = jnp.zeros((BLOCK, 128), F32)
+    for qb in range(blocks):
+        if kb >= reach(qb, blocks):
+            continue
+        rows = pl.ds(qb * BLOCK, BLOCK)
+        q_pair = q_ref[rows, lanes] * jnp.asarray(DH**-0.5, BF)
+        do_pair = do_ref[rows, lanes]
+        for h in range(2):
+            half = lane_half((BLOCK, 128), h)
+            q = jnp.where(half, q_pair, zero)
+            do = jnp.where(half, do_pair, zero)
+            s = dot_nt(key, q)
+            if kb >= qb:
+                key_id = lax.broadcasted_iota(jnp.int32, (BLOCK, BLOCK), 0) + kb * BLOCK
+                row_id = lax.broadcasted_iota(jnp.int32, (BLOCK, BLOCK), 1) + qb * BLOCK
+                seen = key_id <= row_id
+                if kb * BLOCK < length // 2:
+                    seen = jnp.logical_or(seen, key_id.astype(F32) < limit)
+                s = jnp.where(seen, s, MASKED_SCORE)
+            p = jnp.exp(s - lt_ref[2 * pair + h, 0:1, rows])
+            dp = dot_nt(value, do)
+            ds = (p * (dp - dots[h : h + 1, rows])).astype(BF)
+            dv = dv + jnp.dot(p.astype(BF), do, preferred_element_type=F32)
+            dk = dk + jnp.dot(ds, q, preferred_element_type=F32)
+            acc[rows, :] += dot_tn(ds, jnp.where(half, key, zero))
+    dk_ref[keys_at, lanes] = dk.astype(BF)
+    dv_ref[keys_at, lanes] = dv.astype(BF)
 
 
 def chip_local(
@@ -1373,7 +1566,7 @@
     x, cot, (g_qkv, g_out, g_up, g_down, g_small), small_other, heads = gather_attend(
         tokens, cotangent, shards, chunks, bias_qv.shape[1]
     )
-    queries, key_heads, value_heads, context, totals = heads
+    queries, key_heads, value_heads, context, totals, limit = heads
 
     mine = g_small.reshape(2, 8, SMALL, 128)
     theirs = small_other.reshape(2, 8, SMALL, 128)
@@ -1383,11 +1576,6 @@
     up_bias = mine[:, :, 2, : bias_up.shape[0]].astype(F32).reshape(2, hidden)
     rows = every[:, :, 3:9, :per].astype(F32).transpose(2, 1, 0, 3).reshape(6, model_width)
     full_gains, full_shifts = rows[:2], rows[2:]
-    source = lax.dynamic_index_in_dim(every[0, :, 9, :4].astype(F32), 2 * k + t // 2, 0, False)
-    member = t % 2
-    high = jnp.where(member == 0, source[0], source[1])
-    low_part = jnp.where(member == 0, source[2], source[3])
-    prefix = (high * 16 + low_part).astype(jnp.int32)[None]
 
     branch_part = sum(
         jnp.einsum(
@@ -1437,56 +1625,33 @@
     context_grad = jnp.concatenate(
         [jnp.dot(branch_grad, g_out[z], preferred_element_type=F32) for z in range(2)], axis=1
     ).astype(BF)
-    mixed = attend_back(queries, key_heads, value_heads, prefix, totals, context, context_grad)
-    mixed_low = [
-        jnp.concatenate([m[:, z * part : (z + 1) * part] for m in mixed], axis=1)
-        for z in range(2)
-    ]
-    token_part = sum(
-        jnp.einsum("re,de->rd", mixed_low[z], g_qkv[z], preferred_element_type=F32)
-        for z in range(2)
-    ).astype(BF)
-    token_grad = residual_one + (token_part.astype(F32) + pair_swap(token_part).astype(F32))
-
     def outer(a, b):
         return jnp.einsum("rm,rn->mn", a, b, preferred_element_type=F32).astype(BF)
 
     grads = (
-        jnp.stack([outer(x, mixed_low[z]) for z in range(2)]),
         jnp.stack(
             [outer(branch_grad, context[:, z * part : (z + 1) * part]) for z in range(2)]
         ),
         jnp.stack([outer(normed_low, upper[z]) for z in range(2)]),
         jnp.stack([outer(feed_grad, active[z]) for z in range(2)]),
     )
-    up_bias_grad = jnp.stack([jnp.sum(v.astype(F32), axis=0) for v in upper])
-    bias_grad = jnp.stack(
-        [jnp.sum(m.astype(F32), axis=0) for m in (mixed[0], mixed[2])]
-    )
-    row_grads = jnp.stack(
+    tile = jnp.concatenate(
         [
-            gain_one,
-            gain_two,
-            jnp.sum(branch_grad.astype(F32), axis=0),
-            shift_one,
-            jnp.sum(feed_grad.astype(F32), axis=0),
-            shift_two,
+            jnp.zeros((4, hidden), F32),
+            jnp.stack([jnp.sum(v.astype(F32), axis=0) for v in upper]),
+            jnp.stack(
+                [
+                    gain_one,
+                    gain_two,
+                    jnp.sum(branch_grad.astype(F32), axis=0),
+                    shift_one,
+                    jnp.sum(feed_grad.astype(F32), axis=0),
+                    shift_two,
+                ]
+            ),
+            jnp.zeros((4, hidden), F32),
         ]
     )
-    spread_bias = bias_grad.reshape(2, 2, 8, per).transpose(1, 2, 0, 3)
-    spread_rows = row_grads.reshape(6, 8, 4, per).transpose(2, 1, 0, 3)
-    spread_rows = lax.dynamic_slice_in_dim(spread_rows, 2 * c, 2, 0)
-    spread_up = up_bias_grad.reshape(2, 8, 1, bias_up.shape[0])
-
-    def wide(v):
-        return jnp.pad(v, ((0, 0), (0, 0), (0, 0), (0, 128 - v.shape[3])))
-
-    tiles = jnp.concatenate(
-        [wide(spread_bias), wide(spread_up), wide(spread_rows[:, :, :2].reshape(2, 8, 1, 2 * per)),
-         wide(spread_rows[:, :, 2:].reshape(2, 8, 1, 4 * per)),
-         jnp.zeros((2, 8, 3, 128), F32)],
-        axis=2,
-    ).reshape(2, 64, 128)
     back_chunks = (
         (3, 0, half),
         (3, half, half),
@@ -1494,23 +1659,33 @@
         (2, half, half),
         (1, 0, part),
         (0, 0, 3 * part),
-        (4, 0, 128),
-    )
-    out_rows, token_rows, finals = reduce_all(
-        result.astype(BF), token_grad.astype(BF), (*grads, tiles), back_chunks
-    )
-    tile = finals[4]
+    )
+    out_rows, token_rows, tile_own, tile_mate, finals = back_reduce(
+        result.astype(BF),
+        residual_one,
+        x,
+        g_qkv,
+        (queries, key_heads, value_heads, context, context_grad),
+        totals,
+        limit,
+        grads,
+        tile,
+        back_chunks,
+    )
+    plane_rows = jnp.where(c == t // 2, tile_own, tile_mate)[:6].reshape(3, 2, hidden)
+    plane_rows = lax.dynamic_index_in_dim(plane_rows, t % 2, 1, False)
+    mine_rows = lax.dynamic_slice(tile_own, (6, (4 * d + t) * per), (6, per))
     return (
         out_rows,
         token_rows.astype(F32),
         finals[0].reshape(w_qkv.shape),
-        tile[0:2, :per],
+        lax.dynamic_slice(plane_rows, (0, d * per), (2, per)),
         finals[1].T,
         finals[2],
-        tile[2, : bias_up.shape[0]],
+        lax.dynamic_slice(plane_rows, (2, d * bias_up.shape[0]), (1, bias_up.shape[0]))[0],
         finals[3].T,
-        tile[3, : 2 * per].reshape(2, per),
-        tile[4, : 4 * per].reshape(4, per),
+        mine_rows[:2],
+        mine_rows[2:],
     )
 
 

time: 378 us -> 324 us (0.86)
  Pallas kernels: 237 us -> 210 us
  matrix products: 60.4 us -> 49.6 us
  other arithmetic: 41.2 us -> 34.1 us
  local copies, waits for them, and re-layouts: 28.9 us -> 23.3 us
    pallas_call x2 -> x1, Pallas kernels: 123 us -> 100 us  [back_reduce(): pl.pallas_call(kernel, out_shape=[back, back, tiles, tiles, *[jax.ShapeDt...]
    dot_general x8 -> x6, matrix products: 16.1 us -> 7.25 us  [outer(): return jnp.einsum('rm,rn->mn', a, b, preferred_element_type=F32).astype(BF)]
    dot_general x2, matrix products: 18.6 us -> 23.7 us  [chip_local(): jnp.dot(normed_low, g_up[z], preferred_element_type=F32) + up_bias[z]]
    slice x17 -> x2, local copies, waits for them, and re-layouts: 6.05 us -> 1.15 us  [the longest x1 0.58 us: chip_local(): mine_rows[2:]]
    dot_general x2, matrix products: 8.8 us -> 4.43 us  [chip_local(): active_grad = jnp.dot(feed_grad, g_down[z], preferred_element_type=F32)]
    dot_general x2 -> x0, matrix products: 4.01 us -> none  [chip_local(): jnp.einsum('re,de->rd', mixed_low[z], g_qkv[z], preferred_element_type=F32)]
    pallas_call x4 -> x3, Pallas kernels: 19.4 us -> 15.6 us  [pair_swap(): pl.pallas_call(kernel, out_shape=jax.ShapeDtypeStruct(part.shape, part.dt...]
    unnamed x76 -> x57, local copies, waits for them, and re-layouts: 13.3 us -> 12.4 us
where the time goes in v3:
time: 324 us; the launch traced here: 319 us
  Pallas kernels  210 us (65%)
  matrix products  49.6 us (15%)
  other arithmetic  34.1 us (11%)
  local copies, waits for them, and re-layouts  23.3 us (7%)
    pallas_call x1, Pallas kernels, back_reduce(): pl.pallas_call(kernel, out_shape=[back, back, tiles, tiles, *[jax.ShapeDt...  100 us
    pallas_call x1, Pallas kernels, gather_attend(): pl.pallas_call(kernel, out_shape=[rows_shape, rows_shape, *full_shapes, f...  94.7 us
    dot_general x2, matrix products, chip_local(): jnp.dot(normed_low, g_up[z], preferred_element_type=F32) + up_bias[z]  23.7 us
    pallas_call x3, Pallas kernels, pair_swap(): pl.pallas_call(kernel, out_shape=jax.ShapeDtypeStruct(part.shape, part.dt...  15.6 us
    unnamed x57, local copies, waits for them, and re-layouts  12.4 us
    reduce_sum x2, other arithmetic, norm_backward(): jnp.sum(incoming * normal, axis=0)  9.7 us
    dot_general x6, matrix products, outer(): return jnp.einsum('rm,rn->mn', a, b, preferred_element_type=F32).astype(BF)  7.25 us

profile of v3, /device:TPU:0, one launch (start us, length us, event | category | flops | bytes accessed | tf_op | source)
XLA Modules:
  0.0 319.0 jit_solution(10131156265469231125)
XLA Ops:
  4.8 1.1 copy.47
  5.9 0.8 copy.49.refs_2_
  6.7 1.5 copy.48
  8.2 94.7 %shard_map.186 = (bf16[8,128,768]{2,1,0:T(8,128)(2,1)}, bf16[8,128,768]{2,1,0:T(8,128)(2,1)}, bf16[2,768,576]{2,1,0:T(8,128)(2,1)}, bf16[2,768,192]{2,1,0:T(8,12...) custom-call(bf16[2,256,768]{2,1,0:T(8,128)(2,1)} %refs_0_.1, ...), custom_call_target="tpu_custom_call" | custom-call | tf_op jit(solution)/shard_map/pallas_call | solution.py:802
  102.9 1.1 broadcast_select_fusion.1
  104.3 1.8 fusion.55
  106.1 1.8 add_convert_fusion.5.src
  107.9 8.0 %shard_map.187 = bf16[1024,768]{1,0:T(8,128)(2,1)} custom-call(bf16[1024,768]{1,0:T(8,128)(2,1)} %add_convert_fusion.5.src), custom_call_target="tpu_custom_call" | custom-call | tf_op jit(solution)/shard_map/pallas_call | solution.py:415
  115.8 3.1 fusion.73
  119.7 1.7 fusion.19
  121.4 0.8 slice_convert_fusion
  122.3 12.1 %multiply_convert_fusion = (bf16[1024,768]{1,0:T(8,128)(2,1)}, f32[1024,768]{1,0:T(8,128)}, f32[1024,768]{1,0:T(8,128)}) fusion(f32[768]{0:T(1024)S(1)} %add.167, bf16[1024,768]{1,0:T(8,128)(2,1)} %fusion.19, bf16[2,768,768]{2,1,0:T(8,128)(2,1)} %get-tuple-element.37), kind=kOutput, calls=%fused_computation.30 | convolution fusion | flops 1259864064 | bytes 10619904 | tf_op jit(solution)/shard_map/dot_general | solution.py:1594
  134.4 11.5 %multiply_convert_fusion.1 = (bf16[1024,768]{1,0:T(8,128)(2,1)S(1)}, f32[1024,768]{1,0:T(8,128)}, f32[1024,768]{1,0:T(8,128)}) fusion(f32[768]{0:T(1024)S(1)} %add.164, bf16[1024,768]{1,0:T(8,128)(2,1)} %fusion.19, bf16[2,768,768]{2,1,0:T(8,128)(2,1)} %get-tuple-element.37), kind=kOutput, calls=%fused_computation.43 | convolution fusion | flops 1259864064 | bytes 10619904 | tf_op jit(solution)/shard_map/dot_general | solution.py:1594
  146.0 1.1 copy-done.19
  147.1 1.4 fusion.36
  148.6 2.6 add_convert_fusion.4.src
  151.2 3.8 %shard_map.188 = bf16[1024,768]{1,0:T(8,128)(2,1)} custom-call(bf16[1024,768]{1,0:T(8,128)(2,1)} %add_convert_fusion.4.src), custom_call_target="tpu_custom_call" | custom-call | tf_op jit(solution)/shard_map/pallas_call | solution.py:415
  155.1 3.1 fusion.70
  158.2 1.7 copy-done
  160.6 3.7 %fusion.8 = (f32[768]{0:T(1024)S(1)}, f32[1024]{0:T(1024)S(1)}) fusion(bf16[8,128,768]{2,1,0:T(8,128)(2,1)} %get-tuple-element.39, f32[1024,768]{1,0:T(8,128)} %copy-done, f32[1024]{0:T(1024)S(1)} %add_rsqrt_fusion, f32[1024]{0:T(1024)S(1)} %broadcast_multiply_fusion.3, f32[768]{0:T(1024)S(1)} %mul.181), kind=kLoop, calls=%fused_computation.14 | loop fusion | flops 6289664 | bytes 4737024 | tf_op jit(solution)/shard_map/reduce_sum | solution.py:29
  165.0 1.4 convert_reduce_fusion.1
  166.4 1.5 fusion.22
  167.9 1.5 fusion.23
  169.8 0.9 copy-done.23
  170.7 2.2 convert_reduce_fusion.4
  173.0 1.5 fusion.20
  174.8 1.0 copy-done.22
  175.8 2.2 convert_reduce_fusion.3
  178.0 1.5 fusion.21
  179.5 2.4 pad_maximum_fusion
  182.3 1.4 fusion.40
  183.7 2.6 add_convert_fusion.src
  186.3 3.8 %shard_map.189 = bf16[1024,768]{1,0:T(8,128)(2,1)} custom-call(bf16[1024,768]{1,0:T(8,128)(2,1)} %add_convert_fusion.src), custom_call_target="tpu_custom_call" | custom-call | tf_op jit(solution)/shard_map/pallas_call | solution.py:415
  190.2 6.0 %multiply_reduce_fusion = (f32[768]{0:T(1024)S(1)}, f32[1024]{0:T(1024)S(1)}, f32[1024]{0:T(1024)S(1)}, f32[768]{0:T(1024)S(1)}, f32[1024,768]{1,0:T(8,128)S(1)}, /*index=5*/bf16[1024,768]{1,0:T(8,128)(2,1)}) fusion(f32[1024,768]{1,0:T(8,128)S(1)} %get-tuple-element.107, f32[1024]{0:T(1024)S(1)} %add_rsqrt_fusion.1, f32[1024]{0:T(1024)S(1)} %broadcast_multiply_fusion.4, ...), kind=kLoop, calls=%fused_computation.17 | loop fusion | flops 18870784 | bytes 15776768 | tf_op jit(solution)/shard_map/reduce_sum | solution.py:29
  196.2 2.7 convert_reduce_fusion.2
  199.6 0.8 fusion.25
  200.4 1.0 pad_maximum_fusion.3.refs_12_
  201.5 1.3 concatenate.34.refs_11_
  202.8 2.1 convolution_convert_fusion.7
  206.0 1.2 pad_maximum_fusion.2.refs_8_
  207.2 100.1 %shard_map.190 = (bf16[2,256,768]{2,1,0:T(8,128)(2,1)}, bf16[2,256,768]{2,1,0:T(8,128)(2,1)}, f32[16,768]{1,0:T(8,128)}, f32[16,768]{1,0:T(8,128)}, f32[96,576]{...) custom-call(bf16[1024,768]{1,0:T(8,128)(2,1)} %get-tuple-element.108.refs_0_, ...), custom_call_target="tpu_custom_call" | custom-call | tf_op jit(solution)/shard_map/pallas_call | solution.py:1371
  307.3 0.9 slice_select_fusion
  309.4 2.4 convert_element_type.154
  311.8 1.1 copy.60
  312.9 0.9 copy.61
  313.8 0.7 copy.62
  314.5 0.8 constant_dynamic-slice_fusion
  316.5 0.9 copy.74
  (95 shorter events, 13.4 us)
Async XLA Ops:
  102.9 3.1 copy-start.5
  102.9 3.1 copy-start.7
  134.4 12.7 %copy-start.15 = (bf16[2,768,768]{2,1,0:T(8,128)(2,1)S(1)}, bf16[2,768,768]{2,1,0:T(8,128)(2,1)}, u32[]{:S(2)}) copy-start(bf16[2,768,768]{2,1,0:T(8,128)(2,1)} %get-tuple-element.38) | copy-start | bytes 7077892
  146.0 1.1 copy-start.19
  147.1 1.4 copy-start.17
  158.2 1.7 copy-start
  160.5 3.7 %copy-start.2 = (bf16[8,128,768]{2,1,0:T(8,128)(2,1)S(1)}, bf16[8,128,768]{2,1,0:T(8,128)(2,1)}, u32[]{:S(2)}) copy-start(bf16[8,128,768]{2,1,0:T(8,128)(2,1)} %get-tuple-element.39) | copy-start | bytes 4718596
  160.5 4.4 %copy-start.1 = (f32[1024,768]{1,0:T(8,128)S(1)}, f32[1024,768]{1,0:T(8,128)}, u32[]{:S(2)}) copy-start(f32[1024,768]{1,0:T(8,128)} %copy-done) | copy-start | bytes 9437188
  165.0 1.4 copy-start.20
  166.4 1.5 copy-start.18
  166.4 3.0 copy-start.24
  167.9 1.9 copy-start.16
  167.9 2.8 copy-start.23
  170.7 2.2 copy-start.9
  172.9 1.9 copy-start.21
  173.0 2.8 copy-start.22
  179.5 2.8 copy-start.14
  196.2 2.7 copy-start.6
  198.9 1.5 copy-start.3
  199.6 3.2 %copy-start.8 = (bf16[2,768,192]{2,1,0:T(8,128)(2,1)S(1)}, bf16[2,768,192]{2,1,0:T(8,128)(2,1)}, u32[]{:S(2)}) copy-start(bf16[2,768,192]{2,1,0:T(8,128)(2,1)} %get-tuple-element.34) | copy-start | bytes 1769476
  201.4 3.7 %copy-start.4 = (bf16[1024,768]{1,0:T(8,128)(2,1)S(1)}, bf16[1024,768]{1,0:T(8,128)(2,1)}, u32[]{:S(2)}) copy-start(bf16[1024,768]{1,0:T(8,128)(2,1)} %copy-done.3) | copy-start | bytes 4718596
  307.2 6.6 %copy-start.13 = (f32[96,192]{1,0:T(8,128)S(1)}, f32[96,192]{1,0:T(8,128)}, u32[]{:S(2)}) copy-start(f32[96,192]{1,0:T(8,128)} %get-tuple-element.51) | copy-start | bytes 221188
  307.2 9.2 %copy-start.10 = (bf16[2,256,768]{2,1,0:T(8,128)(2,1)S(1)}, bf16[2,256,768]{2,1,0:T(8,128)(2,1)}, u32[]{:S(2)}) copy-start(bf16[2,256,768]{2,1,0:T(8,128)(2,1)} %get-tuple-element.139) | copy-start | bytes 2359300
  307.3 10.1 %copy-start.12 = (f32[96,768]{1,0:T(8,128)S(1)}, f32[96,768]{1,0:T(8,128)}, u32[]{:S(2)}) copy-start(f32[96,768]{1,0:T(8,128)} %get-tuple-element.144) | copy-start | bytes 884740
  307.3 10.8 %copy-start.11 = (f32[96,768]{1,0:T(8,128)S(1)}, f32[96,768]{1,0:T(8,128)}, u32[]{:S(2)}) copy-start(f32[96,768]{1,0:T(8,128)} %get-tuple-element.53) | copy-start | bytes 884740

commit v4 on v3

--- a/solution.py
+++ b/solution.py
@@ -1,3 +1,4 @@
+import math
 from functools import partial
 
 import jax
@@ -386,47 +387,6 @@
         greet(2 * k, other)
         greet(2 * k + 1, other)
     pl.semaphore_wait(barrier, 9)
-
-
-def pair_swap(part):
-    def kernel(src, dst, send, recv):
-        d, t, k, c, xb, yb, dx, dy = place()
-        mate = d + 1 - 2 * c
-        barrier = pltpu.get_barrier_semaphore()
-        pl.semaphore_signal(barrier, inc=1, device_id=(mate, t), device_id_type=MESH_ID)
-        pl.semaphore_wait(barrier, 1)
-        rows = src.shape[0] // 4
-        copies = [
-            remote(
-                src.at[pl.ds(i * rows, rows)],
-                dst.at[pl.ds(i * rows, rows)],
-                send.at[i],
-                recv.at[i],
-                mate,
-                t,
-            )
-            for i in range(4)
-        ]
-        for copy in copies:
-            copy.start()
-        for copy in copies:
-            copy.wait()
-
-    return pl.pallas_call(
-        kernel,
-        out_shape=jax.ShapeDtypeStruct(part.shape, part.dtype),
-        in_specs=[pl.BlockSpec(memory_space=pl.ANY)],
-        out_specs=pl.BlockSpec(memory_space=pl.ANY),
-        scratch_shapes=[pltpu.SemaphoreType.DMA((4,)), pltpu.SemaphoreType.DMA((4,))],
-        compiler_params=pltpu.CompilerParams(collective_id=3, has_side_effects=True),
-    )(part)
-
-
-def skewed(chunks, levels):
-    for slot in range(chunks + len(levels) - 1):
-        for level in reversed(range(len(levels))):
-            if 0 <= slot - level < chunks:
-                levels[level](slot - level)
 
 
 def gather_attend(tokens, cotangent, shards, chunks, per):
@@ -850,10 +810,26 @@
     )
 
 
-def back_reduce(output, residual, x, weight, heads, totals, limit, ready, tile, chunks):
-    part_cols = weight.shape[2] // 3
+def gelu_parts(u):
+    half = math.sqrt(0.5)
+    e = jnp.exp(u * u * -0.5)
+    f = 1.0 / (1.0 + (0.3275911 * half) * jnp.abs(u))
+    series = 0.5 * 1.061405429 * f - 0.5 * 1.453152027
+    series = series * f + 0.5 * 1.421413741
+    series = series * f - 0.5 * 0.284496736
+    series = series * f + 0.5 * 0.254829592
+    tail = series * f * e
+    share = jnp.where(u >= 0.0, 1.0 - tail, tail)
+    return u * share, share + u * e * (1.0 / math.sqrt(2.0 * math.pi))
+
+
+def layer_back(x, cot, weights, heads, totals, limit, small_own, small_other, per, chunks):
+    part_cols = weights[0].shape[2] // 3
     heads_width = 2 * part_cols
-    grads = [jax.ShapeDtypeStruct(weight.shape, BF), *ready]
+    hidden = weights[2].shape[2]
+    up_per = hidden // 8
+    grads = weights
+    output = x
     count = len(grads)
     n_chunks = len(chunks)
     length, width = output.shape
@@ -862,10 +838,12 @@
     rows_of = [g.shape[1] // 8 for g in grads]
 
     def kernel(*refs):
-        res, residual_hbm, x_hbm, weight_hbm = refs[:4]
-        q_ref, k_ref, v_ref, o_ref, do_ref, lt_ref, limit_ref, tile_ref = refs[4:12]
-        others = refs[12 : 11 + count]
-        base = 11 + count
+        x_hbm, cot_hbm = refs[:2]
+        held = refs[2 : 2 + count]
+        q_ref, k_ref, v_ref, o_ref, lt_ref, limit_ref, small_a, small_b = refs[
+            2 + count : 10 + count
+        ]
+        base = 10 + count
         res_out, tgr_out, tile_own, tile_mate = refs[base : base + 4]
         final = refs[base + 4 : base + 4 + count]
         base += 4 + count
@@ -878,7 +856,6 @@
         got4 = refs[base + 6 * count : base + 7 * count]
         got5 = refs[base + 7 * count : base + 8 * count]
         (
-            row_stage,
             row_sem,
             ex_send,
             ex_recv,
@@ -892,22 +869,34 @@
             y_recv,
             p_send,
             p_recv,
-            grad_own,
+            wq,
+            wo,
+            wu,
+            wd,
             x_rows,
-            weight_rows,
+            cot_rows,
+            small_rows,
+            row_values,
+            out_both,
+            n1_rows,
+            inv_rows,
             residual_rows,
+            res_rows,
+            low_rows,
+            feed_rows,
+            branch_rows,
+            sent,
+            got,
+            active,
+            upper,
+            do_ref,
             dots,
             acc,
             acc_rows,
-            dq,
-            dk,
-            dv,
-            mixed,
-            mate_part,
             mate_got,
-            own_part,
-            row_out,
             load_sem,
+            e_send,
+            e_recv,
             s_send,
             s_recv,
             t_send,
@@ -915,7 +904,13 @@
             tile_sum,
             tile_got,
         ) = refs[base + 8 * count :]
-        part = (grad_own, *others)
+        part = (wq, wo, wu, wd)
+        mixed = active
+        dq, dk, dv = (
+            upper.at[0, :, pl.ds(0, heads_width)],
+            upper.at[0, :, pl.ds(heads_width, heads_width)],
+            upper.at[1, :, pl.ds(0, heads_width)],
+        )
         d, t, k, c, xb, yb, dx, dy = place()
         mate = d + 1 - 2 * c
         u = t + c * (3 - 2 * t)
@@ -923,54 +918,6 @@
         down = t - 1 + 2 * c
         source = u <= 1
         enter(k, c, t, d, dx, dy)
-
-        def return_rows(which, src, dst, start):
-            for goal in range(4):
-                piece = src.at[pl.ds((goal * 2 + c) * half, half)]
-                spot = dst.at[t % 2, pl.ds(c * half, half)]
-                here = jnp.logical_and(goal == t, c == t // 2)
-                copy = remote(
-                    piece,
-                    spot,
-                    ex_send.at[which, goal],
-                    ex_recv.at[which, t % 2, c],
-                    2 * k + t // 2,
-                    goal,
-                )
-
-                @pl.when(here)
-                def _():
-                    if start:
-                        load = pltpu.make_async_copy(piece, row_stage, row_sem)
-                        load.start()
-                        load.wait()
-                        store = pltpu.make_async_copy(row_stage, spot, row_sem)
-                        store.start()
-                        store.wait()
-
-                @pl.when(jnp.logical_not(here))
-                def _():
-                    if start:
-                        copy.start()
-                    else:
-                        copy.wait_send()
-
-            if not start:
-                for m in range(2):
-                    for core in range(2):
-                        spot = dst.at[m, pl.ds(core * half, half)]
-                        here = jnp.logical_and(2 * c + m == t, core == c)
-
-                        @pl.when(jnp.logical_not(here))
-                        def _():
-                            remote(
-                                spot,
-                                spot,
-                                ex_send.at[which, 0],
-                                ex_recv.at[which, m, core],
-                                mate,
-                                t,
-                            ).wait_recv()
 
         def plane(b):
             return b + c * (1 - 2 * b)
@@ -1156,10 +1103,181 @@
                 final[s][:, spot] = got5[s][:, spot].astype(F32)
 
         loads = [
-            pltpu.make_async_copy(x_hbm, x_rows, load_sem.at[0]),
-            pltpu.make_async_copy(weight_hbm, weight_rows, load_sem.at[1]),
-            pltpu.make_async_copy(residual_hbm, residual_rows, load_sem.at[2]),
+            pltpu.make_async_copy(src, dst, load_sem.at[i])
+            for i, (src, dst) in enumerate(
+                (
+                    (held[1], wo),
+                    (x_hbm, x_rows),
+                    (held[2], wu),
+                    (held[3], wd),
+                    (cot_hbm, cot_rows),
+                    (held[0], wq),
+                )
+            )
         ]
+
+        def widen(rows, size, spot):
+            n, wide = rows.shape[0], row_values.shape[1]
+            at = lax.broadcasted_iota(jnp.int32, (128, wide), 0)
+            lane = lax.broadcasted_iota(jnp.int32, (128, wide), 1)
+            v = jnp.dot(
+                rows,
+                (at == lane % size).astype(F32),
+                precision=lax.Precision.HIGHEST,
+                preferred_element_type=F32,
+            )
+            row = lax.broadcasted_iota(jnp.int32, (n, wide), 0)
+            lane = lax.broadcasted_iota(jnp.int32, (n, wide), 1)
+            return jnp.sum(jnp.where(lane // size == spot(row), v, 0.0), axis=0, keepdims=True)
+
+        def unpack():
+            for z in range(2):
+                small_rows[pl.ds((2 * c + z) * 8 * SMALL, 8 * SMALL), :] = small_a[z].astype(F32)
+                small_rows[pl.ds((2 - 2 * c + z) * 8 * SMALL, 8 * SMALL), :] = small_b[z].astype(F32)
+            for kind in range(6):
+                rows = small_rows[pl.ds(3 + kind, 32, stride=SMALL), :]
+                row_values[kind : kind + 1, :] = widen(
+                    rows, per, lambda row: (row % 8) * 4 + row // 8
+                )
+            for z in range(2):
+                rows = small_rows[pl.ds((2 * c + z) * 8 * SMALL + 2, 8, stride=SMALL), :]
+                row_values[6 + z : 7 + z, :] = widen(rows, up_per, lambda row: row)
+
+        def value_row(i):
+            return row_values[i : i + 1, :]
+
+        def swap_copy(which, i):
+            rows = pl.ds(i * BLOCK, BLOCK)
+            return remote(
+                sent.at[rows],
+                got.at[which, rows],
+                e_send.at[which, i],
+                e_recv.at[which, i],
+                mate,
+                t,
+            )
+
+        def swapped(which, i):
+            rows = pl.ds(i * BLOCK, BLOCK)
+            swap_copy(which, i).wait()
+            return sent[rows, :].astype(F32) + got[which, rows, :].astype(F32)
+
+        def swap(which, i, share):
+            sent[pl.ds(i * BLOCK, BLOCK), :] = share.astype(BF)
+            swap_copy(which, i).start()
+
+        def normalize(v):
+            center = v - jnp.mean(v, axis=1, keepdims=True)
+            inverse = lax.rsqrt(jnp.mean(center * center, axis=1, keepdims=True) + EPSILON)
+            return center * inverse, inverse
+
+        def norm_pull(scaled, normal, inverse):
+            first = jnp.mean(scaled, axis=1, keepdims=True)
+            second = jnp.mean(scaled * normal, axis=1, keepdims=True)
+            return inverse * (scaled - first - normal * second)
+
+        def tally(row, v):
+            tile_sum[0, row : row + 1, :] += jnp.sum(v, axis=0, keepdims=True)
+
+        def branch_block(i):
+            swap(0, i, dot_nt(o_ref[pl.ds(i * BLOCK, BLOCK), :], out_both[...]))
+
+        def forward_block(i):
+            rows = pl.ds(i * BLOCK, BLOCK)
+            branch = swapped(0, i) + value_row(2)
+            normal, inverse = normalize(x_rows[rows, :].astype(F32) + branch)
+            n1_rows[rows, :] = normal
+            inv_rows[rows, :] = jnp.broadcast_to(inverse, (BLOCK, 128))
+            low_rows[rows, :] = (normal * value_row(0) + value_row(3)).astype(BF)
+            for z in range(2):
+                for col in range(0, hidden, BLOCK):
+                    cols = pl.ds(col, BLOCK)
+                    u = jnp.dot(low_rows[rows, :], wu[z, :, cols], preferred_element_type=F32)
+                    value, slope = gelu_parts(u + row_values[6 + z : 7 + z, cols])
+                    active[z, rows, cols] = value.astype(BF)
+                    upper[z, rows, cols] = slope.astype(BF)
+            swap(1, i, dot_nt(active[0, rows, :], wd[0]) + dot_nt(active[1, rows, :], wd[1]))
+
+        def row_home(i):
+            return jnp.logical_and(i == t, c == t // 2)
+
+        def out_copy(i):
+            return remote(
+                res_rows.at[pl.ds((2 * i + c) * half, half)],
+                res_out.at[t % 2, pl.ds(c * half, half)],
+                ex_send.at[0, i],
+                ex_recv.at[0, t % 2, c],
+                2 * k + t // 2,
+                i,
+            )
+
+        def output_block(i):
+            rows = pl.ds(i * BLOCK, BLOCK)
+            feed_out = swapped(1, i) + value_row(4)
+            normed = n1_rows[rows, :] * value_row(0) + value_row(3)
+            normal, inverse = normalize(normed + feed_out)
+            res_rows[rows, :] = (normal * value_row(1) + value_row(5)).astype(BF)
+            incoming = cot_rows[rows, :].astype(F32)
+            tally(7, incoming * normal)
+            tally(11, incoming)
+            residual = norm_pull(incoming * value_row(1), normal, inverse)
+            residual_rows[rows, :] = residual
+            feed = residual.astype(BF)
+            feed_rows[rows, :] = feed
+            tally(10, feed.astype(F32))
+            for z in range(2):
+                for col in range(0, hidden, BLOCK):
+                    cols = pl.ds(col, BLOCK)
+                    pull = jnp.dot(feed_rows[rows, :], wd[z, :, cols], preferred_element_type=F32)
+                    grad = (pull * upper[z, rows, cols].astype(F32)).astype(BF)
+                    upper[z, rows, cols] = grad
+                    tile_sum[0, 4 + z : 5 + z, cols] += jnp.sum(
+                        grad.astype(F32), axis=0, keepdims=True
+                    )
+            swap(2, i, dot_nt(upper[0, rows, :], wu[0]) + dot_nt(upper[1, rows, :], wu[1]))
+
+            @pl.when(row_home(i))
+            def _():
+                store = pltpu.make_async_copy(
+                    res_rows.at[pl.ds((2 * i + c) * half, half)],
+                    res_out.at[t % 2, pl.ds(c * half, half)],
+                    row_sem,
+                )
+                store.start()
+                store.wait()
+
+            @pl.when(jnp.logical_not(row_home(i)))
+            def _():
+                out_copy(i).start()
+
+        def branch_back_block(i):
+            rows = pl.ds(i * BLOCK, BLOCK)
+            grad = residual_rows[rows, :] + swapped(2, i)
+            normal = n1_rows[rows, :]
+            tally(6, grad * normal)
+            tally(9, grad)
+            residual = norm_pull(grad * value_row(0), normal, inv_rows[rows, 0:1])
+            residual_rows[rows, :] = residual
+            low_grad = residual.astype(BF)
+            branch_rows[rows, :] = low_grad
+            tally(8, low_grad.astype(F32))
+            do_ref[rows, :] = jnp.dot(
+                branch_rows[rows, :], out_both[...], preferred_element_type=F32
+            ).astype(BF)
+
+        def outer(left, j, right):
+            return dot_tn(left[:, pl.ds(j * BLOCK, BLOCK)], right).astype(BF)
+
+        def down_grad(z, j):
+            wd[z, pl.ds(j * BLOCK, BLOCK), :] = outer(feed_rows, j, active[z])
+
+        def up_grad(z, j):
+            wu[z, pl.ds(j * BLOCK, BLOCK), :] = outer(low_rows, j, upper[z])
+
+        def out_grad(j):
+            both = outer(branch_rows, j, o_ref[...])
+            for z in range(2):
+                wo[z, pl.ds(j * BLOCK, BLOCK), :] = both[:, z * part_cols : (z + 1) * part_cols]
 
         def attention(pair, kb):
             if kb == 0:
@@ -1171,7 +1289,14 @@
                 dq[:, pl.ds(pair * 128, 128)] = (acc[...] * DH**-0.5).astype(BF)
 
         def mate_copy(i):
-            return remote(mate_part.at[i], mate_got.at[i], t_send.at[0, i], t_recv.at[0, i], mate, t)
+            return remote(
+                sent.at[pl.ds(i * half, half)],
+                mate_got.at[i],
+                t_send.at[0, i],
+                t_recv.at[0, i],
+                mate,
+                t,
+            )
 
         def mix(i):
             rows = pl.ds(i * BLOCK, BLOCK)
@@ -1181,19 +1306,16 @@
                 both = jnp.concatenate(
                     [v[:, z * part_cols : (z + 1) * part_cols] for v in kinds], axis=1
                 )
-                mixed[z, rows, :] = both
-                share = share + dot_nt(both, weight_rows[z])
+                mixed[z, rows, 0 : 3 * part_cols] = both
+                share = share + dot_nt(both, wq[z])
             acc_rows[...] = share
-            mate_part[i] = acc_rows[pl.ds((1 - c) * half, half), :].astype(BF)
-            own_part[i] = (
-                acc_rows[pl.ds(c * half, half), :]
-                + residual_rows[pl.ds((2 * i + c) * half, half), :]
-            )
+            sent[pl.ds(i * half, half), :] = acc_rows[pl.ds((1 - c) * half, half), :].astype(BF)
+            residual_rows[pl.ds((2 * i + c) * half, half), :] += acc_rows[pl.ds(c * half, half), :]
             mate_copy(i).start()
 
         def row_copy(i):
             return remote(
-                row_out.at[i],
+                low_rows.at[pl.ds(i * half, half)],
                 tgr_out.at[t % 2, pl.ds(c * half, half)],
                 t_send.at[1, i],
                 t_recv.at[1, 2 * (t % 2) + c],
@@ -1203,13 +1325,15 @@
 
         def send_rows(i):
             mate_copy(i).wait_recv()
-            row_out[i] = (own_part[i] + mate_got[i].astype(F32)).astype(BF)
-            here = jnp.logical_and(i == t, c == t // 2)
+            low_rows[pl.ds(i * half, half), :] = (
+                residual_rows[pl.ds((2 * i + c) * half, half), :] + mate_got[i].astype(F32)
+            ).astype(BF)
+            here = row_home(i)
 
             @pl.when(here)
             def _():
                 store = pltpu.make_async_copy(
-                    row_out.at[i], tgr_out.at[t % 2, pl.ds(c * half, half)], row_sem
+                    low_rows.at[pl.ds(i * half, half)], tgr_out.at[t % 2, pl.ds(c * half, half)], row_sem
                 )
                 store.start()
                 store.wait()
@@ -1233,7 +1357,7 @@
                     @pl.when(jnp.logical_not(jnp.logical_and(2 * c + m == t, core == c)))
                     def _():
                         remote(
-                            row_out.at[0],
+                            low_rows.at[pl.ds(0, half)],
                             spot,
                             t_send.at[1, 0],
                             t_recv.at[1, 2 * m + core],
@@ -1244,7 +1368,7 @@
         def weight_grad(j):
             rows = pl.ds(j * BLOCK, BLOCK)
             for z in range(2):
-                grad_own[z, rows, :] = dot_tn(x_rows[:, rows], mixed[z]).astype(BF)
+                wq[z, rows, :] = outer(x_rows, j, mixed[z, :, 0 : 3 * part_cols])
 
         def tile_copy(stage, goal_dp, goal_t, slot):
             return remote(
@@ -1257,7 +1381,6 @@
             )
 
         def tile_start():
-            tile_sum[0] = tile_ref[...]
             for row, ref in ((0, dq), (2, dv)):
                 sums = jnp.sum(ref[...].astype(F32), axis=0, keepdims=True)
                 for z in range(2):
@@ -1291,16 +1414,33 @@
                 tile_copy(stage, mate, t, slot).wait_send()
 
         levels = [level_first, level_second, level_line, level_pass, level_near, level_mate]
-        work = [partial(attention, pair, kb) for pair in range(heads_width // 128) for kb in range(blocks)]
+        for copy in loads:
+            copy.start()
+        unpack()
+        tile_sum[0] = jnp.zeros(tile_sum.shape[1:], F32)
+        loads[0].wait()
+        out_both[...] = jnp.concatenate([wo[0], wo[1]], axis=1)
+        pl.loop(0, blocks)(branch_block)
+        for copy in loads[1:4]:
+            copy.wait()
+        pl.loop(0, blocks)(forward_block)
+        loads[4].wait()
+        pl.loop(0, blocks)(output_block)
+        loads[5].wait()
+        pl.loop(0, width // BLOCK)(lambda j: [down_grad(z, j) for z in range(2)] and None)
+        level_first(0)
+        level_first(1)
+        pl.loop(0, width // BLOCK)(lambda j: [up_grad(z, j) for z in range(2)] and None)
+        level_first(2)
+        pl.loop(0, blocks)(branch_back_block)
+        pl.loop(0, width // BLOCK)(out_grad)
+        work = [
+            partial(attention, pair, kb)
+            for pair in range(heads_width // 128)
+            for kb in range(blocks)
+        ]
         work += [partial(mix, i) for i in range(blocks)]
         work += [partial(weight_grad, j) for j in range(width // BLOCK)]
-        for copy in loads:
-            copy.start()
-        level_first(0)
-        level_first(1)
-        return_rows(0, res, res_out, True)
-        for copy in loads:
-            copy.wait()
         done = 0
         for slot in range(n_chunks + 5):
             if slot < n_chunks - 1:
@@ -1311,9 +1451,9 @@
             if slot == n_chunks - 2:
                 tile_start()
             for lag, level in enumerate(levels):
-                i = slot + 1 - lag
-                if lag == 0 and i < 2:
-                    continue
+                i = slot + (2 if lag == 0 else 1) - lag
+                if lag == 0:
+                    i = {0: 3, 1: 4, n_chunks - 2: n_chunks - 1}.get(slot, -1)
                 if 0 <= i < n_chunks:
                     level(i)
             if slot == n_chunks - 2:
@@ -1323,7 +1463,27 @@
                 tail = slot - (n_chunks - 1)
                 if tail < 4:
                     (tile_second, tile_third, tile_fourth, tile_last)[tail]()
-        return_rows(0, res, res_out, False)
+        for i in range(4):
+
+            @pl.when(jnp.logical_not(row_home(i)))
+            def _():
+                out_copy(i).wait_send()
+
+        for m in range(2):
+            for core in range(2):
+                spot = res_out.at[m, pl.ds(core * half, half)]
+
+                @pl.when(jnp.logical_not(jnp.logical_and(2 * c + m == t, core == c)))
+                def _():
+                    remote(
+                        res_rows.at[pl.ds(0, half)],
+                        spot,
+                        ex_send.at[0, 0],
+                        ex_recv.at[0, m, core],
+                        mate,
+                        t,
+                    ).wait_recv()
+
         settle_rows()
         for i in range(n_chunks):
             for copy in first_copies(i):
@@ -1367,7 +1527,7 @@
             )[kind]
             scratch.append(pltpu.VMEM(shape, dtype))
     back = jax.ShapeDtypeStruct((2, 2 * half, width), output.dtype)
-    tiles = jax.ShapeDtypeStruct(tile.shape, F32)
+    tiles = jax.ShapeDtypeStruct((16, hidden), F32)
     outs = pl.pallas_call(
         kernel,
         out_shape=[
@@ -1377,14 +1537,13 @@
             tiles,
             *[jax.ShapeDtypeStruct((r, g.shape[2]), F32) for r, g in zip(rows_of, grads)],
         ],
-        in_specs=[any_spec] * 4 + [vmem] * (7 + count),
+        in_specs=[any_spec] * (2 + count) + [vmem] * 8,
         out_specs=[any_spec, any_spec] + [vmem] * (2 + count),
         scratch_shapes=[
             *scratch,
-            pltpu.VMEM((half, width), output.dtype),
             dma,
-            dma((2, 4)),
-            dma((2, 2, 2)),
+            dma((1, 4)),
+            dma((1, 2, 2)),
             dma((n_chunks, 3)),
             dma((n_chunks, 3)),
             dma((n_chunks, 2)),
@@ -1395,33 +1554,42 @@
             dma((n_chunks,)),
             dma((n_chunks,)),
             dma((n_chunks,)),
-            pltpu.VMEM(weight.shape, BF),
+            *[pltpu.VMEM(w.shape, BF) for w in weights],
             pltpu.VMEM((length, width), BF),
-            pltpu.VMEM(weight.shape, BF),
+            pltpu.VMEM((length, width), BF),
+            pltpu.VMEM((32 * SMALL, 128), F32),
+            pltpu.VMEM((8, width), F32),
+            pltpu.VMEM((width, heads_width), BF),
             pltpu.VMEM((length, width), F32),
+            pltpu.VMEM((length, 128), F32),
+            pltpu.VMEM((length, width), F32),
+            pltpu.VMEM((length, width), BF),
+            pltpu.VMEM((length, width), BF),
+            pltpu.VMEM((length, width), BF),
+            pltpu.VMEM((length, width), BF),
+            pltpu.VMEM((length, width), BF),
+            pltpu.VMEM((3, length, width), BF),
+            pltpu.VMEM((2, length, hidden), BF),
+            pltpu.VMEM((2, length, hidden), BF),
+            pltpu.VMEM((length, heads_width), BF),
             pltpu.VMEM((8, length), F32),
             pltpu.VMEM((length, 128), F32),
             pltpu.VMEM((BLOCK, width), F32),
-            pltpu.VMEM((length, heads_width), BF),
-            pltpu.VMEM((length, heads_width), BF),
-            pltpu.VMEM((length, heads_width), BF),
-            pltpu.VMEM((2, length, 3 * part_cols), BF),
             pltpu.VMEM((4, half, width), BF),
-            pltpu.VMEM((4, half, width), BF),
-            pltpu.VMEM((4, half, width), F32),
-            pltpu.VMEM((4, half, width), BF),
-            dma((3,)),
+            dma((6,)),
+            dma((3, blocks)),
+            dma((3, blocks)),
             dma((6,)),
             dma((6,)),
             dma((2, 4)),
             dma((2, 4)),
-            pltpu.VMEM((4, *tile.shape), F32),
-            pltpu.VMEM((6, *tile.shape), F32),
+            pltpu.VMEM((4, *tiles.shape), F32),
+            pltpu.VMEM((6, *tiles.shape), F32),
         ],
         compiler_params=pltpu.CompilerParams(
-            collective_id=2, has_side_effects=True, vmem_limit_bytes=62 * 1024 * 1024
+            collective_id=2, has_side_effects=True, vmem_limit_bytes=67043328
         ),
-    )(output, residual, x, weight, *heads, totals, limit, tile, *ready)
+    )(x, cot, *weights, *heads, totals, limit, small_own, small_other)
     return outs[0], outs[1], outs[2], outs[3], outs[4:]
 
 
@@ -1533,8 +1701,6 @@
     tokens, prefix_len, w_qkv, bias_qv, w_out, w_up, bias_up, w_down, gains, shifts, cotangent
 ):
     d, t, k, c, _, _, _, _ = place()
-    model_width = tokens.shape[2]
-    length = tokens.shape[1] * 4
     part = w_qkv.shape[2]
     hidden = w_up.shape[1]
 
@@ -1568,90 +1734,7 @@
     )
     queries, key_heads, value_heads, context, totals, limit = heads
 
-    mine = g_small.reshape(2, 8, SMALL, 128)
-    theirs = small_other.reshape(2, 8, SMALL, 128)
-    first = jnp.where(c == 0, mine, theirs)
-    every = jnp.concatenate([first, jnp.where(c == 0, theirs, mine)], axis=0)
     per = bias_qv.shape[1]
-    up_bias = mine[:, :, 2, : bias_up.shape[0]].astype(F32).reshape(2, hidden)
-    rows = every[:, :, 3:9, :per].astype(F32).transpose(2, 1, 0, 3).reshape(6, model_width)
-    full_gains, full_shifts = rows[:2], rows[2:]
-
-    branch_part = sum(
-        jnp.einsum(
-            "rk,dk->rd", context[:, z * part : (z + 1) * part], g_out[z], preferred_element_type=F32
-        )
-        for z in range(2)
-    ).astype(BF)
-    branch = (
-        branch_part.astype(F32) + pair_swap(branch_part).astype(F32) + full_shifts[0]
-    )
-    normed, normal_one, inverse_one = norm_forward(
-        x.astype(F32) + branch, full_gains[0], full_shifts[1]
-    )
-    normed_low = normed.astype(BF)
-    pre = [
-        jnp.dot(normed_low, g_up[z], preferred_element_type=F32) + up_bias[z] for z in range(2)
-    ]
-    active = [jax.nn.gelu(v, approximate=False).astype(BF) for v in pre]
-    feed_part = sum(
-        jnp.einsum("rf,df->rd", active[z], g_down[z], preferred_element_type=F32)
-        for z in range(2)
-    ).astype(BF)
-    feed_out = feed_part.astype(F32) + pair_swap(feed_part).astype(F32) + full_shifts[2]
-    result, normal_two, inverse_two = norm_forward(
-        normed + feed_out, full_gains[1], full_shifts[3]
-    )
-    incoming = cot.astype(F32)
-    residual_two, gain_two, shift_two = norm_backward(
-        incoming, normal_two, inverse_two, full_gains[1]
-    )
-    feed_grad = residual_two.astype(BF)
-    upper = []
-    for z in range(2):
-        active_grad = jnp.dot(feed_grad, g_down[z], preferred_element_type=F32)
-        _, pull = jax.vjp(partial(jax.nn.gelu, approximate=False), pre[z])
-        upper.append(pull(active_grad)[0].astype(BF))
-    normed_part = sum(
-        jnp.einsum("rf,df->rd", upper[z], g_up[z], preferred_element_type=F32) for z in range(2)
-    ).astype(BF)
-    normed_grad = residual_two + (
-        normed_part.astype(F32) + pair_swap(normed_part).astype(F32)
-    )
-    residual_one, gain_one, shift_one = norm_backward(
-        normed_grad, normal_one, inverse_one, full_gains[0]
-    )
-    branch_grad = residual_one.astype(BF)
-    context_grad = jnp.concatenate(
-        [jnp.dot(branch_grad, g_out[z], preferred_element_type=F32) for z in range(2)], axis=1
-    ).astype(BF)
-    def outer(a, b):
-        return jnp.einsum("rm,rn->mn", a, b, preferred_element_type=F32).astype(BF)
-
-    grads = (
-        jnp.stack(
-            [outer(branch_grad, context[:, z * part : (z + 1) * part]) for z in range(2)]
-        ),
-        jnp.stack([outer(normed_low, upper[z]) for z in range(2)]),
-        jnp.stack([outer(feed_grad, active[z]) for z in range(2)]),
-    )
-    tile = jnp.concatenate(
-        [
-            jnp.zeros((4, hidden), F32),
-            jnp.stack([jnp.sum(v.astype(F32), axis=0) for v in upper]),
-            jnp.stack(
-                [
-                    gain_one,
-                    gain_two,
-                    jnp.sum(branch_grad.astype(F32), axis=0),
-                    shift_one,
-                    jnp.sum(feed_grad.astype(F32), axis=0),
-                    shift_two,
-                ]
-            ),
-            jnp.zeros((4, hidden), F32),
-        ]
-    )
     back_chunks = (
         (3, 0, half),
         (3, half, half),
@@ -1660,16 +1743,16 @@
         (1, 0, part),
         (0, 0, 3 * part),
     )
-    out_rows, token_rows, tile_own, tile_mate, finals = back_reduce(
-        result.astype(BF),
-        residual_one,
+    out_rows, token_rows, tile_own, tile_mate, finals = layer_back(
         x,
-        g_qkv,
-        (queries, key_heads, value_heads, context, context_grad),
+        cot,
+        (g_qkv, g_out, g_up, g_down),
+        (queries, key_heads, value_heads, context),
         totals,
         limit,
-        grads,
-        tile,
+        g_small,
+        small_other,
+        per,
         back_chunks,
     )
     plane_rows = jnp.where(c == t // 2, tile_own, tile_mate)[:6].reshape(3, 2, hidden)

time: 324 us -> 252 us (0.78)
  matrix products: 49.6 us -> 0 us
  other arithmetic: 34.1 us -> 3.98 us
  Pallas kernels: 210 us -> 228 us
  local copies, waits for them, and re-layouts: 23.3 us -> 14 us
    dot_general x18 -> x0, matrix products: 49.6 us -> none  [the longest x2 23.7 us: chip_local(): jnp.dot(normed_low, g_up[z], preferred_element_type=F32) + up_bias[z]]
    reduce_sum x9 -> x0, other arithmetic: 21.7 us -> none  [the longest x2 9.7 us: norm_backward(): jnp.sum(incoming * normal, axis=0)]
    pallas_call x4 -> x1, Pallas kernels: 116 us -> 133 us  [layer_back(): pl.pallas_call(kernel, out_shape=[back, back, tiles, tiles, *[jax.ShapeDt...]
    unnamed x57 -> x17, local copies, waits for them, and re-layouts: 12.4 us -> 6.52 us
    another operation x2 -> x0, other arithmetic: 3.47 us -> none  [the longest x1 2.44 us: chip_local(): jnp.stack([outer(normed_low, upper[z]) for z in range(2)])]
where the time goes in v4:
time: 252 us; the launch traced here: 247 us
  Pallas kernels  228 us (90%)
  local copies, waits for them, and re-layouts  14 us (6%)
  other arithmetic  3.98 us (2%)
    pallas_call x1, Pallas kernels, layer_back(): pl.pallas_call(kernel, out_shape=[back, back, tiles, tiles, *[jax.ShapeDt...  133 us
    pallas_call x1, Pallas kernels, gather_attend(): pl.pallas_call(kernel, out_shape=[rows_shape, rows_shape, *full_shapes, f...  94.7 us
    unnamed x17, local copies, waits for them, and re-layouts  6.52 us

profile of v4, /device:TPU:0, one launch (start us, length us, event | category | flops | bytes accessed | tf_op | source)
XLA Modules:
  0.0 247.4 jit_solution(4617433047535309920)
XLA Ops:
  0.6 0.7 convert_bitcast_fusion
  1.3 0.1 fusion
  1.4 0.7 pad.26
  2.1 0.7 pad.23
  2.7 0.7 pad.24
  3.4 0.7 pad.25
  4.1 0.1 concatenate.21
  4.2 0.6 pad.28.refs_6_
  4.8 1.1 copy.25
  5.9 0.8 copy.27.refs_2_
  6.7 1.5 copy.26
  8.2 94.7 %shard_map.186 = (bf16[8,128,768]{2,1,0:T(8,128)(2,1)}, bf16[8,128,768]{2,1,0:T(8,128)(2,1)}, bf16[2,768,576]{2,1,0:T(8,128)(2,1)}, bf16[2,768,192]{2,1,0:T(8,12...) custom-call(bf16[2,256,768]{2,1,0:T(8,128)(2,1)} %refs_0_.1, ...), custom_call_target="tpu_custom_call" | custom-call | tf_op jit(solution)/shard_map/pallas_call | solution.py:762
  102.9 133.4 %shard_map.187 = (bf16[2,256,768]{2,1,0:T(8,128)(2,1)}, bf16[2,256,768]{2,1,0:T(8,128)(2,1)}, f32[16,768]{1,0:T(8,128)}, f32[16,768]{1,0:T(8,128)}, f32[96,576]{...) custom-call(bf16[1024,768]{1,0:T(8,128)(2,1)} %bitcast.16, bf16[1024,768]{1,0:T(8,128)(2,1)} %bitcast.17, ...), custom_call_target="tpu_custom_call" | custom-call | tf_op jit(solution)/shard_map/pallas_call | solution.py:1531
  236.3 0.0 copy-start.3
  236.3 0.0 copy-start.4
  236.4 0.0 copy-start
  236.4 0.8 slice_select_fusion
  237.3 0.6 dynamic-slice_bitcast_fusion
  237.9 0.6 constant_dynamic-slice_fusion.1
  238.5 2.4 convert_element_type.22
  240.9 0.0 copy-start.2
  240.9 0.0 copy-start.1
  240.9 0.0 copy-done.3
  240.9 0.1 copy.28
  241.0 0.9 copy.29
  241.9 0.0 copy-done.4
  241.9 0.7 copy.30
  242.7 0.8 constant_dynamic-slice_fusion
  243.5 0.6 slice.11
  244.0 0.6 slice.10
  244.6 0.0 copy-done
  244.6 0.9 copy.34
  245.5 0.0 copy-done.2
  245.5 0.7 copy.35
  246.2 0.0 copy-done.1
  246.2 0.7 copy.36
  (1 shorter events, 0.0 us)
Async XLA Ops:
  236.3 4.6 %copy-start.3 = (f32[96,576]{1,0:T(8,128)S(1)}, f32[96,576]{1,0:T(8,128)}, u32[]{:S(2)}) copy-start(f32[96,576]{1,0:T(8,128)} %get-tuple-element.48) | copy-start | bytes 663556
  236.3 5.6 %copy-start.4 = (f32[96,192]{1,0:T(8,128)S(1)}, f32[96,192]{1,0:T(8,128)}, u32[]{:S(2)}) copy-start(f32[96,192]{1,0:T(8,128)} %get-tuple-element.51) | copy-start | bytes 221188
  236.4 8.2 %copy-start = (bf16[2,256,768]{2,1,0:T(8,128)(2,1)S(1)}, bf16[2,256,768]{2,1,0:T(8,128)(2,1)}, u32[]{:S(2)}) copy-start(bf16[2,256,768]{2,1,0:T(8,128)(2,1)} %get-tuple-element.86) | copy-start | bytes 2359300
  240.9 4.6 %copy-start.2 = (f32[96,768]{1,0:T(8,128)S(1)}, f32[96,768]{1,0:T(8,128)}, u32[]{:S(2)}) copy-start(f32[96,768]{1,0:T(8,128)} %get-tuple-element.91) | copy-start | bytes 884740
  240.9 5.3 %copy-start.1 = (f32[96,768]{1,0:T(8,128)S(1)}, f32[96,768]{1,0:T(8,128)}, u32[]{:S(2)}) copy-start(f32[96,768]{1,0:T(8,128)} %get-tuple-element.53) | copy-start | bytes 884740
